TPU v7x, 32 devices: a whole 2x2x4 slice. The times are simulated.
32 devices in a mesh: groups: 2 (over y), center: 8 (over z, x), row: 2 (over core).
Axes of the slice: x: 2, y: 2, z: 4, core: 2. Of those that a mesh axis runs over, the one named last changes fastest.
Arguments:
- dataset: float32 [512, 1024], P(('groups', 'center', 'row')), parts along dimension 0, may hold values from -0.1875 to 0.1875
- centers: float32 [2048, 1024], P(('groups', 'center')), parts along dimension 0, may hold values from -0.1875 to 0.1875
- weights: float32 [2048, 512], P(('groups', 'center'), 'row'), parts along dimension 0, may hold values from -0.1875 to 0.1875
- batch_index: int32 [2, 128], P(None, ('groups', 'center', 'row')), parts along dimension 1, may hold values from 0 to 15
- targets: float32 [2, 128, 512], P(None, ('groups', 'center', 'row')), parts along dimension 1, may hold values from -6 to 6
- gamma: float32 [2], P('groups'), parts along dimension 0, may hold values from 0.3 to 1.5
Outputs:
- new_weights: float32 [2048, 512], P(('groups', 'center'), 'row'), parts along dimension 0
- residual: float32 [128, 512], P(('groups', 'center', 'row')), parts along dimension 0
There are 2 independent parts, one for each index of `groups`. A program takes and returns all parts, laid end to end along the dimension named above; each array names one. Nothing has to cross between parts.
Inputs may be any that keep to these rules, and one draw needn't show every extreme that they name: `batch_index`: each entry picks a row within the block of 16 dataset rows that has the same block number as the entry's block of 4 batch rows.
All inputs are finite; a program needn't handle non-finite values.
Results may differ from a plain program's by a relative error of at most 0.0001.
Values sent between devices are 32-bit elements; how exact they have to be, the bound alone decides.
No kernel may reach another device: no remote copies, remote signals or barrier semaphores. Data moves between devices by JAX's collectives and lax.ppermute only.
A program may use at most 64 MiB of HBM per device.

v0:
```python
import jax
import jax.numpy as jnp
from jax import lax
from jax.sharding import PartitionSpec as P


def per_device(dataset, centers, weights, batch_index, targets, gamma):
    center_sq = jnp.sum(centers * centers, axis=1)
    rows_here = batch_index.shape[1]
    current = weights
    residual = None
    for step in range(2):
        local_rows = dataset[batch_index[step]]
        rows, wanted = (
            lax.all_gather(local_rows, "center", axis=0, tiled=True),
            lax.all_gather(targets[step], "center", axis=0, tiled=True),
        )
        full_weights = lax.all_gather(current, "row", axis=1, tiled=True)
        row_sq = jnp.sum(rows * rows, axis=1)
        cross = jnp.dot(
            rows, centers.T, precision=lax.Precision.HIGHEST, preferred_element_type=jnp.float32
        )
        kernel = jnp.exp(-gamma[0] * (row_sq[:, None] + center_sq[None, :] - 2.0 * cross))
        partial_pred = jnp.dot(
            kernel,
            full_weights,
            precision=lax.Precision.HIGHEST,
            preferred_element_type=jnp.float32,
        )
        summed = lax.psum(partial_pred, "center")
        gathered_res = summed - wanted
        residual = lax.dynamic_slice_in_dim(
            gathered_res, lax.axis_index("center") * rows_here, rows_here, 0
        )
        grad = jnp.dot(
            kernel.T,
            gathered_res,
            precision=lax.Precision.HIGHEST,
            preferred_element_type=jnp.float32,
        )
        own_grad = lax.psum_scatter(grad, "row", scatter_dimension=1, tiled=True)
        batch_total = rows.shape[0] * lax.axis_size("row")
        current = current - 0.5 / batch_total * own_grad
    return (current, residual)


def solution(mesh):
    return jax.shard_map(
        per_device,
        mesh=mesh,
        in_specs=(
            P(("groups", "center", "row"), None),
            P(("groups", "center"), None),
            P(("groups", "center"), "row"),
            P(None, ("groups", "center", "row")),
            P(None, ("groups", "center", "row"), None),
            P("groups"),
        ),
        out_specs=(P(("groups", "center"), "row"), P(("groups", "center", "row"), None)),
        check_vma=False,
    )
```

profile of v0, /device:TPU:0, one launch (start us, length us, event | category | flops | bytes accessed | tf_op | source)
XLA Modules:
  0.0 241.9 jit_solution(545532573906874737)
XLA Ops:
  7.2 0.0 copy-start
  7.2 0.0 all-reduce.3.cloned.1.call-start
  7.9 0.0 copy-start.4
  7.9 1.2 multiply_reduce_fusion
  9.0 0.0 copy-done.4
  9.1 0.0 copy-done
  9.1 0.0 copy-start.1
  9.1 0.6 gather_fusion
  9.7 32.3 %all-gather.4 = f32[8,4,1024]{2,1,0:T(4,128)S(1)} all-gather(f32[1,4,1024]{2,1,0:T(4,128)S(1)} %bitcast.27), channel_id=2, replica_groups=mesh['groups'=2,'center'=8,'row'=2] {'center'}, dimensions={0}, use_global_device_ids=true | all-gather | bytes 147456 | tf_op jit(solution)/shard_map/all_gather | solution.py:15
  42.1 0.0 copy-start.2
  42.1 0.1 multiply_reduce_fusion.2
  42.2 0.8 copy-done.2
  43.0 2.0 all_gather.19
  44.9 0.0 copy-done.1
  44.9 0.6 fusion.5
  45.6 0.9 fusion.11
  46.5 0.0 copy-start.3
  46.5 0.0 all-reduce.3.cloned.1.call-update
  46.5 0.0 reduce-scatter.3.cloned.1.call-start
  46.5 0.6 copy-done.3
  47.2 30.5 %all-gather.1 = f32[1,32,512]{2,0,1:T(1,128)S(1)} all-gather(f32[1,4,512]{2,0,1:T(1,128)S(1)} %copy.12), channel_id=3, replica_groups=mesh['groups'=2,'center'=8,'row'=2] {'center'}, dimensions={1}, use_global_device_ids=true | all-gather | bytes 73728 | tf_op jit(solution)/shard_map/all_gather | solution.py:16
  77.7 39.1 %all-reduce.3.cloned.1.call-done = f32[32,512]{1,0:T(8,128)} async-done(((f32[32,512]{1,0:T(8,128)}), f32[32,512]{1,0:T(8,128)}) %all-reduce.3.cloned.1.call-update) | async-done | bytes 65552 | tf_op jit(solution)/shard_map/psum | solution.py:30
  116.8 2.0 fusion.6
  118.8 0.0 reduce-scatter.3.cloned.1.call-update
  118.8 0.0 all-reduce.5.cloned.1.call-start
  118.8 0.6 gather_fusion.1
  119.4 30.5 %all-gather.5 = f32[8,4,1024]{2,1,0:T(4,128)S(1)} all-gather(f32[1,4,1024]{2,1,0:T(4,128)S(1)} %bitcast.28), channel_id=4, replica_groups=mesh['groups'=2,'center'=8,'row'=2] {'center'}, dimensions={0}, use_global_device_ids=true | all-gather | bytes 147456 | tf_op jit(solution)/shard_map/all_gather | solution.py:15
  150.0 0.1 multiply_reduce_fusion.1
  150.1 0.6 fusion.2
  150.8 0.0 reduce-scatter.3.cloned.1.call-done
  150.8 0.9 multiply_subtract_fusion.1
  151.7 2.0 all_gather.22
  153.7 0.9 fusion.12
  154.6 0.0 all-reduce.5.cloned.1.call-update
  154.6 0.0 reduce-scatter.5.cloned.1.call-start
  154.7 30.5 %all-gather.3 = f32[1,32,512]{2,0,1:T(1,128)S(1)} all-gather(f32[1,4,512]{2,0,1:T(1,128)S(1)} %copy.13), channel_id=5, replica_groups=mesh['groups'=2,'center'=8,'row'=2] {'center'}, dimensions={1}, use_global_device_ids=true | all-gather | bytes 73728 | tf_op jit(solution)/shard_map/all_gather | solution.py:16
  185.2 38.8 %all-reduce.5.cloned.1.call-done = f32[32,512]{1,0:T(8,128)} async-done(((f32[32,512]{1,0:T(8,128)}), f32[32,512]{1,0:T(8,128)}) %all-reduce.5.cloned.1.call-update) | async-done | bytes 65552 | tf_op jit(solution)/shard_map/psum | solution.py:30
  224.0 0.8 bitcast_subtract_fusion
  224.8 1.1 fusion.13
  226.0 0.0 reduce-scatter.5.cloned.1.call-update
  226.0 0.6 constant_dynamic-slice_fusion
  226.6 7.2 %reduce-scatter.5.cloned.1.call-done = f32[128,256]{1,0:T(8,128)} async-done(((f32[128,512]{1,0:T(8,128)}), f32[128,256]{1,0:T(8,128)}) %reduce-scatter.5.cloned.1.call-update) | async-done | bytes 131088 | tf_op jit(solution)/shard_map/reduce_scatter | solution.py:41
  233.8 1.6 multiply_subtract_fusion
  (7 shorter events, 0.1 us)
Async XLA Ops:
  7.2 1.9 copy-start
  7.2 109.6 %all-reduce.3.cloned.1.call-start = ((), (), s32[]{:S(2)}) async-start(), calls=%async_computation.2 | async-start | bytes 131072 | tf_op jit(solution)/shard_map/psum | solution.py:30
  7.9 1.2 copy-start.4
  9.1 35.9 %copy-start.1 = (f32[128,1024]{1,0:T(8,128)S(1)}, f32[128,1024]{1,0:T(8,128)}, u32[]{:S(2)}) copy-start(f32[128,1024]{1,0:T(8,128)} %param.7) | copy-start | bytes 1572868
  42.1 0.9 copy-start.2
  46.5 0.7 copy-start.3
  46.5 104.3 %reduce-scatter.3.cloned.1.call-start = ((), (), s32[]{:S(2)}) async-start(), calls=%async_computation.3 | async-start | bytes 393216 | tf_op jit(solution)/shard_map/reduce_scatter | solution.py:41
  118.8 105.2 %all-reduce.5.cloned.1.call-start = ((), (), s32[]{:S(2)}) async-start(), calls=%async_computation.4 | async-start | bytes 131072 | tf_op jit(solution)/shard_map/psum | solution.py:30
  154.6 79.2 %reduce-scatter.5.cloned.1.call-start = ((), (), s32[]{:S(2)}) async-start(), calls=%async_computation.5 | async-start | bytes 393216 | tf_op jit(solution)/shard_map/reduce_scatter | solution.py:41
Sparse Core Ops, SparseCore 0:
  46.6 70.1 all-reduce.2
  119.0 7.6 reduce-scatter.2
  154.7 69.2 all-reduce.4
  226.1 7.6 reduce-scatter.4
where the time goes:
time: 242 us
  blocking collectives  128 us (53%)
  waiting for transfers between devices  85.2 us (35%)
  between operations  14.5 us (6%)
  matrix products  6.1 us (3%)
  other arithmetic  4.76 us (2%)
  local copies, waits for them, and re-layouts  3.3 us (1%)
    psum x2, waiting for transfers between devices, per_device(): summed = lax.psum(partial_pred, 'center')  77.8 us
    all_gather x2, blocking collectives, per_device(): lax.all_gather(local_rows, 'center', axis=0, tiled=True)  62.9 us
    all_gather x2, blocking collectives, per_device(): lax.all_gather(targets[step], 'center', axis=0, tiled=True)  61.1 us
    reduce_scatter x2, waiting for transfers between devices, per_device(): own_grad = lax.psum_scatter(grad, 'row', scatter_dimension=1, tiled=True)  7.25 us
  transfers between devices with their start and end apart: 4, of which 3 were waited for; matrix products, arithmetic and copies ran while one was open for 1% of the time, Pallas kernels for 0%

commit v1 on v0

v1 whole, which is shorter than its diff:
```python
import jax
import jax.numpy as jnp
from jax import lax
from jax.sharding import PartitionSpec as P

HIGH = lax.Precision.HIGHEST


def dot(a, b, contract):
    return lax.dot_general(
        a, b, (contract, ((), ())), precision=HIGH, preferred_element_type=jnp.float32
    )


def swap_cores(x):
    return lax.ppermute(x, "row", [(0, 1), (1, 0)])


def exchange(x):
    return lax.all_to_all(x, "center", 0, 0, tiled=True)


def per_device(dataset, centers, weights, batch_index, targets, gamma):
    shards = lax.axis_size("center")
    cores = lax.axis_size("row")
    assert cores == 2
    me = lax.axis_index("row")
    rows_here = batch_index.shape[1]
    features = dataset.shape[1]
    cols = weights.shape[1]
    count = centers.shape[0]
    batch_total = shards * cores * rows_here
    rate = 0.5 / batch_total

    local = dataset.at[batch_index.reshape(-1)].get(mode="promise_in_bounds")
    rows = exchange(jnp.broadcast_to(local[None], (shards,) + local.shape))
    rows = rows.reshape(-1, features)

    halves = targets.reshape(2, rows_here, 2, cols)
    mine = lax.dynamic_index_in_dim(halves, me, 2, keepdims=False)
    theirs = swap_cores(lax.dynamic_index_in_dim(halves, 1 - me, 2, keepdims=False))
    wanted = jnp.concatenate([mine.reshape(-1, cols), theirs.reshape(-1, cols)], 0)

    center_sq = jnp.sum(centers * centers, axis=1)
    row_sq = jnp.sum(rows * rows, axis=1)
    cross = dot(rows, centers, ((1,), (1,)))
    own = jnp.exp(-gamma[0] * (row_sq[:, None] + center_sq[None, :] - 2.0 * cross))
    other = swap_cores(own)
    split = (shards, 1, 2, rows_here, count)
    kernel = jnp.concatenate([own.reshape(split), other.reshape(split)], 1)
    first = kernel[:, :, 0].reshape(-1, count)
    second = kernel[:, :, 1].reshape(-1, count)
    part = dot(kernel.reshape(-1, count), weights, ((1,), (0,))).reshape(shards, -1, cols)
    gram = dot(second, first, ((1,), (1,)))
    width = -(-batch_total // 128) * 128
    gram = jnp.pad(gram, ((0, 0), (0, width - batch_total))).reshape(shards, -1, width)

    tiles = lambda x: [x[:, :, i : i + 128] for i in range(0, x.shape[2], 128)]
    sent = jnp.concatenate(tiles(part) + tiles(gram), 1)
    got = jnp.sum(exchange(sent), axis=0)
    chip_rows = part.shape[1]
    split_at = chip_rows * (cols // 128)
    done = jnp.concatenate(
        [
            got[i * chip_rows : (i + 1) * chip_rows] - wanted[:, i * 128 : (i + 1) * 128]
            for i in range(cols // 128)
        ]
        + [got[split_at:]],
        0,
    )
    full = exchange(jnp.broadcast_to(done[None], (shards,) + done.shape))
    values = jnp.concatenate(
        [full[:, i * chip_rows : (i + 1) * chip_rows] for i in range(cols // 128)], 2
    )
    gram_rows = gram.shape[1]
    gram = jnp.concatenate(
        [
            full[:, split_at + i * gram_rows : split_at + (i + 1) * gram_rows]
            for i in range(width // 128)
        ],
        2,
    )
    gram = gram.reshape(batch_total, width)[:, :batch_total]
    values = values.reshape(shards, cores, 2, rows_here, cols)
    res0 = values[:, :, 0].reshape(-1, cols)
    res1 = values[:, :, 1].reshape(-1, cols) - rate * dot(gram, res0, ((1,), (0,)))
    grad = dot(first, res0, ((0,), (0,))) + dot(second, res1, ((0,), (0,)))
    new_weights = weights - rate * grad

    chip = lax.dynamic_index_in_dim(
        res1.reshape(shards, cores, rows_here, cols), lax.axis_index("center"), 0, keepdims=False
    )
    back = swap_cores(chip[1])
    residual = jnp.where(
        me == 0,
        jnp.concatenate([chip[0], back], 1),
        jnp.concatenate([back, chip[0]], 1),
    )
    return (new_weights, residual)


def solution(mesh):
    return jax.shard_map(
        per_device,
        mesh=mesh,
        in_specs=(
            P(("groups", "center", "row"), None),
            P(("groups", "center"), None),
            P(("groups", "center"), "row"),
            P(None, ("groups", "center", "row")),
            P(None, ("groups", "center", "row"), None),
            P("groups"),
        ),
        out_specs=(P(("groups", "center"), "row"), P(("groups", "center", "row"), None)),
        check_vma=False,
    )
```

time: 242 us -> 49.4 us (0.20)
  blocking collectives: 128 us -> 0 us
  waiting for transfers between devices: 85.2 us -> 24.5 us
  starting transfers between devices: 0.16 us -> 14.5 us
  between operations: 14.5 us -> 1.59 us
  matrix products: 6.1 us -> 2.59 us
  other arithmetic: 4.76 us -> 1.54 us
    all_gather x6 -> x0, blocking collectives: 128 us -> none  [the longest x2 62.9 us: per_device(): lax.all_gather(local_rows, 'center', axis=0, tiled=True)]
    psum x2 -> x0, waiting for transfers between devices: 77.8 us -> none  [per_device(): summed = lax.psum(partial_pred, 'center')]
    all_to_all x0 -> x3, waiting for transfers between devices: none -> 22 us  [exchange(): return lax.all_to_all(x, 'center', 0, 0, tiled=True)]
    all_to_all x0 -> x3, starting transfers between devices: none -> 14.2 us  [exchange(): return lax.all_to_all(x, 'center', 0, 0, tiled=True)]
    reduce_scatter x2 -> x0, waiting for transfers between devices: 7.25 us -> none  [per_device(): own_grad = lax.psum_scatter(grad, 'row', scatter_dimension=1, tiled=True)]
    dot_general x6, matrix products: 6.1 us -> 2.59 us  [dot(): lax.dot_general(a, b, (contract, ((), ())), precision=HIGH, preferred_ele...]
    sub x3 -> x1, other arithmetic: 3.35 us -> 0.01 us  [per_device(): got[i * chip_rows:(i + 1) * chip_rows] - wanted[:, i * 128:(i + 1) * 128]]
    ppermute x0 -> x3, waiting for transfers between devices: none -> 2.5 us  [swap_cores(): return lax.ppermute(x, 'row', [(0, 1), (1, 0)])]
  transfers between devices with their start and end apart: 4 -> 6, of which waited for: 3 -> 6; matrix products, arithmetic and copies ran while one was open for 1% -> 2% of each run, Pallas kernels for 0% -> 0%
where the time goes in v1:
time: 49.4 us; the launch traced here: 48.9 us
  waiting for transfers between devices  24.5 us (50%)
  starting transfers between devices  14.5 us (29%)
  local copies, waits for them, and re-layouts  4.14 us (8%)
  matrix products  2.59 us (5%)
  between operations  1.59 us (3%)
  other arithmetic  1.54 us (3%)
    all_to_all x3, waiting for transfers between devices, exchange(): return lax.all_to_all(x, 'center', 0, 0, tiled=True)  22 us
    all_to_all x3, starting transfers between devices, exchange(): return lax.all_to_all(x, 'center', 0, 0, tiled=True)  14.2 us
    dot_general x6, matrix products, dot(): lax.dot_general(a, b, (contract, ((), ())), precision=HIGH, preferred_ele...  2.59 us
    ppermute x3, waiting for transfers between devices, swap_cores(): return lax.ppermute(x, 'row', [(0, 1), (1, 0)])  2.5 us
    unnamed x14, local copies, waits for them, and re-layouts  1.02 us
  transfers between devices with their start and end apart: 6, of which 6 were waited for; matrix products, arithmetic and copies ran while one was open for 2% of the time, Pallas kernels for 0%

profile of v1, /device:TPU:0, one launch (start us, length us, event | category | flops | bytes accessed | tf_op | source)
XLA Modules:
  0.0 48.9 jit_solution(2676549587638465668)
XLA Ops:
  0.6 0.0 copy-start
  0.6 0.8 %reshape.87 = s32[8,1]{0,1:T(1,128)S(1)} reshape(s32[2,4]{1,0:T(2,128)} %param.9) | data formatting | bytes 64 | tf_op jit(solution)/shard_map/reshape | solution.py:35
  1.5 0.0 copy-done
  1.5 0.0 copy-start.1
  1.5 0.6 %gather_fusion = f32[8,1024]{1,0:T(8,128)S(1)} fusion(f32[16,1024]{1,0:T(8,128)S(1)} %copy-done, s32[1024]{0:T(1024)S(1)} %pad_clamp_fusion), kind=kCustom, calls=%fused_computation | custom fusion | bytes 65568 | tf_op jit(solution)/shard_map/gather | solution.py:35
  2.0 0.7 %broadcast_in_dim.4 = f32[8,8,1024]{2,1,0:T(8,128)} broadcast(f32[8,1024]{1,0:T(8,128)S(1)} %gather_fusion), dimensions={1,2} | broadcast | bytes 294912 | tf_op jit(solution)/shard_map/broadcast_in_dim | solution.py:36
  2.8 7.3 %all-to-all-start = ((f32[8,8,1024]{2,1,0:T(8,128)}), f32[8,8,1024]{2,1,0:T(8,128)S(1)}, u32[]{:S(2)}, u32[]{:S(2)}) async-start(f32[8,8,1024]{2,1,0:T(8,128)} %broadcast_in_dim.4), calls=%async_computation | async-start | bytes 524288 | tf_op jit(solution)/shard_map/all_to_all | solution.py:20
  10.0 0.0 copy-start.3
  10.7 0.0 copy-done.3
  10.8 0.0 copy-done.1
  10.8 0.1 multiply_reduce_fusion
  10.9 8.0 %all-to-all-done = f32[8,8,1024]{2,1,0:T(8,128)S(1)} async-done(((f32[8,8,1024]{2,1,0:T(8,128)}), f32[8,8,1024]{2,1,0:T(8,128)S(1)}, u32[]{:S(2)}, u32[]{:S(2)}) %all-to-all-start) | async-done | bytes 262176 | tf_op jit(solution)/shard_map/all_to_all | solution.py:20
  19.0 0.1 multiply_reduce_fusion.1
  19.1 0.1 add.43
  19.1 0.7 %fusion.5 = f32[64,128]{1,0:T(8,128)S(1)} fusion(f32[128,1024]{1,0:T(8,128)S(1)} %copy-done.1, f32[8,8,1024]{2,1,0:T(8,128)S(1)} %all-to-all-done, f32[128]{0:T(128)S(1)} %multiply_reduce_fusion, f32[64]{0:T(128)S(1)} %add.43, f32[]{:T(128)} %bitcast), kind=kOutput, calls=%fused_computation.10 | convolution fusion | flops 100696064 | bytes 819972 | tf_op jit(solution)/shard_map/dot_general | solution.py:10
  19.8 0.1 collective-permute-start
  19.9 1.2 %collective-permute-done = f32[64,128]{1,0:T(8,128)S(1)} collective-permute-done((f32[64,128]{1,0:T(8,128)S(1)}, f32[64,128]{1,0:T(8,128)S(1)}, u32[]{:S(2)}, u32[]{:S(2)}) %collective-permute-start) | collective-permute-done | bytes 32800 | tf_op jit(solution)/shard_map/ppermute | solution.py:16
  21.1 0.0 copy-start.2
  21.1 0.9 %copy-done.2 = f32[128,256]{1,0:T(8,128)S(1)} copy-done((f32[128,256]{1,0:T(8,128)S(1)}, f32[128,256]{1,0:T(8,128)}, u32[]{:S(2)}) %copy-start.2) | copy-done | bytes 131096
  22.0 0.3 fusion.7
  22.3 0.2 fusion.18
  22.5 0.7 %pad_maximum_fusion = f32[8,40,128]{2,1,0:T(8,128)} fusion(f32[8,8,128]{2,1,0:T(8,128)S(1)} %pad_bitcast_fusion, f32[8,16,128]{2,1,0:T(8,128)S(1)} %get-tuple-element.7, f32[8,16,128]{2,1,0:T(8,128)S(1)} %get-tuple-element.6), kind=kLoop, calls=%fused_computation.14 | loop fusion | flops 81920 | bytes 327680 | tf_op jit(solution)/shard_map/concatenate | solution.py:59
  23.2 3.6 %all-to-all-start.1 = ((f32[8,40,128]{2,1,0:T(8,128)}), f32[8,40,128]{2,1,0:T(8,128)S(1)}, u32[]{:S(2)}, u32[]{:S(2)}) async-start(f32[8,40,128]{2,1,0:T(8,128)} %pad_maximum_fusion), calls=%async_computation.1 | async-start | bytes 327680 | tf_op jit(solution)/shard_map/all_to_all | solution.py:20
  26.8 0.1 collective-permute-start.1
  26.9 1.1 %collective-permute-done.1 = f32[2,4,256]{2,1,0:T(4,128)S(1)} collective-permute-done((f32[2,4,256]{2,1,0:T(4,128)S(1)}, f32[2,4,256]{2,1,0:T(4,128)S(1)}, u32[]{:S(2)}, u32[]{:S(2)}) %collective-permute-start.1) | collective-permute-done | bytes 8224 | tf_op jit(solution)/shard_map/ppermute | solution.py:16
  28.1 6.5 %all-to-all-done.1 = f32[8,40,128]{2,1,0:T(8,128)S(1)} async-done(((f32[8,40,128]{2,1,0:T(8,128)}), f32[8,40,128]{2,1,0:T(8,128)S(1)}, u32[]{:S(2)}, u32[]{:S(2)}) %all-to-all-start.1) | async-done | bytes 163872 | tf_op jit(solution)/shard_map/all_to_all | solution.py:20
  34.6 0.7 %broadcast_in_dim.5 = f32[8,40,128]{2,1,0:T(8,128)} broadcast(f32[40,128]{1,0:T(8,128)S(1)} %pad_maximum_fusion.2), dimensions={1,2} | broadcast | bytes 184320 | tf_op jit(solution)/shard_map/broadcast_in_dim | solution.py:71
  35.3 3.4 %all-to-all-start.2 = ((f32[8,40,128]{2,1,0:T(8,128)}), f32[8,40,128]{2,1,0:T(8,128)S(1)}, u32[]{:S(2)}, u32[]{:S(2)}) async-start(f32[8,40,128]{2,1,0:T(8,128)} %broadcast_in_dim.5), calls=%async_computation.2 | async-start | bytes 327680 | tf_op jit(solution)/shard_map/all_to_all | solution.py:20
  38.7 7.5 %all-to-all-done.2 = f32[8,40,128]{2,1,0:T(8,128)S(1)} async-done(((f32[8,40,128]{2,1,0:T(8,128)}), f32[8,40,128]{2,1,0:T(8,128)S(1)}, u32[]{:S(2)}, u32[]{:S(2)}) %all-to-all-start.2) | async-done | bytes 163872 | tf_op jit(solution)/shard_map/all_to_all | solution.py:20
  46.3 0.3 convolution_bitcast_fusion
  46.8 0.2 fusion.2
  47.0 0.1 collective-permute-start.2
  47.1 1.0 %fusion.1 = f32[128,256]{1,0:T(8,128)} fusion(f32[128,256]{1,0:T(8,128)S(1)} %copy-done.2, f32[128,256]{1,0:T(8,128)S(1)} %convolution_bitcast_fusion, f32[64,128]{1,0:T(8,128)S(1)} %bitcast.53, f32[64,256]{1,0:T(8,128)S(1)} %fusion.2), kind=kOutput, calls=%fused_computation.4 | convolution fusion | flops 25264128 | bytes 491520 | tf_op jit(solution)/shard_map/dot_general | solution.py:10
  48.1 0.2 collective-permute-done.2
  48.3 0.6 %maximum_select_fusion = f32[4,512]{1,0:T(4,128)} fusion(f32[4,256]{1,0:T(4,128)S(1)} %collective-permute-done.2, f32[4,256]{1,0:T(4,128)S(1)} %get-tuple-element.8, pred[]{:T(512)S(6)} %eq.3), kind=kLoop, calls=%fused_computation.32 | loop fusion | flops 6144 | bytes 16385 | tf_op jit(solution)/shard_map/jit(_where)/select_n | solution.py:94
  (33 shorter events, 0.4 us)
Async XLA Ops:
  0.6 0.8 %copy-start = (f32[16,1024]{1,0:T(8,128)S(1)}, f32[16,1024]{1,0:T(8,128)}, u32[]{:S(2)}) copy-start(f32[16,1024]{1,0:T(8,128)} %param.6) | copy-start | bytes 196612
  1.5 9.3 %copy-start.1 = (f32[128,1024]{1,0:T(8,128)S(1)}, f32[128,1024]{1,0:T(8,128)}, u32[]{:S(2)}) copy-start(f32[128,1024]{1,0:T(8,128)} %param.7) | copy-start | bytes 1572868
  2.8 16.2 %all-to-all-start = ((f32[8,8,1024]{2,1,0:T(8,128)}), f32[8,8,1024]{2,1,0:T(8,128)S(1)}, u32[]{:S(2)}, u32[]{:S(2)}) async-start(f32[8,8,1024]{2,1,0:T(8,128)} %broadcast_in_dim.4), calls=%async_computation | async-start | bytes 524288 | tf_op jit(solution)/shard_map/all_to_all | solution.py:20
  10.0 0.7 %copy-start.3 = (f32[2,4,512]{2,1,0:T(4,128)S(1)}, f32[2,4,512]{2,1,0:T(4,128)}, u32[]{:S(2)}) copy-start(f32[2,4,512]{2,1,0:T(4,128)} %param.10) | copy-start | bytes 49156
  19.8 1.3 %collective-permute-start = (f32[64,128]{1,0:T(8,128)S(1)}, f32[64,128]{1,0:T(8,128)S(1)}, u32[]{:S(2)}, u32[]{:S(2)}) collective-permute-start(f32[64,128]{1,0:T(8,128)S(1)} %fusion.5), channel_id=1, source_target_pairs={{0,1},{1,0},{2,3},{3,2},{4,5},{5,4},{6,7},{7,6},{8,9},{9,8},{10,11... | collective-permute-start | bytes 98312 | tf_op jit(solution)/shard_map/ppermute | solution.py:16
  21.1 0.9 %copy-start.2 = (f32[128,256]{1,0:T(8,128)S(1)}, f32[128,256]{1,0:T(8,128)}, u32[]{:S(2)}) copy-start(f32[128,256]{1,0:T(8,128)} %param.8) | copy-start | bytes 393220
  23.2 11.4 %all-to-all-start.1 = ((f32[8,40,128]{2,1,0:T(8,128)}), f32[8,40,128]{2,1,0:T(8,128)S(1)}, u32[]{:S(2)}, u32[]{:S(2)}) async-start(f32[8,40,128]{2,1,0:T(8,128)} %pad_maximum_fusion), calls=%async_computation.1 | async-start | bytes 327680 | tf_op jit(solution)/shard_map/all_to_all | solution.py:20
  26.8 1.2 %collective-permute-start.1 = (f32[2,4,256]{2,1,0:T(4,128)S(1)}, f32[2,4,256]{2,1,0:T(4,128)S(1)}, u32[]{:S(2)}, u32[]{:S(2)}) collective-permute-start(f32[2,4,256]{2,1,0:T(4,128)S(1)} %bitcast.58), channel_id=1, source_target_pairs={{0,1},{1,0},{2,3},{3,2},{4,5},{5,4},{6,7},{7,6},{8,9},{9,8},{10,11... | collective-permute-start | bytes 24584 | tf_op jit(solution)/shard_map/ppermute | solution.py:16
  35.3 10.9 %all-to-all-start.2 = ((f32[8,40,128]{2,1,0:T(8,128)}), f32[8,40,128]{2,1,0:T(8,128)S(1)}, u32[]{:S(2)}, u32[]{:S(2)}) async-start(f32[8,40,128]{2,1,0:T(8,128)} %broadcast_in_dim.5), calls=%async_computation.2 | async-start | bytes 327680 | tf_op jit(solution)/shard_map/all_to_all | solution.py:20
  47.0 1.2 %collective-permute-start.2 = (f32[4,256]{1,0:T(4,128)S(1)}, f32[4,256]{1,0:T(4,128)S(1)}, u32[]{:S(2)}, u32[]{:S(2)}) collective-permute-start(f32[4,256]{1,0:T(4,128)S(1)} %get-tuple-element.9), channel_id=1, source_target_pairs={{0,1},{1,0},{2,3},{3,2},{4,5},{5,4},{6,7},{7,6},{8,9},{9,8},{10,11... | collective-permute-start | bytes 12296 | tf_op jit(solution)/shard_map/ppermute | solution.py:16

commit v2 on v0

v2 whole, which is shorter than its diff:
```python
import functools
import math

import jax
import jax.numpy as jnp
from jax import lax
from jax.experimental import pallas as pl
from jax.experimental.pallas import tpu as pltpu
from jax.sharding import PartitionSpec as P

LANES = 128
KEPT_BYTES = 1 << 20


def dot(a, b, contract):
    return lax.dot_general(
        a,
        b,
        (contract, ((), ())),
        precision=lax.Precision.HIGHEST,
        preferred_element_type=jnp.float32,
    )


def small(x):
    return math.prod(x.shape) * 4 <= KEPT_BYTES


def call(body, outs, name, *args):
    args = [a if isinstance(a, tuple) else (a, pltpu.VMEM) for a in args]
    return pl.pallas_call(
        body,
        out_shape=outs,
        in_specs=[pl.BlockSpec(memory_space=space) for _, space in args],
        out_specs=[pl.BlockSpec(memory_space=pltpu.VMEM)] * len(outs),
        name=name,
    )(
        *[
            pltpu.with_memory_space_constraint(a, space)
            if space == pltpu.VMEM and small(a)
            else a
            for a, space in args
        ]
    )


def stored(*shape):
    return jax.ShapeDtypeStruct(shape, jnp.float32)


def kept(*shape):
    return pltpu.VMEM(shape, jnp.float32) if small(stored(*shape)) else stored(*shape)


def swap_cores(x):
    return lax.ppermute(x, "row", [(0, 1), (1, 0)])


def exchange(x):
    return lax.all_to_all(x, "center", 0, 0, tiled=True)


def pick_body(index, gamma, dataset, out, spread):
    spread[...] = jnp.full(spread.shape, gamma[0])
    batches, count = index.shape
    rows = jnp.concatenate(
        [dataset[pl.ds(index[b, j], 1), :] for b in range(batches) for j in range(count)], 0
    )
    out[...] = jnp.broadcast_to(rows[None], out.shape)


def kernel_body(gamma, rows, centers, targets, out):
    x, c = rows[...], centers[...]
    count = c.shape[0]
    row_sq = jnp.sum(x * x, axis=1, keepdims=True)
    center_sq = jnp.sum(c * c, axis=1, keepdims=True)
    center_sq = jnp.broadcast_to(center_sq, (count, LANES)).T[:1]
    cross = dot(x, c, ((1,), (1,)))
    n = x.shape[0]
    out[:n] = jnp.exp(-gamma[:1] * (row_sq + center_sq - 2.0 * cross))
    wanted = target_rows(targets, 1 - lax.axis_index("row"))
    for i, tile in enumerate(wanted):
        out[n + i * tile.shape[0] : n + (i + 1) * tile.shape[0]] = tile


def target_rows(targets, side):
    cols = targets.shape[2] // 2
    both = jnp.concatenate([targets[b] for b in range(targets.shape[0])], 0)
    half = jnp.where(side == 0, both[:, :cols], both[:, cols:])
    return [half[:, i : i + LANES] for i in range(0, cols, LANES)]


def merge_batch(own, other):
    half = own.shape[1] // 2
    low = lax.broadcasted_iota(jnp.int32, own.shape, 1) < half
    return jnp.where(low, pltpu.roll(own, half, 1), other)


def predict_body(each, made, swapped, weights, out):
    shards, _, lanes = out.shape
    n, count = shards * each, made.shape[1]
    w = weights[...]
    a, b = made[:n], swapped[:n]
    tile = 0
    for half in (a, b):
        part = dot(half, w, ((1,), (0,)))
        for i in range(0, w.shape[1], lanes):
            out[:, tile : tile + each] = part[:, i : i + lanes].reshape(shards, each, lanes)
            tile += each
    second = merge_batch(a.reshape(shards, each, count), b.reshape(shards, each, count))
    second = second.reshape(n, count)
    gram = jnp.concatenate([dot(second, a, ((1,), (1,))), dot(second, b, ((1,), (1,)))], 1)
    first = lax.broadcasted_iota(jnp.int32, gram.shape, 1) % each < each // 2
    gram = jnp.where(first, gram, 0.0)
    for i in range(0, gram.shape[1], lanes):
        out[:, tile : tile + each] = gram[:, i : i + lanes].reshape(shards, each, lanes)
        tile += each


def residual_body(got, swapped, targets, out):
    total = jnp.sum(got[...], axis=0)
    mine = target_rows(targets, lax.axis_index("row"))
    each = mine[0].shape[0]
    n = swapped.shape[0] - each * len(mine)
    theirs = [swapped[n + i * each : n + (i + 1) * each] for i in range(len(mine))]
    wanted = mine + theirs
    total = jnp.concatenate(
        [total[i * each : (i + 1) * each] - t for i, t in enumerate(wanted)]
        + [total[each * len(wanted) :]],
        0,
    )
    out[...] = jnp.broadcast_to(total[None], out.shape)


def second_body(rate, full, own_out, other_out, mine_out, theirs_out):
    shards, _, lanes = full.shape
    n, cols = own_out.shape
    each = n // shards
    tiles = cols // lanes
    take = lambda i: full[:, i * each : (i + 1) * each].reshape(n, lanes)
    own = jnp.concatenate([take(i) for i in range(tiles)], 1)
    other = jnp.concatenate([take(i) for i in range(tiles, 2 * tiles)], 1)
    gram = jnp.concatenate([take(i) for i in range(2 * tiles, full.shape[1] // each)], 1)
    step = dot(gram, jnp.concatenate([own, other], 0), ((1,), (0,))) * rate
    step = step.reshape(shards, each, cols)
    half = each // 2
    late = lax.broadcasted_iota(jnp.int32, step.shape, 1) >= half
    move = lambda x: jnp.where(late, x, 0.0).reshape(n, cols)
    own_out[...] = own - move(pltpu.roll(step, half, 1))
    other_out[...] = other - move(step)
    at = lax.axis_index("center") * each
    mine_out[...] = own_out[pl.ds(at, each), :][half:]
    theirs_out[...] = other_out[pl.ds(at, each), :][half:]


def update_body(rate, made, swapped, res_own, res_other, weights, out):
    n = res_own.shape[0]
    k = jnp.concatenate([made[:n], swapped[:n]], 0)
    r = jnp.concatenate([res_own[...], res_other[...]], 0)
    out[...] = weights[...] - rate * dot(k, r, ((0,), (0,)))


def finish_body(mine, back, out):
    first = lax.axis_index("row") == 0
    a, b = mine[...], back[...]
    cols = a.shape[1]
    out[:, :cols] = jnp.where(first, a, b)
    out[:, cols:] = jnp.where(first, b, a)


def per_device(dataset, centers, weights, batch_index, targets, gamma):
    shards = lax.axis_size("center")
    assert lax.axis_size("row") == 2
    batches, rows_here = batch_index.shape
    features = dataset.shape[1]
    count, cols = weights.shape
    each = batches * rows_here
    n = shards * each
    rate = 0.5 / (shards * 2 * rows_here)
    tiles = 2 * (cols // LANES)
    packed = (shards, each * tiles + each * (2 * n // LANES), LANES)

    local, spread = call(
        pick_body,
        [kept(shards, each, features), kept(8, count)],
        "pick",
        (batch_index, pltpu.SMEM),
        (gamma, pltpu.SMEM),
        dataset,
    )
    rows = exchange(local).reshape(n, features)
    (made,) = call(
        kernel_body,
        [kept(n + each * (tiles // 2), count)],
        "kernel",
        spread,
        rows,
        centers,
        targets,
    )
    swapped = swap_cores(made)
    (sent,) = call(functools.partial(predict_body, each), [kept(*packed)], "predict", made, swapped, weights)
    got = exchange(sent)
    (done,) = call(residual_body, [kept(*packed)], "residual", got, swapped, targets)
    full = exchange(done)
    res_own, res_other, mine, theirs = call(
        functools.partial(second_body, rate),
        [kept(n, cols), kept(n, cols), kept(rows_here, cols), kept(rows_here, cols)],
        "second",
        full,
    )
    back = swap_cores(theirs)
    (new_weights,) = call(
        functools.partial(update_body, rate),
        [stored(count, cols)],
        "update",
        made,
        swapped,
        res_own,
        res_other,
        weights,
    )
    (residual,) = call(finish_body, [stored(rows_here, 2 * cols)], "finish", mine, back)
    return (new_weights, residual)


def solution(mesh):
    return jax.shard_map(
        per_device,
        mesh=mesh,
        in_specs=(
            P(("groups", "center", "row"), None),
            P(("groups", "center"), None),
            P(("groups", "center"), "row"),
            P(None, ("groups", "center", "row")),
            P(None, ("groups", "center", "row"), None),
            P("groups"),
        ),
        out_specs=(P(("groups", "center"), "row"), P(("groups", "center", "row"), None)),
        check_vma=False,
    )
```

time: 242 us -> 45.2 us (0.19)
  blocking collectives: 128 us -> 37.5 us
  waiting for transfers between devices: 85.2 us -> 1.38 us
  between operations: 14.5 us -> 1.41 us
  matrix products: 6.1 us -> 0 us
  other arithmetic: 4.76 us -> 0 us
  Pallas kernels: 0 us -> 3.66 us
  local copies, waits for them, and re-layouts: 3.3 us -> 0.85 us
    all_gather x6 -> x0, blocking collectives: 128 us -> none  [the longest x2 62.9 us: per_device(): lax.all_gather(local_rows, 'center', axis=0, tiled=True)]
    psum x2 -> x0, waiting for transfers between devices: 77.8 us -> none  [per_device(): summed = lax.psum(partial_pred, 'center')]
    all_to_all x0 -> x3, blocking collectives: none -> 37.5 us  [exchange(): return lax.all_to_all(x, 'center', 0, 0, tiled=True)]
    reduce_scatter x2 -> x0, waiting for transfers between devices: 7.25 us -> none  [per_device(): own_grad = lax.psum_scatter(grad, 'row', scatter_dimension=1, tiled=True)]
    dot_general x6 -> x0, matrix products: 6.1 us -> none  [the longest x2 3.07 us: per_device(): jnp.dot(kernel.T, gathered_res, precision=lax.Precision.HIGHEST, preferre...]
    pallas_call x0 -> x7, Pallas kernels: none -> 3.66 us  [call(): pl.pallas_call(body, out_shape=outs, in_specs=[pl.BlockSpec(memory_space=...]
    sub x3 -> x0, other arithmetic: 3.35 us -> none  [the longest x2 2.5 us: per_device(): current = current - 0.5 / batch_total * own_grad]
  transfers between devices with their start and end apart: 4 -> 2, of which waited for: 3 -> 2; matrix products, arithmetic and copies ran while one was open for 1% -> 0% of each run, Pallas kernels for 0% -> 2%
where the time goes in v2:
time: 45.2 us; the launch traced here: 44.9 us
  blocking collectives  37.5 us (83%)
  Pallas kernels  3.66 us (8%)
  between operations  1.41 us (3%)
  waiting for transfers between devices  1.38 us (3%)
  local copies, waits for them, and re-layouts  0.85 us (2%)
    all_to_all x3, blocking collectives, exchange(): return lax.all_to_all(x, 'center', 0, 0, tiled=True)  37.5 us
    pallas_call x7, Pallas kernels, call(): pl.pallas_call(body, out_shape=outs, in_specs=[pl.BlockSpec(memory_space=...  3.66 us
    ppermute x2, waiting for transfers between devices, swap_cores(): return lax.ppermute(x, 'row', [(0, 1), (1, 0)])  1.38 us
  transfers between devices with their start and end apart: 2, of which 2 were waited for; matrix products, arithmetic and copies ran while one was open for 0% of the time, Pallas kernels for 2%

profile of v2, /device:TPU:0, one launch (start us, length us, event | category | flops | bytes accessed | tf_op | source)
XLA Modules:
  0.0 44.9 jit_solution(1904700046405500368)
XLA Ops:
  0.6 0.0 copy-start
  1.3 0.0 copy-start.3
  1.4 0.8 %copy-done.3 = f32[16,1024]{1,0:T(8,128)S(1)} copy-done((f32[16,1024]{1,0:T(8,128)S(1)}, f32[16,1024]{1,0:T(8,128)}, u32[]{:S(2)}) %copy-start.3) | copy-done | bytes 65560
  2.2 0.7 %pick.1 = (f32[8,8,1024]{2,1,0:T(8,128)S(1)}, f32[8,128]{1,0:T(8,128)S(1)}) custom-call(s32[2,4]{1,0:T(2,128)} %index.1, f32[1]{0:T(128)S(6)} %copy.8.gamma, f32[16,1024]{1,0:T(8,128)S(1)} %copy-done.3), custom_call_target="tpu_custom_call" | custom-call | tf_op jit(solution)/shard_map/pick/pallas_call | solution.py:31
  2.9 0.0 copy-start.2
  2.9 16.0 %all_to_all.15 = f32[8,8,1024]{2,1,0:T(8,128)S(1)} all-to-all(f32[8,8,1024]{2,1,0:T(8,128)S(1)} %get-tuple-element.9), channel_id=1, replica_groups=mesh['groups'=2,'center'=8,'row'=2] {'center'}, dimensions={0} | all-to-all | bytes 524288 | tf_op jit(solution)/shard_map/all_to_all | solution.py:60
  18.9 0.0 copy-done
  18.9 0.0 copy-done.2
  18.9 0.0 copy-start.1
  18.9 0.7 %kernel.1.made = f32[80,128]{1,0:T(8,128)S(1)} custom-call(f32[8,128]{1,0:T(8,128)S(1)} %get-tuple-element.8.gamma, f32[64,1024]{1,0:T(8,128)S(1)} %bitcast.1, f32[128,1024]{1,0:T(8,128)S(1)} %copy-done, f32[2,4,512]{2,1,0:T(4,128)S(1)} %copy-done.2), custom_call_target="tpu_custom_call" | custom-call | tf_op jit(solution)/shard_map/kernel/pallas_call | solution.py:31
  19.6 0.1 collective-permute-start
  19.7 1.2 %collective-permute-done.swapped = f32[80,128]{1,0:T(8,128)S(1)} collective-permute-done((f32[80,128]{1,0:T(8,128)S(1)}, f32[80,128]{1,0:T(8,128)S(1)}, u32[]{:S(2)}, u32[]{:S(2)}) %collective-permute-start) | collective-permute-done | bytes 40992 | tf_op jit(solution)/shard_map/ppermute | solution.py:56
  20.9 0.0 copy-done.1
  20.9 0.4 predict.1
  21.4 11.2 %all_to_all.16.got = f32[8,40,128]{2,1,0:T(8,128)S(1)} all-to-all(f32[8,40,128]{2,1,0:T(8,128)S(1)} %predict.1), channel_id=1, replica_groups=mesh['groups'=2,'center'=8,'row'=2] {'center'}, dimensions={0} | all-to-all | bytes 327680 | tf_op jit(solution)/shard_map/all_to_all | solution.py:60
  32.6 10.3 %all_to_all.17.full = f32[8,40,128]{2,1,0:T(8,128)S(1)} all-to-all(f32[8,40,128]{2,1,0:T(8,128)S(1)} %residual.1), channel_id=1, replica_groups=mesh['groups'=2,'center'=8,'row'=2] {'center'}, dimensions={0} | all-to-all | bytes 327680 | tf_op jit(solution)/shard_map/all_to_all | solution.py:60
  42.9 0.2 second.1
  43.1 0.1 collective-permute-start.1
  43.1 1.0 %update.1 = f32[128,256]{1,0:T(8,128)} custom-call(f32[80,128]{1,0:T(8,128)S(1)} %kernel.1.made, f32[80,128]{1,0:T(8,128)S(1)} %collective-permute-done.swapped, f32[64,256]{1,0:T(8,128)S(1)} %get-tuple-element.10.res_own, f32[64,256]{1,0:T(8,128)S(1)} %get-tuple-element.11.res_other, f32[128,256]{1,0:T(8,128)S(1)} %copy-done.1), custom_call_target="tpu_custom_call" | custom-call | tf_op jit(solution)/shard_map/update/pallas_call | solution.py:31
  44.1 0.2 collective-permute-done.1.back
  44.3 0.6 %finish.1 = f32[4,512]{1,0:T(4,128)} custom-call(f32[4,256]{1,0:T(4,128)S(1)} %get-tuple-element.12.mine, f32[4,256]{1,0:T(4,128)S(1)} %collective-permute-done.1.back), custom_call_target="tpu_custom_call" | custom-call | tf_op jit(solution)/shard_map/finish/pallas_call | solution.py:31
  (1 shorter events, 0.0 us)
Async XLA Ops:
  0.6 18.3 %copy-start = (f32[128,1024]{1,0:T(8,128)S(1)}, f32[128,1024]{1,0:T(8,128)}, u32[]{:S(2)}) copy-start(f32[128,1024]{1,0:T(8,128)} %centers.1) | copy-start | bytes 1572868
  1.3 0.8 %copy-start.3 = (f32[16,1024]{1,0:T(8,128)S(1)}, f32[16,1024]{1,0:T(8,128)}, u32[]{:S(2)}) copy-start(f32[16,1024]{1,0:T(8,128)} %dataset.1) | copy-start | bytes 196612
  2.9 16.0 %copy-start.2 = (f32[2,4,512]{2,1,0:T(4,128)S(1)}, f32[2,4,512]{2,1,0:T(4,128)}, u32[]{:S(2)}) copy-start(f32[2,4,512]{2,1,0:T(4,128)} %targets.3) | copy-start | bytes 49156
  18.9 2.0 %copy-start.1 = (f32[128,256]{1,0:T(8,128)S(1)}, f32[128,256]{1,0:T(8,128)}, u32[]{:S(2)}) copy-start(f32[128,256]{1,0:T(8,128)} %weights.3) | copy-start | bytes 393220
  19.6 1.3 %collective-permute-start = (f32[80,128]{1,0:T(8,128)S(1)}, f32[80,128]{1,0:T(8,128)S(1)}, u32[]{:S(2)}, u32[]{:S(2)}) collective-permute-start(f32[80,128]{1,0:T(8,128)S(1)} %kernel.1.made), channel_id=1, source_target_pairs={{0,1},{1,0},{2,3},{3,2},{4,5},{5,4},{6,7},{7,6},{8,9},{9,8},{10,11... | collective-permute-start | bytes 122888 | tf_op jit(solution)/shard_map/ppermute | solution.py:56
  43.1 1.2 %collective-permute-start.1 = (f32[4,256]{1,0:T(4,128)S(1)}, f32[4,256]{1,0:T(4,128)S(1)}, u32[]{:S(2)}, u32[]{:S(2)}) collective-permute-start(f32[4,256]{1,0:T(4,128)S(1)} %get-tuple-element.13), channel_id=1, source_target_pairs={{0,1},{1,0},{2,3},{3,2},{4,5},{5,4},{6,7},{7,6},{8,9},{9,8},{10,11... | collective-permute-start | bytes 12296 | tf_op jit(solution)/shard_map/ppermute | solution.py:56

commit v3 on v0

v3 whole, which is shorter than its diff:
```python
import functools
import math
from typing import NamedTuple

import jax
import jax.numpy as jnp
from jax import lax
from jax.experimental import pallas as pl
from jax.experimental.pallas import tpu as pltpu
from jax.sharding import PartitionSpec as P

LANES = 128
QUAD = 4
KEPT_BYTES = 1 << 20


class Plan(NamedTuple):
    high: int
    each: int
    col_tiles: int
    width: int
    pack: int

    @property
    def sums(self):
        return 2 * self.col_tiles * self.high

    @property
    def gram_rows(self):
        return self.high // self.pack

    @property
    def gram_tiles(self):
        return self.width * self.pack // LANES

    @property
    def tiles(self):
        return self.sums + self.gram_rows * self.gram_tiles


def dot(a, b, contract):
    return lax.dot_general(
        a,
        b,
        (contract, ((), ())),
        precision=lax.Precision.HIGHEST,
        preferred_element_type=jnp.float32,
    )


def small(x):
    return math.prod(x.shape) * 4 <= KEPT_BYTES


def call(body, outs, name, *args, **kwargs):
    args = [a if isinstance(a, tuple) else (a, pltpu.VMEM) for a in args]
    return pl.pallas_call(
        body,
        out_shape=outs,
        in_specs=[pl.BlockSpec(memory_space=space) for _, space in args],
        out_specs=[pl.BlockSpec(memory_space=pltpu.VMEM)] * len(outs),
        name=name,
        **kwargs,
    )(
        *[
            pltpu.with_memory_space_constraint(a, space)
            if space == pltpu.VMEM and small(a)
            else a
            for a, space in args
        ]
    )


def stored(*shape):
    return jax.ShapeDtypeStruct(shape, jnp.float32)


def kept(*shape):
    return pltpu.VMEM(shape, jnp.float32) if small(stored(*shape)) else stored(*shape)


def swap_cores(x):
    return lax.ppermute(x, "row", [(0, 1), (1, 0)])


def partner(x, bits):
    return lax.ppermute(x, "center", [(i, i ^ bits) for i in range(lax.axis_size("center"))])


def xor_lanes(tiles, stride):
    if stride >= LANES:
        return [tiles[i ^ (stride // LANES)] for i in range(len(tiles))]
    lane = lax.broadcasted_iota(jnp.int32, tiles[0].shape, tiles[0].ndim - 1)
    axis = tiles[0].ndim - 1
    return [
        jnp.where(
            lane & stride != 0, pltpu.roll(t, stride, axis), pltpu.roll(t, LANES - stride, axis)
        )
        for t in tiles
    ]


def seen_by(plan, tiles, q):
    for bit in (1, 2):
        if q & bit:
            tiles = xor_lanes(tiles, bit * plan.high * plan.each)
    return tiles


def pick_body(index, gamma, dataset, out, spread, index_s, gamma_s, data, sems):
    copies = [
        pltpu.make_async_copy(a, b, sems.at[i])
        for i, (a, b) in enumerate(((index, index_s), (gamma, gamma_s), (dataset, data)))
    ]
    for c in copies:
        c.start()
    for c in copies:
        c.wait()
    spread[...] = jnp.full(spread.shape, gamma_s[0])
    batches, count = index.shape
    for b in range(batches):
        for j in range(count):
            at = b * count + j
            out[at : at + 1] = data[pl.ds(index_s[b, j], 1), :]


def center_body(centers, out):
    c = centers[...]
    count = c.shape[0]
    sq = jnp.sum(c * c, axis=1, keepdims=True)
    out[...] = jnp.broadcast_to(sq, (count, LANES)).T[: out.shape[0]]


def kernel_body(gamma, rows, centers, center_sq, out):
    x = rows[...]
    row_sq = jnp.sum(x * x, axis=1, keepdims=True)
    cross = dot(x, centers[...], ((1,), (1,)))
    out[...] = jnp.exp(-gamma[:1] * (row_sq + center_sq[:1] - 2.0 * cross))


def target_rows(targets, side):
    cols = targets.shape[2] // 2
    both = jnp.concatenate([targets[b] for b in range(targets.shape[0])], 0)
    half = jnp.where(side == 0, both[:, :cols], both[:, cols:])
    return [half[:, i : i + LANES] for i in range(0, cols, LANES)]


def target_body(targets, out):
    for i, tile in enumerate(target_rows(targets, 1 - lax.axis_index("row"))):
        out[i * tile.shape[0] : (i + 1) * tile.shape[0]] = tile


def by_batch(own, other):
    axis = own.ndim - 2
    half = own.shape[axis] // 2
    low = lax.broadcasted_iota(jnp.int32, own.shape, axis) < half
    return (
        jnp.where(low, own, pltpu.roll(other, half, axis)),
        jnp.where(low, pltpu.roll(own, half, axis), other),
    )


def predict_body(plan, own, swapped, weights, wanted, targets, k0_out, k1_out, *outs):
    each, high = plan.each, plan.high
    n, count = own.shape
    tiled = lambda x: x.reshape(n // each, each, count)
    k0, k1 = (k.reshape(n, count) for k in by_batch(tiled(own[...]), tiled(swapped[...])))
    k0_out[...] = k0
    k1_out[...] = k1
    w = weights[...]
    span = high * each
    for b, k in enumerate((k0, k1)):
        part = dot(k, w, ((1,), (0,)))
        for q, out in enumerate(outs):
            for c in range(plan.col_tiles):
                tile = part[q * span : (q + 1) * span, c * LANES : (c + 1) * LANES]
                at = (b * plan.col_tiles + c) * high
                out[at : at + high] = tile.reshape(high, each, LANES)
    for c, mine in enumerate(target_rows(targets, lax.axis_index("row"))):
        for b, tile in enumerate(by_batch(mine, wanted[c * each : (c + 1) * each])):
            at = (b * plan.col_tiles + c) * high
            outs[0][at] = outs[0][at] - tile
    gram = dot(k1, jnp.concatenate([k0] * plan.pack, 0), ((1,), (1,)))
    for q, out in enumerate(outs):
        rows = gram[q * span : (q + 1) * span]
        rows = rows.reshape(plan.gram_rows, plan.pack, each, rows.shape[1])
        lane = lax.broadcasted_iota(jnp.int32, rows.shape[:1] + rows.shape[2:], 2)
        packed = rows[:, 0]
        for i in range(1, plan.pack):
            packed = jnp.where(lane >= i * plan.width, rows[:, i], packed)
        tiles = [packed[:, :, i : i + LANES] for i in range(0, packed.shape[2], LANES)]
        for u, tile in enumerate(seen_by(plan, tiles, q)):
            at = plan.sums + u * plan.gram_rows
            out[at : at + plan.gram_rows] = tile


def quad_body(own, *refs):
    *others, out = refs
    total = own[...]
    for other in others:
        total = total + other[...]
    out[...] = total


def high_body(plan, bit, mine, other, out):
    for at in range(0, plan.sums, plan.high):
        for h in range(plan.high):
            out[at + h] = mine[at + h] + other[at + (h ^ bit)]
    t = plan.gram_rows
    step = bit // plan.pack
    for r in range(t):
        tiles = [other[plan.sums + u * t + (r ^ step)] for u in range(plan.gram_tiles)]
        if bit < plan.pack:
            tiles = xor_lanes(tiles, bit * plan.width)
        for u, tile in enumerate(xor_lanes(tiles, bit * plan.each)):
            out[plan.sums + u * t + r] = mine[plan.sums + u * t + r] + tile


def second_body(plan, rate, *refs):
    *packets, out0, out1, mine_out, theirs_out = refs
    span = plan.high * plan.each
    half = plan.each // 2
    for b, out in enumerate((out0, out1)):
        for q, packet in enumerate(packets):
            for c in range(plan.col_tiles):
                at = (b * plan.col_tiles + c) * plan.high
                out[q * span : (q + 1) * span, c * LANES : (c + 1) * LANES] = packet[
                    at : at + plan.high
                ].reshape(span, LANES)
    res0 = out0[...]
    res0 = jnp.concatenate([res0] * plan.pack, 0)
    t = plan.gram_rows
    grams = []
    for q, packet in enumerate(packets):
        tiles = [
            packet[plan.sums + u * t : plan.sums + (u + 1) * t] for u in range(plan.gram_tiles)
        ]
        tiles = seen_by(plan, tiles, q)
        packed = jnp.concatenate(tiles, 2)
        lane = lax.broadcasted_iota(jnp.int32, packed.shape, 2) // plan.width
        rows = [jnp.where(lane == i, packed, 0.0) for i in range(plan.pack)]
        grams.append(jnp.stack(rows, 1).reshape(span, packed.shape[2]))
    gram = jnp.concatenate(grams, 0)
    out1[...] = out1[...] - rate * dot(gram, res0, ((1,), (0,)))
    mine_out[...] = out1[:half]
    theirs_out[...] = out1[half : 2 * half]


def update_body(rate, k0, k1, res0, res1, weights, out):
    grad = dot(k0[...], res0[...], ((0,), (0,))) + dot(k1[...], res1[...], ((0,), (0,)))
    out[...] = weights[...] - rate * grad


def finish_body(mine, back, out):
    first = lax.axis_index("row") == 0
    a, b = mine[...], back[...]
    cols = a.shape[1]
    out[:, :cols] = jnp.where(first, a, b)
    out[:, cols:] = jnp.where(first, b, a)


def per_device(dataset, centers, weights, batch_index, targets, gamma):
    shards = lax.axis_size("center")
    cores = lax.axis_size("row")
    batches, rows_here = batch_index.shape
    assert cores == 2 and batches == 2 and shards % QUAD == 0 and shards & (shards - 1) == 0
    features = dataset.shape[1]
    count, cols = weights.shape
    each = batches * rows_here
    high = shards // QUAD
    span = high * each
    n = shards * each
    width = shards * cores * rows_here
    rate = 0.5 / width
    plan = Plan(high, each, cols // LANES, width, max(1, LANES // width))
    quad = range(1, QUAD)
    bits = [1 << i for i in range(high.bit_length() - 1)]

    local, spread = call(
        pick_body,
        [kept(each, features), kept(8, count)],
        "pick",
        (batch_index, pl.ANY),
        (gamma, pl.ANY),
        (dataset, pl.ANY),
        scratch_shapes=[
            pltpu.SMEM(batch_index.shape, jnp.int32),
            pltpu.SMEM(gamma.shape, jnp.float32),
            pltpu.VMEM(dataset.shape, jnp.float32),
            pltpu.SemaphoreType.DMA((3,)),
        ],
    )
    rows = local
    for bit in bits:
        rows = jnp.concatenate([rows, partner(rows, QUAD * bit)], 0)
    blocks = [rows] + [partner(rows, q) for q in quad]

    (center_sq,) = call(center_body, [kept(8, count)], "center_sq", centers)
    (half,) = call(target_body, [kept(each * plan.col_tiles, LANES)], "targets", targets)
    wanted = swap_cores(half)
    own = [
        call(kernel_body, [kept(span, count)], "kernel", spread, x, centers, center_sq)[0]
        for x in blocks
    ]
    own = jnp.concatenate(own, 0)
    swapped = swap_cores(own)
    packet = (plan.tiles, each, LANES)
    k0, k1, keep, *sent = call(
        functools.partial(predict_body, plan),
        [kept(n, count)] * 2 + [kept(*packet)] * QUAD,
        "predict",
        own,
        swapped,
        weights,
        wanted,
        targets,
    )
    (total,) = call(
        quad_body, [kept(*packet)], "quad", keep, *[partner(s, q) for q, s in zip(quad, sent)]
    )
    for bit in bits:
        (total,) = call(
            functools.partial(high_body, plan, bit),
            [kept(*packet)],
            "high",
            total,
            partner(total, QUAD * bit),
        )
    res0, res1, mine, theirs = call(
        functools.partial(second_body, plan, rate),
        [kept(n, cols)] * 2 + [kept(rows_here, cols)] * 2,
        "second",
        total,
        *[partner(total, q) for q in quad],
    )
    back = swap_cores(theirs)
    (new_weights,) = call(
        functools.partial(update_body, rate),
        [stored(count, cols)],
        "update",
        k0,
        k1,
        res0,
        res1,
        weights,
    )
    (residual,) = call(finish_body, [stored(rows_here, 2 * cols)], "finish", mine, back)
    return (new_weights, residual)


def solution(mesh):
    return jax.shard_map(
        per_device,
        mesh=mesh,
        in_specs=(
            P(("groups", "center", "row"), None),
            P(("groups", "center"), None),
            P(("groups", "center"), "row"),
            P(None, ("groups", "center", "row")),
            P(None, ("groups", "center", "row"), None),
            P("groups"),
        ),
        out_specs=(P(("groups", "center"), "row"), P(("groups", "center", "row"), None)),
        check_vma=False,
    )
```

time: 242 us -> 40.5 us (0.17)
  blocking collectives: 128 us -> 0 us
  waiting for transfers between devices: 85.2 us -> 12.9 us
  starting transfers between devices: 0.16 us -> 17.7 us
  between operations: 14.5 us -> 1.36 us
  matrix products: 6.1 us -> 0 us
  Pallas kernels: 0 us -> 5.73 us
  other arithmetic: 4.76 us -> 0.01 us
    all_gather x6 -> x0, blocking collectives: 128 us -> none  [the longest x2 62.9 us: per_device(): lax.all_gather(local_rows, 'center', axis=0, tiled=True)]
    psum x2 -> x0, waiting for transfers between devices: 77.8 us -> none  [per_device(): summed = lax.psum(partial_pred, 'center')]
    ppermute x0 -> x14, starting transfers between devices: none -> 17.7 us  [the longest x11 17.5 us: partner(): lax.ppermute(x, 'center', [(i, i ^ bits) for i in range(lax.axis_size('ce...]
    ppermute x0 -> x14, waiting for transfers between devices: none -> 12.9 us  [the longest x11 11.6 us: partner(): lax.ppermute(x, 'center', [(i, i ^ bits) for i in range(lax.axis_size('ce...]
    reduce_scatter x2 -> x0, waiting for transfers between devices: 7.25 us -> none  [per_device(): own_grad = lax.psum_scatter(grad, 'row', scatter_dimension=1, tiled=True)]
    dot_general x6 -> x0, matrix products: 6.1 us -> none  [the longest x2 3.07 us: per_device(): jnp.dot(kernel.T, gathered_res, precision=lax.Precision.HIGHEST, preferre...]
    pallas_call x0 -> x13, Pallas kernels: none -> 5.73 us  [call(): pl.pallas_call(body, out_shape=outs, in_specs=[pl.BlockSpec(memory_space=...]
    sub x3 -> x0, other arithmetic: 3.35 us -> none  [the longest x2 2.5 us: per_device(): current = current - 0.5 / batch_total * own_grad]
  transfers between devices with their start and end apart: 4 -> 14, of which waited for: 3 -> 11; matrix products, arithmetic and copies ran while one was open for 1% -> 0% of each run, Pallas kernels for 0% -> 7%
where the time goes in v3:
time: 40.5 us; the launch traced here: 40.2 us
  starting transfers between devices  17.7 us (44%)
  waiting for transfers between devices  12.9 us (32%)
  Pallas kernels  5.73 us (14%)
  local copies, waits for them, and re-layouts  2.59 us (6%)
  between operations  1.36 us (3%)
    ppermute x11, starting transfers between devices, partner(): lax.ppermute(x, 'center', [(i, i ^ bits) for i in range(lax.axis_size('ce...  17.5 us
    ppermute x11, waiting for transfers between devices, partner(): lax.ppermute(x, 'center', [(i, i ^ bits) for i in range(lax.axis_size('ce...  11.6 us
    pallas_call x13, Pallas kernels, call(): pl.pallas_call(body, out_shape=outs, in_specs=[pl.BlockSpec(memory_space=...  5.73 us
    unnamed x9, local copies, waits for them, and re-layouts  2.59 us
    ppermute x3, waiting for transfers between devices, swap_cores(): return lax.ppermute(x, 'row', [(0, 1), (1, 0)])  1.24 us
  transfers between devices with their start and end apart: 14, of which 11 were waited for; matrix products, arithmetic and copies ran while one was open for 0% of the time, Pallas kernels for 7%

profile of v3, /device:TPU:0, one launch (start us, length us, event | category | flops | bytes accessed | tf_op | source)
XLA Modules:
  0.0 40.2 jit_solution(6302597863528084960)
XLA Ops:
  1.3 0.9 %pick.1 = (f32[8,1024]{1,0:T(8,128)S(1)}, f32[8,128]{1,0:T(8,128)S(1)}) custom-call(s32[2,4]{1,0:T(2,128)} %index.1, f32[1]{0:T(128)S(6)} %copy.9.gamma, f32[16,1024]{1,0:T(8,128)} %dataset.1), custom_call_target="tpu_custom_call" | custom-call | tf_op jit(solution)/shard_map/pick/pallas_call | solution.py:57
  2.2 4.1 %collective-permute-start = (f32[8,1024]{1,0:T(8,128)S(1)}, f32[8,1024]{1,0:T(8,128)S(1)}, u32[]{:S(2)}, u32[]{:S(2)}) collective-permute-start(f32[8,1024]{1,0:T(8,128)S(1)} %get-tuple-element.15), channel_id=1, source_target_pairs={{0,8},{2,10},{4,12},{6,14},{8,0},{10,2},{12,4},{14,6},{1,9},{3,11}... | collective-permute-start | bytes 98312 | tf_op jit(solution)/shard_map/ppermute | solution.py:87
  6.3 2.2 %collective-permute-done = f32[8,1024]{1,0:T(8,128)S(1)} collective-permute-done((f32[8,1024]{1,0:T(8,128)S(1)}, f32[8,1024]{1,0:T(8,128)S(1)}, u32[]{:S(2)}, u32[]{:S(2)}) %collective-permute-start) | collective-permute-done | bytes 32800 | tf_op jit(solution)/shard_map/ppermute | solution.py:87
  8.5 2.5 %collective-permute-start.3 = (f32[16,1024]{1,0:T(8,128)S(1)}, f32[16,1024]{1,0:T(8,128)S(1)}, u32[]{:S(2)}, u32[]{:S(2)}) collective-permute-start(f32[16,1024]{1,0:T(8,128)S(1)} %constant_dynamic-update-slice_fusion.rows), channel_id=1, source_target_pairs={{0,6},{2,4},{4,2},{6,0},{8,14},{10,12},{12,10},{14,8},{1,7},{3,5},... | collective-permute-start | bytes 196616 | tf_op jit(solution)/shard_map/ppermute | solution.py:87
  11.0 0.7 %collective-permute-start.2 = (f32[16,1024]{1,0:T(8,128)S(1)}, f32[16,1024]{1,0:T(8,128)S(1)}, u32[]{:S(2)}, u32[]{:S(2)}) collective-permute-start(f32[16,1024]{1,0:T(8,128)S(1)} %constant_dynamic-update-slice_fusion.rows), channel_id=1, source_target_pairs={{0,4},{2,6},{4,0},{6,2},{8,12},{10,14},{12,8},{14,10},{1,5},{3,7},... | collective-permute-start | bytes 196616 | tf_op jit(solution)/shard_map/ppermute | solution.py:87
  11.7 0.3 collective-permute-start.1
  12.0 0.0 copy-start
  12.0 1.0 %copy-done = f32[128,1024]{1,0:T(8,128)S(1)} copy-done((f32[128,1024]{1,0:T(8,128)S(1)}, f32[128,1024]{1,0:T(8,128)}, u32[]{:S(2)}) %copy-start) | copy-done | bytes 524312
  13.1 0.0 copy-start.1
  13.1 0.1 center_sq.1
  13.2 0.9 %copy-done.1 = f32[128,1024]{1,0:T(8,128)S(1)} copy-done((f32[128,1024]{1,0:T(8,128)S(1)}, f32[128,1024]{1,0:T(8,128)}, u32[]{:S(2)}) %copy-start.1) | copy-done | bytes 524312
  14.1 0.5 %kernel.4 = f32[16,128]{1,0:T(8,128)S(1)} custom-call(f32[8,128]{1,0:T(8,128)S(1)} %get-tuple-element.14.gamma, f32[16,1024]{1,0:T(8,128)S(1)} %constant_dynamic-update-slice_fusion.rows, f32[128,1024]{1,0:T(8,128)S(1)} %copy-done.1, f32[8,128]{1,0:T(8,128)S(1)} %center_sq.1), custom_call_target="tpu_custom_call" | custom-call | tf_op jit(solution)/shard_map/kernel/pallas_call | solution.py:57
  14.6 0.0 collective-permute-done.3.rows
  14.7 0.5 %kernel.7 = f32[16,128]{1,0:T(8,128)S(1)} custom-call(f32[8,128]{1,0:T(8,128)S(1)} %get-tuple-element.14.gamma, f32[16,1024]{1,0:T(8,128)S(1)} %collective-permute-done.3.rows, f32[128,1024]{1,0:T(8,128)S(1)} %copy-done.1, f32[8,128]{1,0:T(8,128)S(1)} %center_sq.1), custom_call_target="tpu_custom_call" | custom-call | tf_op jit(solution)/shard_map/kernel/pallas_call | solution.py:57
  15.2 0.1 collective-permute-done.2.rows
  15.3 0.5 %kernel.6 = f32[16,128]{1,0:T(8,128)S(1)} custom-call(f32[8,128]{1,0:T(8,128)S(1)} %get-tuple-element.14.gamma, f32[16,1024]{1,0:T(8,128)S(1)} %collective-permute-done.2.rows, f32[128,1024]{1,0:T(8,128)S(1)} %copy-done.1, f32[8,128]{1,0:T(8,128)S(1)} %center_sq.1), custom_call_target="tpu_custom_call" | custom-call | tf_op jit(solution)/shard_map/kernel/pallas_call | solution.py:57
  15.8 0.2 collective-permute-done.1.rows
  16.0 0.0 copy-start.2
  16.0 0.5 %kernel.5 = f32[16,128]{1,0:T(8,128)S(1)} custom-call(f32[8,128]{1,0:T(8,128)S(1)} %get-tuple-element.14.gamma, f32[16,1024]{1,0:T(8,128)S(1)} %collective-permute-done.1.rows, f32[128,1024]{1,0:T(8,128)S(1)} %copy-done.1, f32[8,128]{1,0:T(8,128)S(1)} %center_sq.1), custom_call_target="tpu_custom_call" | custom-call | tf_op jit(solution)/shard_map/kernel/pallas_call | solution.py:57
  16.5 0.0 copy-start.3
  16.5 0.1 collective-permute-start.4
  16.6 0.6 %copy-done.3 = f32[2,4,512]{2,1,0:T(4,128)S(1)} copy-done((f32[2,4,512]{2,1,0:T(4,128)S(1)}, f32[2,4,512]{2,1,0:T(4,128)}, u32[]{:S(2)}) %copy-start.3) | copy-done | bytes 16408
  17.2 0.0 collective-permute-start.5
  17.2 1.2 %collective-permute-done.5.wanted = f32[16,128]{1,0:T(8,128)S(1)} collective-permute-done((f32[16,128]{1,0:T(8,128)S(1)}, f32[16,128]{1,0:T(8,128)S(1)}, u32[]{:S(2)}, u32[]{:S(2)}) %collective-permute-start.5) | collective-permute-done | bytes 8224 | tf_op jit(solution)/shard_map/ppermute | solution.py:83
  18.4 0.0 collective-permute-done.4.swapped
  18.4 0.0 copy-done.2
  18.4 0.5 %predict.1 = (f32[64,128]{1,0:T(8,128)S(1)}, f32[64,128]{1,0:T(8,128)S(1)}, f32[9,8,128]{2,1,0:T(8,128)S(1)}, f32[9,8,128]{2,1,0:T(8,128)S(1)}, f32[9,8,128]{2,1,0:T(8,128)S(1)}, /*index=5*/f32[9,8,128]{2,1,0:T(8,128)S(1)}) custom-call(f32[64,128]{1,0:T(8,128)S(1)} %pad_maximum_fusion.own, f32[64,128]{1,0:T(8,128)S(1)} %collective-permute-done.4.swapped, ...), custom_call_target="tpu_custom_call" | custom-call | tf_op jit(solution)/shard_map/predict/pallas_call | solution.py:57
  18.9 1.5 %collective-permute-start.6 = (f32[9,8,128]{2,1,0:T(8,128)S(1)}, f32[9,8,128]{2,1,0:T(8,128)S(1)}, u32[]{:S(2)}, u32[]{:S(2)}) collective-permute-start(f32[9,8,128]{2,1,0:T(8,128)S(1)} %get-tuple-element.19), channel_id=1, source_target_pairs={{0,2},{2,0},{4,6},{6,4},{8,10},{10,8},{12,14},{14,12},{1,3},{3,1},... | collective-permute-start | bytes 110600 | tf_op jit(solution)/shard_map/ppermute | solution.py:87
  20.4 1.3 %collective-permute-start.7 = (f32[9,8,128]{2,1,0:T(8,128)S(1)}, f32[9,8,128]{2,1,0:T(8,128)S(1)}, u32[]{:S(2)}, u32[]{:S(2)}) collective-permute-start(f32[9,8,128]{2,1,0:T(8,128)S(1)} %get-tuple-element.20), channel_id=1, source_target_pairs={{0,4},{2,6},{4,0},{6,2},{8,12},{10,14},{12,8},{14,10},{1,5},{3,7},... | collective-permute-start | bytes 110600 | tf_op jit(solution)/shard_map/ppermute | solution.py:87
  21.8 0.7 %collective-permute-start.8 = (f32[9,8,128]{2,1,0:T(8,128)S(1)}, f32[9,8,128]{2,1,0:T(8,128)S(1)}, u32[]{:S(2)}, u32[]{:S(2)}) collective-permute-start(f32[9,8,128]{2,1,0:T(8,128)S(1)} %get-tuple-element.21), channel_id=1, source_target_pairs={{0,6},{2,4},{4,2},{6,0},{8,14},{10,12},{12,10},{14,8},{1,7},{3,5},... | collective-permute-start | bytes 110600 | tf_op jit(solution)/shard_map/ppermute | solution.py:87
  22.4 0.5 %collective-permute-done.6.refs_0_ = f32[9,8,128]{2,1,0:T(8,128)S(1)} collective-permute-done((f32[9,8,128]{2,1,0:T(8,128)S(1)}, f32[9,8,128]{2,1,0:T(8,128)S(1)}, u32[]{:S(2)}, u32[]{:S(2)}) %collective-permute-start.6) | collective-permute-done | bytes 36896 | tf_op jit(solution)/shard_map/ppermute | solution.py:87
  22.9 1.8 %collective-permute-done.7.refs_1_ = f32[9,8,128]{2,1,0:T(8,128)S(1)} collective-permute-done((f32[9,8,128]{2,1,0:T(8,128)S(1)}, f32[9,8,128]{2,1,0:T(8,128)S(1)}, u32[]{:S(2)}, u32[]{:S(2)}) %collective-permute-start.7) | collective-permute-done | bytes 36896 | tf_op jit(solution)/shard_map/ppermute | solution.py:87
  24.7 1.9 %collective-permute-done.8.refs_2_ = f32[9,8,128]{2,1,0:T(8,128)S(1)} collective-permute-done((f32[9,8,128]{2,1,0:T(8,128)S(1)}, f32[9,8,128]{2,1,0:T(8,128)S(1)}, u32[]{:S(2)}, u32[]{:S(2)}) %collective-permute-start.8) | collective-permute-done | bytes 36896 | tf_op jit(solution)/shard_map/ppermute | solution.py:87
  26.6 2.9 %collective-permute-start.9 = (f32[9,8,128]{2,1,0:T(8,128)S(1)}, f32[9,8,128]{2,1,0:T(8,128)S(1)}, u32[]{:S(2)}, u32[]{:S(2)}) collective-permute-start(f32[9,8,128]{2,1,0:T(8,128)S(1)} %quad.1.mine), channel_id=1, source_target_pairs={{0,8},{2,10},{4,12},{6,14},{8,0},{10,2},{12,4},{14,6},{1,9},{3,11}... | collective-permute-start | bytes 110600 | tf_op jit(solution)/shard_map/ppermute | solution.py:87
  29.5 2.4 %collective-permute-done.9.other = f32[9,8,128]{2,1,0:T(8,128)S(1)} collective-permute-done((f32[9,8,128]{2,1,0:T(8,128)S(1)}, f32[9,8,128]{2,1,0:T(8,128)S(1)}, u32[]{:S(2)}, u32[]{:S(2)}) %collective-permute-start.9) | collective-permute-done | bytes 36896 | tf_op jit(solution)/shard_map/ppermute | solution.py:87
  31.9 0.1 high.1.refs_0_
  32.1 0.4 collective-permute-start.12
  32.5 1.6 %collective-permute-start.11 = (f32[9,8,128]{2,1,0:T(8,128)S(1)}, f32[9,8,128]{2,1,0:T(8,128)S(1)}, u32[]{:S(2)}, u32[]{:S(2)}) collective-permute-start(f32[9,8,128]{2,1,0:T(8,128)S(1)} %high.1.refs_0_), channel_id=1, source_target_pairs={{0,4},{2,6},{4,0},{6,2},{8,12},{10,14},{12,8},{14,10},{1,5},{3,7},... | collective-permute-start | bytes 110600 | tf_op jit(solution)/shard_map/ppermute | solution.py:87
  34.1 1.5 %collective-permute-start.10 = (f32[9,8,128]{2,1,0:T(8,128)S(1)}, f32[9,8,128]{2,1,0:T(8,128)S(1)}, u32[]{:S(2)}, u32[]{:S(2)}) collective-permute-start(f32[9,8,128]{2,1,0:T(8,128)S(1)} %high.1.refs_0_), channel_id=1, source_target_pairs={{0,2},{2,0},{4,6},{6,4},{8,10},{10,8},{12,14},{14,12},{1,3},{3,1},... | collective-permute-start | bytes 110600 | tf_op jit(solution)/shard_map/ppermute | solution.py:87
  35.6 1.4 %collective-permute-done.12.refs_3_ = f32[9,8,128]{2,1,0:T(8,128)S(1)} collective-permute-done((f32[9,8,128]{2,1,0:T(8,128)S(1)}, f32[9,8,128]{2,1,0:T(8,128)S(1)}, u32[]{:S(2)}, u32[]{:S(2)}) %collective-permute-start.12) | collective-permute-done | bytes 36896 | tf_op jit(solution)/shard_map/ppermute | solution.py:87
  36.9 0.0 collective-permute-done.11.refs_2_
  36.9 1.1 %collective-permute-done.10.refs_1_ = f32[9,8,128]{2,1,0:T(8,128)S(1)} collective-permute-done((f32[9,8,128]{2,1,0:T(8,128)S(1)}, f32[9,8,128]{2,1,0:T(8,128)S(1)}, u32[]{:S(2)}, u32[]{:S(2)}) %collective-permute-start.10) | collective-permute-done | bytes 36896 | tf_op jit(solution)/shard_map/ppermute | solution.py:87
  38.1 0.3 second.1
  38.4 0.1 collective-permute-start.13
  38.5 1.1 %update.1 = f32[128,256]{1,0:T(8,128)} custom-call(f32[64,128]{1,0:T(8,128)S(1)} %get-tuple-element.16.k0, f32[64,128]{1,0:T(8,128)S(1)} %get-tuple-element.17.k1, f32[64,256]{1,0:T(8,128)S(1)} %get-tuple-element.22.res0, f32[64,256]{1,0:T(8,128)S(1)} %get-tuple-element.23.res1, f32[128,256]{1,0:T(8,128)S(1)} %copy-done.2), custom_call_target="tpu_custom_call" | custom-call | tf_op jit(solution)/shard_map/update/pallas_call | solution.py:57
  39.5 0.1 collective-permute-done.13.back
  39.6 0.6 %finish.1 = f32[4,512]{1,0:T(4,128)} custom-call(f32[4,256]{1,0:T(4,128)S(1)} %get-tuple-element.24.mine, f32[4,256]{1,0:T(4,128)S(1)} %collective-permute-done.13.back), custom_call_target="tpu_custom_call" | custom-call | tf_op jit(solution)/shard_map/finish/pallas_call | solution.py:57
  (5 shorter events, 0.0 us)
Async XLA Ops:
  2.2 6.4 %collective-permute-start = (f32[8,1024]{1,0:T(8,128)S(1)}, f32[8,1024]{1,0:T(8,128)S(1)}, u32[]{:S(2)}, u32[]{:S(2)}) collective-permute-start(f32[8,1024]{1,0:T(8,128)S(1)} %get-tuple-element.15), channel_id=1, source_target_pairs={{0,8},{2,10},{4,12},{6,14},{8,0},{10,2},{12,4},{14,6},{1,9},{3,11}... | collective-permute-start | bytes 98312 | tf_op jit(solution)/shard_map/ppermute | solution.py:87
  8.5 6.1 %collective-permute-start.3 = (f32[16,1024]{1,0:T(8,128)S(1)}, f32[16,1024]{1,0:T(8,128)S(1)}, u32[]{:S(2)}, u32[]{:S(2)}) collective-permute-start(f32[16,1024]{1,0:T(8,128)S(1)} %constant_dynamic-update-slice_fusion.rows), channel_id=1, source_target_pairs={{0,6},{2,4},{4,2},{6,0},{8,14},{10,12},{12,10},{14,8},{1,7},{3,5},... | collective-permute-start | bytes 196616 | tf_op jit(solution)/shard_map/ppermute | solution.py:87
  11.0 4.3 %collective-permute-start.2 = (f32[16,1024]{1,0:T(8,128)S(1)}, f32[16,1024]{1,0:T(8,128)S(1)}, u32[]{:S(2)}, u32[]{:S(2)}) collective-permute-start(f32[16,1024]{1,0:T(8,128)S(1)} %constant_dynamic-update-slice_fusion.rows), channel_id=1, source_target_pairs={{0,4},{2,6},{4,0},{6,2},{8,12},{10,14},{12,8},{14,10},{1,5},{3,7},... | collective-permute-start | bytes 196616 | tf_op jit(solution)/shard_map/ppermute | solution.py:87
  11.7 4.3 %collective-permute-start.1 = (f32[16,1024]{1,0:T(8,128)S(1)}, f32[16,1024]{1,0:T(8,128)S(1)}, u32[]{:S(2)}, u32[]{:S(2)}) collective-permute-start(f32[16,1024]{1,0:T(8,128)S(1)} %constant_dynamic-update-slice_fusion.rows), channel_id=1, source_target_pairs={{0,2},{2,0},{4,6},{6,4},{8,10},{10,8},{12,14},{14,12},{1,3},{3,1},... | collective-permute-start | bytes 196616 | tf_op jit(solution)/shard_map/ppermute | solution.py:87
  12.0 1.0 %copy-start = (f32[128,1024]{1,0:T(8,128)S(1)}, f32[128,1024]{1,0:T(8,128)}, u32[]{:S(2)}) copy-start(f32[128,1024]{1,0:T(8,128)} %centers.9) | copy-start | bytes 1572868
  13.1 1.0 %copy-start.1 = (f32[128,1024]{1,0:T(8,128)S(1)}, f32[128,1024]{1,0:T(8,128)}, u32[]{:S(2)}) copy-start(f32[128,1024]{1,0:T(8,128)} %centers.9) | copy-start | bytes 1572868
  16.0 2.4 %copy-start.2 = (f32[128,256]{1,0:T(8,128)S(1)}, f32[128,256]{1,0:T(8,128)}, u32[]{:S(2)}) copy-start(f32[128,256]{1,0:T(8,128)} %weights.3) | copy-start | bytes 393220
  16.5 0.7 %copy-start.3 = (f32[2,4,512]{2,1,0:T(4,128)S(1)}, f32[2,4,512]{2,1,0:T(4,128)}, u32[]{:S(2)}) copy-start(f32[2,4,512]{2,1,0:T(4,128)} %targets.5) | copy-start | bytes 49156
  16.5 1.9 %collective-permute-start.4 = (f32[64,128]{1,0:T(8,128)S(1)}, f32[64,128]{1,0:T(8,128)S(1)}, u32[]{:S(2)}, u32[]{:S(2)}) collective-permute-start(f32[64,128]{1,0:T(8,128)S(1)} %pad_maximum_fusion.own), channel_id=1, source_target_pairs={{0,1},{1,0},{2,3},{3,2},{4,5},{5,4},{6,7},{7,6},{8,9},{9,8},{10,11... | collective-permute-start | bytes 98312 | tf_op jit(solution)/shard_map/ppermute | solution.py:83
  17.2 1.2 %collective-permute-start.5 = (f32[16,128]{1,0:T(8,128)S(1)}, f32[16,128]{1,0:T(8,128)S(1)}, u32[]{:S(2)}, u32[]{:S(2)}) collective-permute-start(f32[16,128]{1,0:T(8,128)S(1)} %targets.3), channel_id=1, source_target_pairs={{0,1},{1,0},{2,3},{3,2},{4,5},{5,4},{6,7},{7,6},{8,9},{9,8},{10,11... | collective-permute-start | bytes 24584 | tf_op jit(solution)/shard_map/ppermute | solution.py:83
  18.9 4.0 %collective-permute-start.6 = (f32[9,8,128]{2,1,0:T(8,128)S(1)}, f32[9,8,128]{2,1,0:T(8,128)S(1)}, u32[]{:S(2)}, u32[]{:S(2)}) collective-permute-start(f32[9,8,128]{2,1,0:T(8,128)S(1)} %get-tuple-element.19), channel_id=1, source_target_pairs={{0,2},{2,0},{4,6},{6,4},{8,10},{10,8},{12,14},{14,12},{1,3},{3,1},... | collective-permute-start | bytes 110600 | tf_op jit(solution)/shard_map/ppermute | solution.py:87
  20.4 4.3 %collective-permute-start.7 = (f32[9,8,128]{2,1,0:T(8,128)S(1)}, f32[9,8,128]{2,1,0:T(8,128)S(1)}, u32[]{:S(2)}, u32[]{:S(2)}) collective-permute-start(f32[9,8,128]{2,1,0:T(8,128)S(1)} %get-tuple-element.20), channel_id=1, source_target_pairs={{0,4},{2,6},{4,0},{6,2},{8,12},{10,14},{12,8},{14,10},{1,5},{3,7},... | collective-permute-start | bytes 110600 | tf_op jit(solution)/shard_map/ppermute | solution.py:87
  21.8 4.9 %collective-permute-start.8 = (f32[9,8,128]{2,1,0:T(8,128)S(1)}, f32[9,8,128]{2,1,0:T(8,128)S(1)}, u32[]{:S(2)}, u32[]{:S(2)}) collective-permute-start(f32[9,8,128]{2,1,0:T(8,128)S(1)} %get-tuple-element.21), channel_id=1, source_target_pairs={{0,6},{2,4},{4,2},{6,0},{8,14},{10,12},{12,10},{14,8},{1,7},{3,5},... | collective-permute-start | bytes 110600 | tf_op jit(solution)/shard_map/ppermute | solution.py:87
  26.6 5.3 %collective-permute-start.9 = (f32[9,8,128]{2,1,0:T(8,128)S(1)}, f32[9,8,128]{2,1,0:T(8,128)S(1)}, u32[]{:S(2)}, u32[]{:S(2)}) collective-permute-start(f32[9,8,128]{2,1,0:T(8,128)S(1)} %quad.1.mine), channel_id=1, source_target_pairs={{0,8},{2,10},{4,12},{6,14},{8,0},{10,2},{12,4},{14,6},{1,9},{3,11}... | collective-permute-start | bytes 110600 | tf_op jit(solution)/shard_map/ppermute | solution.py:87
  32.1 4.9 %collective-permute-start.12 = (f32[9,8,128]{2,1,0:T(8,128)S(1)}, f32[9,8,128]{2,1,0:T(8,128)S(1)}, u32[]{:S(2)}, u32[]{:S(2)}) collective-permute-start(f32[9,8,128]{2,1,0:T(8,128)S(1)} %high.1.refs_0_), channel_id=1, source_target_pairs={{0,6},{2,4},{4,2},{6,0},{8,14},{10,12},{12,10},{14,8},{1,7},{3,5},... | collective-permute-start | bytes 110600 | tf_op jit(solution)/shard_map/ppermute | solution.py:87
  32.5 4.5 %collective-permute-start.11 = (f32[9,8,128]{2,1,0:T(8,128)S(1)}, f32[9,8,128]{2,1,0:T(8,128)S(1)}, u32[]{:S(2)}, u32[]{:S(2)}) collective-permute-start(f32[9,8,128]{2,1,0:T(8,128)S(1)} %high.1.refs_0_), channel_id=1, source_target_pairs={{0,4},{2,6},{4,0},{6,2},{8,12},{10,14},{12,8},{14,10},{1,5},{3,7},... | collective-permute-start | bytes 110600 | tf_op jit(solution)/shard_map/ppermute | solution.py:87
  34.1 4.0 %collective-permute-start.10 = (f32[9,8,128]{2,1,0:T(8,128)S(1)}, f32[9,8,128]{2,1,0:T(8,128)S(1)}, u32[]{:S(2)}, u32[]{:S(2)}) collective-permute-start(f32[9,8,128]{2,1,0:T(8,128)S(1)} %high.1.refs_0_), channel_id=1, source_target_pairs={{0,2},{2,0},{4,6},{6,4},{8,10},{10,8},{12,14},{14,12},{1,3},{3,1},... | collective-permute-start | bytes 110600 | tf_op jit(solution)/shard_map/ppermute | solution.py:87
  38.4 1.2 %collective-permute-start.13 = (f32[4,256]{1,0:T(4,128)S(1)}, f32[4,256]{1,0:T(4,128)S(1)}, u32[]{:S(2)}, u32[]{:S(2)}) collective-permute-start(f32[4,256]{1,0:T(4,128)S(1)} %get-tuple-element.25), channel_id=1, source_target_pairs={{0,1},{1,0},{2,3},{3,2},{4,5},{5,4},{6,7},{7,6},{8,9},{9,8},{10,11... | collective-permute-start | bytes 12296 | tf_op jit(solution)/shard_map/ppermute | solution.py:83

commit v4 on v3

--- a/solution.py
+++ b/solution.py
@@ -87,6 +87,15 @@
     return lax.ppermute(x, "center", [(i, i ^ bits) for i in range(lax.axis_size("center"))])
 
 
+def across(x, bits):
+    pairs = [
+        (2 * i + core, 2 * (i ^ bits) + 1 - core)
+        for i in range(lax.axis_size("center"))
+        for core in range(2)
+    ]
+    return lax.ppermute(x, ("center", "row"), pairs)
+
+
 def xor_lanes(tiles, stride):
     if stride >= LANES:
         return [tiles[i ^ (stride // LANES)] for i in range(len(tiles))]
@@ -107,16 +116,15 @@
     return tiles
 
 
-def pick_body(index, gamma, dataset, out, spread, index_s, gamma_s, data, sems):
+def pick_body(index, dataset, out, index_s, data, sems):
     copies = [
         pltpu.make_async_copy(a, b, sems.at[i])
-        for i, (a, b) in enumerate(((index, index_s), (gamma, gamma_s), (dataset, data)))
+        for i, (a, b) in enumerate(((index, index_s), (dataset, data)))
     ]
     for c in copies:
         c.start()
     for c in copies:
         c.wait()
-    spread[...] = jnp.full(spread.shape, gamma_s[0])
     batches, count = index.shape
     for b in range(batches):
         for j in range(count):
@@ -124,11 +132,13 @@
             out[at : at + 1] = data[pl.ds(index_s[b, j], 1), :]
 
 
-def center_body(centers, out):
-    c = centers[...]
-    count = c.shape[0]
+def prepare_body(centers, centers_out, sq_out, sem):
+    copy = pltpu.make_async_copy(centers, centers_out, sem)
+    copy.start()
+    copy.wait()
+    c = centers_out[...]
     sq = jnp.sum(c * c, axis=1, keepdims=True)
-    out[...] = jnp.broadcast_to(sq, (count, LANES)).T[: out.shape[0]]
+    sq_out[...] = jnp.broadcast_to(sq, (c.shape[0], LANES)).T[: sq_out.shape[0]]
 
 
 def kernel_body(gamma, rows, centers, center_sq, out):
@@ -138,46 +148,49 @@
     out[...] = jnp.exp(-gamma[:1] * (row_sq + center_sq[:1] - 2.0 * cross))
 
 
-def target_rows(targets, side):
+def by_batch(is_first, mine, theirs):
+    first, second = jnp.where(is_first, mine, theirs), jnp.where(is_first, theirs, mine)
+    half = mine.shape[0] // 2
+    low = lax.broadcasted_iota(jnp.int32, mine.shape, 0) < half
+    return (
+        jnp.where(low, first, pltpu.roll(second, half, 0)),
+        jnp.where(low, pltpu.roll(first, half, 0), second),
+    )
+
+
+def target_tiles(targets, side):
     cols = targets.shape[2] // 2
     both = jnp.concatenate([targets[b] for b in range(targets.shape[0])], 0)
     half = jnp.where(side == 0, both[:, :cols], both[:, cols:])
     return [half[:, i : i + LANES] for i in range(0, cols, LANES)]
 
 
-def target_body(targets, out):
-    for i, tile in enumerate(target_rows(targets, 1 - lax.axis_index("row"))):
-        out[i * tile.shape[0] : (i + 1) * tile.shape[0]] = tile
-
-
-def by_batch(own, other):
-    axis = own.ndim - 2
-    half = own.shape[axis] // 2
-    low = lax.broadcasted_iota(jnp.int32, own.shape, axis) < half
-    return (
-        jnp.where(low, own, pltpu.roll(other, half, axis)),
-        jnp.where(low, pltpu.roll(own, half, axis), other),
-    )
-
-
-def predict_body(plan, own, swapped, weights, wanted, targets, k0_out, k1_out, *outs):
+def predict_body(plan, *refs):
+    own, swapped, w_mine, w_theirs, t_mine, t_theirs, k0_out, k1_out, *outs = refs
     each, high = plan.each, plan.high
-    n, count = own.shape
-    tiled = lambda x: x.reshape(n // each, each, count)
-    k0, k1 = (k.reshape(n, count) for k in by_batch(tiled(own[...]), tiled(swapped[...])))
-    k0_out[...] = k0
-    k1_out[...] = k1
-    w = weights[...]
+    n = own.shape[0]
+    me = lax.axis_index("row")
     span = high * each
+    for q in range(QUAD):
+        for h in range(high):
+            at = q * span + h * each
+            crossed = (q > 0) ^ (h.bit_count() & 1)
+            tile = slice(at, at + each)
+            k0_out[tile], k1_out[tile] = by_batch(me == crossed, own[tile], swapped[tile])
+    k0, k1 = k0_out[...], k1_out[...]
     for b, k in enumerate((k0, k1)):
-        part = dot(k, w, ((1,), (0,)))
+        kept_part = dot(k[:span], w_theirs[...], ((1,), (0,)))
+        sent_part = dot(k[span:], w_mine[...], ((1,), (0,)))
+        part = jnp.concatenate([kept_part, sent_part], 0)
         for q, out in enumerate(outs):
             for c in range(plan.col_tiles):
                 tile = part[q * span : (q + 1) * span, c * LANES : (c + 1) * LANES]
                 at = (b * plan.col_tiles + c) * high
                 out[at : at + high] = tile.reshape(high, each, LANES)
-    for c, mine in enumerate(target_rows(targets, lax.axis_index("row"))):
-        for b, tile in enumerate(by_batch(mine, wanted[c * each : (c + 1) * each])):
+    for c, (mine, theirs) in enumerate(
+        zip(target_tiles(t_mine, 1 - me), target_tiles(t_theirs, 1 - me))
+    ):
+        for b, tile in enumerate(by_batch(me == 0, mine, theirs)):
             at = (b * plan.col_tiles + c) * high
             outs[0][at] = outs[0][at] - tile
     gram = dot(k1, jnp.concatenate([k0] * plan.pack, 0), ((1,), (1,)))
@@ -242,8 +255,10 @@
         grams.append(jnp.stack(rows, 1).reshape(span, packed.shape[2]))
     gram = jnp.concatenate(grams, 0)
     out1[...] = out1[...] - rate * dot(gram, res0, ((1,), (0,)))
-    mine_out[...] = out1[:half]
-    theirs_out[...] = out1[half : 2 * half]
+    first = lax.axis_index("row") == 0
+    a, b = out1[:half], out1[half : 2 * half]
+    mine_out[...] = jnp.where(first, a, b)
+    theirs_out[...] = jnp.where(first, b, a)
 
 
 def update_body(rate, k0, k1, res0, res1, weights, out):
@@ -276,47 +291,49 @@
     quad = range(1, QUAD)
     bits = [1 << i for i in range(high.bit_length() - 1)]
 
-    local, spread = call(
+    (local,) = call(
         pick_body,
-        [kept(each, features), kept(8, count)],
+        [kept(each, features)],
         "pick",
         (batch_index, pl.ANY),
-        (gamma, pl.ANY),
         (dataset, pl.ANY),
         scratch_shapes=[
             pltpu.SMEM(batch_index.shape, jnp.int32),
-            pltpu.SMEM(gamma.shape, jnp.float32),
             pltpu.VMEM(dataset.shape, jnp.float32),
-            pltpu.SemaphoreType.DMA((3,)),
+            pltpu.SemaphoreType.DMA((2,)),
         ],
     )
+    held, center_sq = call(
+        prepare_body,
+        [kept(count, features), kept(8, count)],
+        "prepare",
+        (centers, pl.ANY),
+        scratch_shapes=[pltpu.SemaphoreType.DMA],
+    )
+    spread = jnp.broadcast_to(gamma, (8, count))
     rows = local
     for bit in bits:
-        rows = jnp.concatenate([rows, partner(rows, QUAD * bit)], 0)
-    blocks = [rows] + [partner(rows, q) for q in quad]
-
-    (center_sq,) = call(center_body, [kept(8, count)], "center_sq", centers)
-    (half,) = call(target_body, [kept(each * plan.col_tiles, LANES)], "targets", targets)
-    wanted = swap_cores(half)
+        rows = jnp.concatenate([rows, across(rows, QUAD * bit)], 0)
+    rows, held, center_sq, spread = lax.optimization_barrier((rows, held, center_sq, spread))
     own = [
-        call(kernel_body, [kept(span, count)], "kernel", spread, x, centers, center_sq)[0]
-        for x in blocks
+        call(kernel_body, [kept(span, count)], "kernel", spread, x, held, center_sq)[0]
+        for x in [rows] + [across(rows, q) for q in quad]
     ]
     own = jnp.concatenate(own, 0)
-    swapped = swap_cores(own)
     packet = (plan.tiles, each, LANES)
     k0, k1, keep, *sent = call(
         functools.partial(predict_body, plan),
         [kept(n, count)] * 2 + [kept(*packet)] * QUAD,
         "predict",
         own,
-        swapped,
+        swap_cores(own),
         weights,
-        wanted,
+        swap_cores(weights),
         targets,
+        swap_cores(targets),
     )
     (total,) = call(
-        quad_body, [kept(*packet)], "quad", keep, *[partner(s, q) for q, s in zip(quad, sent)]
+        quad_body, [kept(*packet)], "quad", keep, *[across(s, q) for q, s in zip(quad, sent)]
     )
     for bit in bits:
         (total,) = call(
@@ -330,8 +347,8 @@
         functools.partial(second_body, plan, rate),
         [kept(n, cols)] * 2 + [kept(rows_here, cols)] * 2,
         "second",
-        total,
-        *[partner(total, q) for q in quad],
+        swap_cores(total),
+        *[across(total, q) for q in quad],
     )
     back = swap_cores(theirs)
     (new_weights,) = call(

time: 40.5 us -> 38.9 us (0.960)
  local copies, waits for them, and re-layouts: 2.59 us -> 0.34 us
  Pallas kernels: 5.73 us -> 6.9 us
  waiting for transfers between devices: 12.9 us -> 11.8 us
  starting transfers between devices: 17.7 us -> 18.2 us
    ppermute x11 -> x1, starting transfers between devices: 17.5 us -> 3.63 us  [partner(): lax.ppermute(x, 'center', [(i, i ^ bits) for i in range(lax.axis_size('ce...]
    ppermute x0 -> x10, starting transfers between devices: none -> 13.6 us  [across(): return lax.ppermute(x, ('center', 'row'), pairs)]
    ppermute x11 -> x1, waiting for transfers between devices: 11.6 us -> 2.5 us  [partner(): lax.ppermute(x, 'center', [(i, i ^ bits) for i in range(lax.axis_size('ce...]
    ppermute x0 -> x10, waiting for transfers between devices: none -> 8.39 us  [across(): return lax.ppermute(x, ('center', 'row'), pairs)]
    unnamed x9 -> x4, local copies, waits for them, and re-layouts: 2.59 us -> 0.33 us
    pallas_call x13 -> x12, Pallas kernels: 5.73 us -> 6.9 us  [call(): pl.pallas_call(body, out_shape=outs, in_specs=[pl.BlockSpec(memory_space=...]
    ppermute x3 -> x5, starting transfers between devices: 0.14 us -> 0.95 us  [swap_cores(): return lax.ppermute(x, 'row', [(0, 1), (1, 0)])]
    ppermute x3 -> x5, waiting for transfers between devices: 1.24 us -> 0.87 us  [swap_cores(): return lax.ppermute(x, 'row', [(0, 1), (1, 0)])]
  transfers between devices with their start and end apart: 14 -> 16, of which waited for: 11 -> 10; matrix products, arithmetic and copies ran while one was open for 0% -> 0% of each run, Pallas kernels for 7% -> 11%
where the time goes in v4:
time: 38.9 us; the launch traced here: 38.6 us
  starting transfers between devices  18.2 us (47%)
  waiting for transfers between devices  11.8 us (30%)
  Pallas kernels  6.9 us (18%)
  between operations  1.41 us (4%)
    ppermute x10, starting transfers between devices, across(): return lax.ppermute(x, ('center', 'row'), pairs)  13.6 us
    ppermute x10, waiting for transfers between devices, across(): return lax.ppermute(x, ('center', 'row'), pairs)  8.39 us
    pallas_call x12, Pallas kernels, call(): pl.pallas_call(body, out_shape=outs, in_specs=[pl.BlockSpec(memory_space=...  6.9 us
    ppermute x1, starting transfers between devices, partner(): lax.ppermute(x, 'center', [(i, i ^ bits) for i in range(lax.axis_size('ce...  3.63 us
    ppermute x1, waiting for transfers between devices, partner(): lax.ppermute(x, 'center', [(i, i ^ bits) for i in range(lax.axis_size('ce...  2.5 us
    ppermute x5, starting transfers between devices, swap_cores(): return lax.ppermute(x, 'row', [(0, 1), (1, 0)])  0.95 us
    ppermute x5, waiting for transfers between devices, swap_cores(): return lax.ppermute(x, 'row', [(0, 1), (1, 0)])  0.87 us
  transfers between devices with their start and end apart: 16, of which 10 were waited for; matrix products, arithmetic and copies ran while one was open for 0% of the time, Pallas kernels for 11%

profile of v4, /device:TPU:0, one launch (start us, length us, event | category | flops | bytes accessed | tf_op | source)
XLA Modules:
  0.0 38.6 jit_solution(17798421540091073607)
XLA Ops:
  0.6 0.9 %pick.1 = f32[8,1024]{1,0:T(8,128)S(1)} custom-call(s32[2,4]{1,0:T(2,128)} %index.1, f32[16,1024]{1,0:T(8,128)} %dataset.1), custom_call_target="tpu_custom_call" | custom-call | tf_op jit(solution)/shard_map/pick/pallas_call | solution.py:57
  1.5 3.6 %collective-permute-start = (f32[8,1024]{1,0:T(8,128)S(1)}, f32[8,1024]{1,0:T(8,128)S(1)}, u32[]{:S(2)}, u32[]{:S(2)}) collective-permute-start(f32[8,1024]{1,0:T(8,128)S(1)} %pick.1), channel_id=1, source_target_pairs={{0,9},{1,8},{2,11},{3,10},{4,13},{5,12},{6,15},{7,14},{8,1},{9,0},... | collective-permute-start | bytes 98312 | tf_op jit(solution)/shard_map/ppermute | solution.py:96
  5.1 1.2 %prepare.1 = (f32[128,1024]{1,0:T(8,128)S(1)}, f32[8,128]{1,0:T(8,128)S(1)}) custom-call(f32[128,1024]{1,0:T(8,128)} %centers.1), custom_call_target="tpu_custom_call" | custom-call | tf_op jit(solution)/shard_map/prepare/pallas_call | solution.py:57
  6.3 0.0 copy-start
  7.0 0.0 collective-permute-done
  7.0 2.8 %collective-permute-start.3 = (f32[16,1024]{1,0:T(8,128)S(1)}, f32[16,1024]{1,0:T(8,128)S(1)}, u32[]{:S(2)}, u32[]{:S(2)}) collective-permute-start(f32[16,1024]{1,0:T(8,128)S(1)} %pad_maximum_fusion.rows), channel_id=1, source_target_pairs={{0,7},{1,6},{2,5},{3,4},{4,3},{5,2},{6,1},{7,0},{8,15},{9,14},{10,... | collective-permute-start | bytes 196616 | tf_op jit(solution)/shard_map/ppermute | solution.py:96
  9.9 0.3 collective-permute-start.2
  10.1 0.4 %collective-permute-start.1 = (f32[16,1024]{1,0:T(8,128)S(1)}, f32[16,1024]{1,0:T(8,128)S(1)}, u32[]{:S(2)}, u32[]{:S(2)}) collective-permute-start(f32[16,1024]{1,0:T(8,128)S(1)} %pad_maximum_fusion.rows), channel_id=1, source_target_pairs={{0,3},{1,2},{2,1},{3,0},{4,7},{5,6},{6,5},{7,4},{8,11},{9,10},{10,... | collective-permute-start | bytes 196616 | tf_op jit(solution)/shard_map/ppermute | solution.py:96
  10.6 0.0 copy-done
  10.6 0.1 collective-permute-start.5
  10.6 0.5 %kernel.4 = f32[16,128]{1,0:T(8,128)S(1)} custom-call(f32[8,128]{1,0:T(8,128)S(1)} %broadcast_in_dim.2.gamma, f32[16,1024]{1,0:T(8,128)S(1)} %pad_maximum_fusion.rows, f32[128,1024]{1,0:T(8,128)S(1)} %get-tuple-element.22.centers, f32[8,128]{1,0:T(8,128)S(1)} %get-tuple-element.23.center_sq), custom_call_target="tpu_custom_call" | custom-call | tf_op jit(solution)/shard_map/kernel/pallas_call | solution.py:57
  11.1 1.2 %collective-permute-done.3.rows = f32[16,1024]{1,0:T(8,128)S(1)} collective-permute-done((f32[16,1024]{1,0:T(8,128)S(1)}, f32[16,1024]{1,0:T(8,128)S(1)}, u32[]{:S(2)}, u32[]{:S(2)}) %collective-permute-start.3) | collective-permute-done | bytes 65568 | tf_op jit(solution)/shard_map/ppermute | solution.py:96
  12.4 0.5 %kernel.7 = f32[16,128]{1,0:T(8,128)S(1)} custom-call(f32[8,128]{1,0:T(8,128)S(1)} %broadcast_in_dim.2.gamma, f32[16,1024]{1,0:T(8,128)S(1)} %collective-permute-done.3.rows, f32[128,1024]{1,0:T(8,128)S(1)} %get-tuple-element.22.centers, f32[8,128]{1,0:T(8,128)S(1)} %get-tuple-element.23.center_sq), custom_call_target="tpu_custom_call" | custom-call | tf_op jit(solution)/shard_map/kernel/pallas_call | solution.py:57
  12.9 1.0 %collective-permute-done.2.rows = f32[16,1024]{1,0:T(8,128)S(1)} collective-permute-done((f32[16,1024]{1,0:T(8,128)S(1)}, f32[16,1024]{1,0:T(8,128)S(1)}, u32[]{:S(2)}, u32[]{:S(2)}) %collective-permute-start.2) | collective-permute-done | bytes 65568 | tf_op jit(solution)/shard_map/ppermute | solution.py:96
  13.9 0.5 %kernel.6 = f32[16,128]{1,0:T(8,128)S(1)} custom-call(f32[8,128]{1,0:T(8,128)S(1)} %broadcast_in_dim.2.gamma, f32[16,1024]{1,0:T(8,128)S(1)} %collective-permute-done.2.rows, f32[128,1024]{1,0:T(8,128)S(1)} %get-tuple-element.22.centers, f32[8,128]{1,0:T(8,128)S(1)} %get-tuple-element.23.center_sq), custom_call_target="tpu_custom_call" | custom-call | tf_op jit(solution)/shard_map/kernel/pallas_call | solution.py:57
  14.4 0.0 collective-permute-done.1.rows
  14.4 0.5 %kernel.5 = f32[16,128]{1,0:T(8,128)S(1)} custom-call(f32[8,128]{1,0:T(8,128)S(1)} %broadcast_in_dim.2.gamma, f32[16,1024]{1,0:T(8,128)S(1)} %collective-permute-done.1.rows, f32[128,1024]{1,0:T(8,128)S(1)} %get-tuple-element.22.centers, f32[8,128]{1,0:T(8,128)S(1)} %get-tuple-element.23.center_sq), custom_call_target="tpu_custom_call" | custom-call | tf_op jit(solution)/shard_map/kernel/pallas_call | solution.py:57
  14.9 0.0 copy-start.1
  15.0 0.4 %collective-permute-start.4 = (f32[64,128]{1,0:T(8,128)S(1)}, f32[64,128]{1,0:T(8,128)S(1)}, u32[]{:S(2)}, u32[]{:S(2)}) collective-permute-start(f32[64,128]{1,0:T(8,128)S(1)} %pad_maximum_fusion.1.refs_0_), channel_id=1, source_target_pairs={{0,1},{1,0},{2,3},{3,2},{4,5},{5,4},{6,7},{7,6},{8,9},{9,8},{10,11... | collective-permute-start | bytes 98312 | tf_op jit(solution)/shard_map/ppermute | solution.py:83
  15.3 0.3 copy-done.1
  15.7 0.3 collective-permute-start.6
  16.0 0.9 %collective-permute-done.6.refs_5_ = f32[2,4,512]{2,1,0:T(4,128)S(1)} collective-permute-done((f32[2,4,512]{2,1,0:T(4,128)S(1)}, f32[2,4,512]{2,1,0:T(4,128)S(1)}, u32[]{:S(2)}, u32[]{:S(2)}) %collective-permute-start.6) | collective-permute-done | bytes 16416 | tf_op jit(solution)/shard_map/ppermute | solution.py:83
  16.8 0.0 collective-permute-done.4.refs_1_
  16.8 0.0 collective-permute-done.5.refs_3_
  16.8 0.6 %predict.1 = (f32[64,128]{1,0:T(8,128)S(1)}, f32[64,128]{1,0:T(8,128)S(1)}, f32[9,8,128]{2,1,0:T(8,128)S(1)}, f32[9,8,128]{2,1,0:T(8,128)S(1)}, f32[9,8,128]{2,1,0:T(8,128)S(1)}, /*index=5*/f32[9,8,128]{2,1,0:T(8,128)S(1)}) custom-call(f32[64,128]{1,0:T(8,128)S(1)} %pad_maximum_fusion.1.refs_0_, f32[64,128]{1,0:T(8,128)S(1)} %collective-permute-done.4.refs_1_, ...), custom_call_target="tpu_custom_call" | custom-call | tf_op jit(solution)/shard_map/predict/pallas_call | solution.py:57
  17.5 1.0 %collective-permute-start.7 = (f32[9,8,128]{2,1,0:T(8,128)S(1)}, f32[9,8,128]{2,1,0:T(8,128)S(1)}, u32[]{:S(2)}, u32[]{:S(2)}) collective-permute-start(f32[9,8,128]{2,1,0:T(8,128)S(1)} %get-tuple-element.27), channel_id=1, source_target_pairs={{0,3},{1,2},{2,1},{3,0},{4,7},{5,6},{6,5},{7,4},{8,11},{9,10},{10,... | collective-permute-start | bytes 110600 | tf_op jit(solution)/shard_map/ppermute | solution.py:96
  18.4 1.4 %collective-permute-start.8 = (f32[9,8,128]{2,1,0:T(8,128)S(1)}, f32[9,8,128]{2,1,0:T(8,128)S(1)}, u32[]{:S(2)}, u32[]{:S(2)}) collective-permute-start(f32[9,8,128]{2,1,0:T(8,128)S(1)} %get-tuple-element.28), channel_id=1, source_target_pairs={{0,5},{1,4},{2,7},{3,6},{4,1},{5,0},{6,3},{7,2},{8,13},{9,12},{10,... | collective-permute-start | bytes 110600 | tf_op jit(solution)/shard_map/ppermute | solution.py:96
  19.9 0.8 %collective-permute-start.9 = (f32[9,8,128]{2,1,0:T(8,128)S(1)}, f32[9,8,128]{2,1,0:T(8,128)S(1)}, u32[]{:S(2)}, u32[]{:S(2)}) collective-permute-start(f32[9,8,128]{2,1,0:T(8,128)S(1)} %get-tuple-element.29), channel_id=1, source_target_pairs={{0,7},{1,6},{2,5},{3,4},{4,3},{5,2},{6,1},{7,0},{8,15},{9,14},{10,... | collective-permute-start | bytes 110600 | tf_op jit(solution)/shard_map/ppermute | solution.py:96
  20.6 0.2 collective-permute-done.7.refs_0_
  20.9 1.0 %collective-permute-done.8.refs_1_ = f32[9,8,128]{2,1,0:T(8,128)S(1)} collective-permute-done((f32[9,8,128]{2,1,0:T(8,128)S(1)}, f32[9,8,128]{2,1,0:T(8,128)S(1)}, u32[]{:S(2)}, u32[]{:S(2)}) %collective-permute-start.8) | collective-permute-done | bytes 36896 | tf_op jit(solution)/shard_map/ppermute | solution.py:96
  21.8 2.4 %collective-permute-done.9.refs_2_ = f32[9,8,128]{2,1,0:T(8,128)S(1)} collective-permute-done((f32[9,8,128]{2,1,0:T(8,128)S(1)}, f32[9,8,128]{2,1,0:T(8,128)S(1)}, u32[]{:S(2)}, u32[]{:S(2)}) %collective-permute-start.9) | collective-permute-done | bytes 36896 | tf_op jit(solution)/shard_map/ppermute | solution.py:96
  24.2 3.6 %collective-permute-start.10 = (f32[9,8,128]{2,1,0:T(8,128)S(1)}, f32[9,8,128]{2,1,0:T(8,128)S(1)}, u32[]{:S(2)}, u32[]{:S(2)}) collective-permute-start(f32[9,8,128]{2,1,0:T(8,128)S(1)} %quad.1.mine), channel_id=1, source_target_pairs={{0,8},{2,10},{4,12},{6,14},{8,0},{10,2},{12,4},{14,6},{1,9},{3,11}... | collective-permute-start | bytes 110600 | tf_op jit(solution)/shard_map/ppermute | solution.py:87
  27.8 2.5 %collective-permute-done.10.other = f32[9,8,128]{2,1,0:T(8,128)S(1)} collective-permute-done((f32[9,8,128]{2,1,0:T(8,128)S(1)}, f32[9,8,128]{2,1,0:T(8,128)S(1)}, u32[]{:S(2)}, u32[]{:S(2)}) %collective-permute-start.10) | collective-permute-done | bytes 36896 | tf_op jit(solution)/shard_map/ppermute | solution.py:87
  30.3 0.1 high.1
  30.5 0.0 collective-permute-start.11
  30.5 1.2 %collective-permute-start.12 = (f32[9,8,128]{2,1,0:T(8,128)S(1)}, f32[9,8,128]{2,1,0:T(8,128)S(1)}, u32[]{:S(2)}, u32[]{:S(2)}) collective-permute-start(f32[9,8,128]{2,1,0:T(8,128)S(1)} %high.1), channel_id=1, source_target_pairs={{0,3},{1,2},{2,1},{3,0},{4,7},{5,6},{6,5},{7,4},{8,11},{9,10},{10,... | collective-permute-start | bytes 110600 | tf_op jit(solution)/shard_map/ppermute | solution.py:96
  31.7 0.0 collective-permute-start.13
  31.7 2.1 %collective-permute-start.14 = (f32[9,8,128]{2,1,0:T(8,128)S(1)}, f32[9,8,128]{2,1,0:T(8,128)S(1)}, u32[]{:S(2)}, u32[]{:S(2)}) collective-permute-start(f32[9,8,128]{2,1,0:T(8,128)S(1)} %high.1), channel_id=1, source_target_pairs={{0,7},{1,6},{2,5},{3,4},{4,3},{5,2},{6,1},{7,0},{8,15},{9,14},{10,... | collective-permute-start | bytes 110600 | tf_op jit(solution)/shard_map/ppermute | solution.py:96
  33.8 0.0 collective-permute-done.11.refs_0_
  33.8 0.1 collective-permute-done.12.refs_1_
  33.9 1.3 %collective-permute-done.13.refs_2_ = f32[9,8,128]{2,1,0:T(8,128)S(1)} collective-permute-done((f32[9,8,128]{2,1,0:T(8,128)S(1)}, f32[9,8,128]{2,1,0:T(8,128)S(1)}, u32[]{:S(2)}, u32[]{:S(2)}) %collective-permute-start.13) | collective-permute-done | bytes 36896 | tf_op jit(solution)/shard_map/ppermute | solution.py:96
  35.2 1.2 %collective-permute-done.14.refs_3_ = f32[9,8,128]{2,1,0:T(8,128)S(1)} collective-permute-done((f32[9,8,128]{2,1,0:T(8,128)S(1)}, f32[9,8,128]{2,1,0:T(8,128)S(1)}, u32[]{:S(2)}, u32[]{:S(2)}) %collective-permute-start.14) | collective-permute-done | bytes 36896 | tf_op jit(solution)/shard_map/ppermute | solution.py:96
  36.4 0.3 second.1
  36.7 0.2 collective-permute-start.15
  36.9 1.1 %update.1 = f32[128,256]{1,0:T(8,128)} custom-call(f32[64,128]{1,0:T(8,128)S(1)} %get-tuple-element.24.k0, f32[64,128]{1,0:T(8,128)S(1)} %get-tuple-element.25.k1, f32[64,256]{1,0:T(8,128)S(1)} %get-tuple-element.30.res0, f32[64,256]{1,0:T(8,128)S(1)} %get-tuple-element.31.res1, f32[128,256]{1,0:T(8,128)S(1)} %copy-done), custom_call_target="tpu_custom_call" | custom-call | tf_op jit(solution)/shard_map/update/pallas_call | solution.py:57
  38.0 0.0 collective-permute-done.15.back
  38.0 0.6 %finish.1 = f32[4,512]{1,0:T(4,128)} custom-call(f32[4,256]{1,0:T(4,128)S(1)} %get-tuple-element.32.mine, f32[4,256]{1,0:T(4,128)S(1)} %collective-permute-done.15.back), custom_call_target="tpu_custom_call" | custom-call | tf_op jit(solution)/shard_map/finish/pallas_call | solution.py:57
  (4 shorter events, 0.0 us)
Async XLA Ops:
  1.5 5.5 %collective-permute-start = (f32[8,1024]{1,0:T(8,128)S(1)}, f32[8,1024]{1,0:T(8,128)S(1)}, u32[]{:S(2)}, u32[]{:S(2)}) collective-permute-start(f32[8,1024]{1,0:T(8,128)S(1)} %pick.1), channel_id=1, source_target_pairs={{0,9},{1,8},{2,11},{3,10},{4,13},{5,12},{6,15},{7,14},{8,1},{9,0},... | collective-permute-start | bytes 98312 | tf_op jit(solution)/shard_map/ppermute | solution.py:96
  6.3 4.3 %copy-start = (f32[128,256]{1,0:T(8,128)S(1)}, f32[128,256]{1,0:T(8,128)}, u32[]{:S(2)}) copy-start(f32[128,256]{1,0:T(8,128)} %weights.1) | copy-start | bytes 393220
  7.0 5.3 %collective-permute-start.3 = (f32[16,1024]{1,0:T(8,128)S(1)}, f32[16,1024]{1,0:T(8,128)S(1)}, u32[]{:S(2)}, u32[]{:S(2)}) collective-permute-start(f32[16,1024]{1,0:T(8,128)S(1)} %pad_maximum_fusion.rows), channel_id=1, source_target_pairs={{0,7},{1,6},{2,5},{3,4},{4,3},{5,2},{6,1},{7,0},{8,15},{9,14},{10,... | collective-permute-start | bytes 196616 | tf_op jit(solution)/shard_map/ppermute | solution.py:96
  9.9 4.0 %collective-permute-start.2 = (f32[16,1024]{1,0:T(8,128)S(1)}, f32[16,1024]{1,0:T(8,128)S(1)}, u32[]{:S(2)}, u32[]{:S(2)}) collective-permute-start(f32[16,1024]{1,0:T(8,128)S(1)} %pad_maximum_fusion.rows), channel_id=1, source_target_pairs={{0,5},{1,4},{2,7},{3,6},{4,1},{5,0},{6,3},{7,2},{8,13},{9,12},{10,... | collective-permute-start | bytes 196616 | tf_op jit(solution)/shard_map/ppermute | solution.py:96
  10.1 4.2 %collective-permute-start.1 = (f32[16,1024]{1,0:T(8,128)S(1)}, f32[16,1024]{1,0:T(8,128)S(1)}, u32[]{:S(2)}, u32[]{:S(2)}) collective-permute-start(f32[16,1024]{1,0:T(8,128)S(1)} %pad_maximum_fusion.rows), channel_id=1, source_target_pairs={{0,3},{1,2},{2,1},{3,0},{4,7},{5,6},{6,5},{7,4},{8,11},{9,10},{10,... | collective-permute-start | bytes 196616 | tf_op jit(solution)/shard_map/ppermute | solution.py:96
  10.6 6.3 %collective-permute-start.5 = (f32[128,256]{1,0:T(8,128)S(1)}, f32[128,256]{1,0:T(8,128)S(1)}, u32[]{:S(2)}, u32[]{:S(2)}) collective-permute-start(f32[128,256]{1,0:T(8,128)S(1)} %copy-done), channel_id=1, source_target_pairs={{0,1},{1,0},{2,3},{3,2},{4,5},{5,4},{6,7},{7,6},{8,9},{9,8},{10,11... | collective-permute-start | bytes 393224 | tf_op jit(solution)/shard_map/ppermute | solution.py:83
  14.9 0.7 %copy-start.1 = (f32[2,4,512]{2,1,0:T(4,128)S(1)}, f32[2,4,512]{2,1,0:T(4,128)}, u32[]{:S(2)}) copy-start(f32[2,4,512]{2,1,0:T(4,128)} %refs_4_.1) | copy-start | bytes 49156
  15.0 1.9 %collective-permute-start.4 = (f32[64,128]{1,0:T(8,128)S(1)}, f32[64,128]{1,0:T(8,128)S(1)}, u32[]{:S(2)}, u32[]{:S(2)}) collective-permute-start(f32[64,128]{1,0:T(8,128)S(1)} %pad_maximum_fusion.1.refs_0_), channel_id=1, source_target_pairs={{0,1},{1,0},{2,3},{3,2},{4,5},{5,4},{6,7},{7,6},{8,9},{9,8},{10,11... | collective-permute-start | bytes 98312 | tf_op jit(solution)/shard_map/ppermute | solution.py:83
  15.7 1.2 %collective-permute-start.6 = (f32[2,4,512]{2,1,0:T(4,128)S(1)}, f32[2,4,512]{2,1,0:T(4,128)S(1)}, u32[]{:S(2)}, u32[]{:S(2)}) collective-permute-start(f32[2,4,512]{2,1,0:T(4,128)S(1)} %copy-done.1), channel_id=1, source_target_pairs={{0,1},{1,0},{2,3},{3,2},{4,5},{5,4},{6,7},{7,6},{8,9},{9,8},{10,11... | collective-permute-start | bytes 49160 | tf_op jit(solution)/shard_map/ppermute | solution.py:83
  17.5 3.4 %collective-permute-start.7 = (f32[9,8,128]{2,1,0:T(8,128)S(1)}, f32[9,8,128]{2,1,0:T(8,128)S(1)}, u32[]{:S(2)}, u32[]{:S(2)}) collective-permute-start(f32[9,8,128]{2,1,0:T(8,128)S(1)} %get-tuple-element.27), channel_id=1, source_target_pairs={{0,3},{1,2},{2,1},{3,0},{4,7},{5,6},{6,5},{7,4},{8,11},{9,10},{10,... | collective-permute-start | bytes 110600 | tf_op jit(solution)/shard_map/ppermute | solution.py:96
  18.4 3.4 %collective-permute-start.8 = (f32[9,8,128]{2,1,0:T(8,128)S(1)}, f32[9,8,128]{2,1,0:T(8,128)S(1)}, u32[]{:S(2)}, u32[]{:S(2)}) collective-permute-start(f32[9,8,128]{2,1,0:T(8,128)S(1)} %get-tuple-element.28), channel_id=1, source_target_pairs={{0,5},{1,4},{2,7},{3,6},{4,1},{5,0},{6,3},{7,2},{8,13},{9,12},{10,... | collective-permute-start | bytes 110600 | tf_op jit(solution)/shard_map/ppermute | solution.py:96
  19.9 4.3 %collective-permute-start.9 = (f32[9,8,128]{2,1,0:T(8,128)S(1)}, f32[9,8,128]{2,1,0:T(8,128)S(1)}, u32[]{:S(2)}, u32[]{:S(2)}) collective-permute-start(f32[9,8,128]{2,1,0:T(8,128)S(1)} %get-tuple-element.29), channel_id=1, source_target_pairs={{0,7},{1,6},{2,5},{3,4},{4,3},{5,2},{6,1},{7,0},{8,15},{9,14},{10,... | collective-permute-start | bytes 110600 | tf_op jit(solution)/shard_map/ppermute | solution.py:96
  24.2 6.1 %collective-permute-start.10 = (f32[9,8,128]{2,1,0:T(8,128)S(1)}, f32[9,8,128]{2,1,0:T(8,128)S(1)}, u32[]{:S(2)}, u32[]{:S(2)}) collective-permute-start(f32[9,8,128]{2,1,0:T(8,128)S(1)} %quad.1.mine), channel_id=1, source_target_pairs={{0,8},{2,10},{4,12},{6,14},{8,0},{10,2},{12,4},{14,6},{1,9},{3,11}... | collective-permute-start | bytes 110600 | tf_op jit(solution)/shard_map/ppermute | solution.py:87
  30.5 3.3 %collective-permute-start.11 = (f32[9,8,128]{2,1,0:T(8,128)S(1)}, f32[9,8,128]{2,1,0:T(8,128)S(1)}, u32[]{:S(2)}, u32[]{:S(2)}) collective-permute-start(f32[9,8,128]{2,1,0:T(8,128)S(1)} %high.1), channel_id=1, source_target_pairs={{0,1},{1,0},{2,3},{3,2},{4,5},{5,4},{6,7},{7,6},{8,9},{9,8},{10,11... | collective-permute-start | bytes 110600 | tf_op jit(solution)/shard_map/ppermute | solution.py:83
  30.5 3.4 %collective-permute-start.12 = (f32[9,8,128]{2,1,0:T(8,128)S(1)}, f32[9,8,128]{2,1,0:T(8,128)S(1)}, u32[]{:S(2)}, u32[]{:S(2)}) collective-permute-start(f32[9,8,128]{2,1,0:T(8,128)S(1)} %high.1), channel_id=1, source_target_pairs={{0,3},{1,2},{2,1},{3,0},{4,7},{5,6},{6,5},{7,4},{8,11},{9,10},{10,... | collective-permute-start | bytes 110600 | tf_op jit(solution)/shard_map/ppermute | solution.py:96
  31.7 3.5 %collective-permute-start.13 = (f32[9,8,128]{2,1,0:T(8,128)S(1)}, f32[9,8,128]{2,1,0:T(8,128)S(1)}, u32[]{:S(2)}, u32[]{:S(2)}) collective-permute-start(f32[9,8,128]{2,1,0:T(8,128)S(1)} %high.1), channel_id=1, source_target_pairs={{0,5},{1,4},{2,7},{3,6},{4,1},{5,0},{6,3},{7,2},{8,13},{9,12},{10,... | collective-permute-start | bytes 110600 | tf_op jit(solution)/shard_map/ppermute | solution.py:96
  31.7 4.8 %collective-permute-start.14 = (f32[9,8,128]{2,1,0:T(8,128)S(1)}, f32[9,8,128]{2,1,0:T(8,128)S(1)}, u32[]{:S(2)}, u32[]{:S(2)}) collective-permute-start(f32[9,8,128]{2,1,0:T(8,128)S(1)} %high.1), channel_id=1, source_target_pairs={{0,7},{1,6},{2,5},{3,4},{4,3},{5,2},{6,1},{7,0},{8,15},{9,14},{10,... | collective-permute-start | bytes 110600 | tf_op jit(solution)/shard_map/ppermute | solution.py:96
  36.7 1.3 %collective-permute-start.15 = (f32[4,256]{1,0:T(4,128)S(1)}, f32[4,256]{1,0:T(4,128)S(1)}, u32[]{:S(2)}, u32[]{:S(2)}) collective-permute-start(f32[4,256]{1,0:T(4,128)S(1)} %get-tuple-element.33), channel_id=1, source_target_pairs={{0,1},{1,0},{2,3},{3,2},{4,5},{5,4},{6,7},{7,6},{8,9},{9,8},{10,11... | collective-permute-start | bytes 12296 | tf_op jit(solution)/shard_map/ppermute | solution.py:83

commit v5 on v4

--- a/solution.py
+++ b/solution.py
@@ -49,7 +49,7 @@
 
 
 def small(x):
-    return math.prod(x.shape) * 4 <= KEPT_BYTES
+    return math.prod(x.shape) * jnp.dtype(x.dtype).itemsize <= KEPT_BYTES
 
 
 def call(body, outs, name, *args, **kwargs):
@@ -132,20 +132,44 @@
             out[at : at + 1] = data[pl.ds(index_s[b, j], 1), :]
 
 
-def prepare_body(centers, centers_out, sq_out, sem):
-    copy = pltpu.make_async_copy(centers, centers_out, sem)
-    copy.start()
-    copy.wait()
-    c = centers_out[...]
+def parts(x):
+    out = []
+    for _ in range(3):
+        out.append(x.astype(jnp.bfloat16))
+        x = x - out[-1].astype(jnp.float32)
+    return out
+
+
+def prepare_body(centers, targets, split_out, row_out, targets_out, held, sems):
+    copies = [
+        pltpu.make_async_copy(a, b, sems.at[i])
+        for i, (a, b) in enumerate(((centers, held), (targets, targets_out)))
+    ]
+    for c in copies:
+        c.start()
+    for c in copies:
+        c.wait()
+    c = held[...]
+    for i, part in enumerate(parts(c)):
+        split_out[i] = part
     sq = jnp.sum(c * c, axis=1, keepdims=True)
-    sq_out[...] = jnp.broadcast_to(sq, (c.shape[0], LANES)).T[: sq_out.shape[0]]
-
-
-def kernel_body(gamma, rows, centers, center_sq, out):
+    row_out[...] = jnp.broadcast_to(sq, (c.shape[0], LANES)).T[: row_out.shape[0]]
+
+
+def kernel_body(gamma, rows, split, row, out):
     x = rows[...]
+    n = x.shape[0]
     row_sq = jnp.sum(x * x, axis=1, keepdims=True)
-    cross = dot(x, centers[...], ((1,), (1,)))
-    out[...] = jnp.exp(-gamma[:1] * (row_sq + center_sq[:1] - 2.0 * cross))
+    xs = parts(x)
+    cross = 0.0
+    for i in (2, 1, 0):
+        left = jnp.concatenate(xs[: 3 - i], 0)
+        part = lax.dot_general(
+            left, split[i], (((1,), (1,)), ((), ())), preferred_element_type=jnp.float32
+        )
+        for j in reversed(range(3 - i)):
+            cross = cross + part[j * n : (j + 1) * n]
+    out[...] = jnp.exp(-gamma[:1] * (row_sq + row[:1] - 2.0 * cross))
 
 
 def by_batch(is_first, mine, theirs):
@@ -303,22 +327,33 @@
             pltpu.SemaphoreType.DMA((2,)),
         ],
     )
-    held, center_sq = call(
+    split, row, targets = call(
         prepare_body,
-        [kept(count, features), kept(8, count)],
+        [
+            pltpu.VMEM((3, count, features), jnp.bfloat16),
+            kept(8, count),
+            kept(*targets.shape),
+        ],
         "prepare",
         (centers, pl.ANY),
-        scratch_shapes=[pltpu.SemaphoreType.DMA],
+        (targets, pl.ANY),
+        scratch_shapes=[
+            pltpu.VMEM(centers.shape, jnp.float32),
+            pltpu.SemaphoreType.DMA((2,)),
+        ],
     )
     spread = jnp.broadcast_to(gamma, (8, count))
     rows = local
     for bit in bits:
         rows = jnp.concatenate([rows, across(rows, QUAD * bit)], 0)
-    rows, held, center_sq, spread = lax.optimization_barrier((rows, held, center_sq, spread))
+    rows, split, row, targets = lax.optimization_barrier((rows, split, row, targets))
     own = [
-        call(kernel_body, [kept(span, count)], "kernel", spread, x, held, center_sq)[0]
+        call(kernel_body, [kept(span, count)], "kernel", spread, x, split, row)[0]
         for x in [rows] + [across(rows, q) for q in quad]
     ]
+    own[0], weights_other, targets_other = lax.optimization_barrier(
+        (own[0], swap_cores(weights), swap_cores(targets))
+    )
     own = jnp.concatenate(own, 0)
     packet = (plan.tiles, each, LANES)
     k0, k1, keep, *sent = call(
@@ -328,12 +363,16 @@
         own,
         swap_cores(own),
         weights,
-        swap_cores(weights),
+        weights_other,
         targets,
-        swap_cores(targets),
+        targets_other,
     )
     (total,) = call(
-        quad_body, [kept(*packet)], "quad", keep, *[across(s, q) for q, s in zip(quad, sent)]
+        quad_body,
+        [kept(*packet)],
+        "quad",
+        keep,
+        *[across(sent[q - 1], q) for q in reversed(quad)],
     )
     for bit in bits:
         (total,) = call(

time: 38.9 us -> 37.1 us (0.954)
  waiting for transfers between devices: 11.8 us -> 11.1 us
  Pallas kernels: 6.9 us -> 6.2 us
    ppermute x5, starting transfers between devices: 0.95 us -> 1.98 us  [swap_cores(): return lax.ppermute(x, 'row', [(0, 1), (1, 0)])]
    pallas_call x12, Pallas kernels: 6.9 us -> 6.2 us  [call(): pl.pallas_call(body, out_shape=outs, in_specs=[pl.BlockSpec(memory_space=...]
    ppermute x1, starting transfers between devices: 3.63 us -> 3.05 us  [partner(): lax.ppermute(x, 'center', [(i, i ^ bits) for i in range(lax.axis_size('ce...]
    ppermute x1, waiting for transfers between devices: 2.5 us -> 1.99 us  [partner(): lax.ppermute(x, 'center', [(i, i ^ bits) for i in range(lax.axis_size('ce...]
  transfers between devices with their start and end apart: 16 -> 16, of which waited for: 10 -> 11; matrix products, arithmetic and copies ran while one was open for 0% -> 0% of each run, Pallas kernels for 11% -> 10%
where the time goes in v5:
time: 37.1 us; the launch traced here: 36.9 us
  starting transfers between devices  18.2 us (49%)
  waiting for transfers between devices  11.1 us (30%)
  Pallas kernels  6.2 us (17%)
  between operations  1.37 us (4%)
    ppermute x10, starting transfers between devices, across(): return lax.ppermute(x, ('center', 'row'), pairs)  13.2 us
    ppermute x10, waiting for transfers between devices, across(): return lax.ppermute(x, ('center', 'row'), pairs)  8.21 us
    pallas_call x12, Pallas kernels, call(): pl.pallas_call(body, out_shape=outs, in_specs=[pl.BlockSpec(memory_space=...  6.2 us
    ppermute x1, starting transfers between devices, partner(): lax.ppermute(x, 'center', [(i, i ^ bits) for i in range(lax.axis_size('ce...  3.05 us
    ppermute x1, waiting for transfers between devices, partner(): lax.ppermute(x, 'center', [(i, i ^ bits) for i in range(lax.axis_size('ce...  1.99 us
    ppermute x5, starting transfers between devices, swap_cores(): return lax.ppermute(x, 'row', [(0, 1), (1, 0)])  1.98 us
    ppermute x5, waiting for transfers between devices, swap_cores(): return lax.ppermute(x, 'row', [(0, 1), (1, 0)])  0.9 us
  transfers between devices with their start and end apart: 16, of which 11 were waited for; matrix products, arithmetic and copies ran while one was open for 0% of the time, Pallas kernels for 10%

profile of v5, /device:TPU:0, one launch (start us, length us, event | category | flops | bytes accessed | tf_op | source)
XLA Modules:
  0.0 36.9 jit_solution(12902659283624315389)
XLA Ops:
  0.6 0.9 %pick.1 = f32[8,1024]{1,0:T(8,128)S(1)} custom-call(s32[2,4]{1,0:T(2,128)} %index.1, f32[16,1024]{1,0:T(8,128)} %dataset.1), custom_call_target="tpu_custom_call" | custom-call | tf_op jit(solution)/shard_map/pick/pallas_call | solution.py:57
  1.5 3.6 %collective-permute-start = (f32[8,1024]{1,0:T(8,128)S(1)}, f32[8,1024]{1,0:T(8,128)S(1)}, u32[]{:S(2)}, u32[]{:S(2)}) collective-permute-start(f32[8,1024]{1,0:T(8,128)S(1)} %pick.1), channel_id=1, source_target_pairs={{0,9},{1,8},{2,11},{3,10},{4,13},{5,12},{6,15},{7,14},{8,1},{9,0},... | collective-permute-start | bytes 98312 | tf_op jit(solution)/shard_map/ppermute | solution.py:96
  5.1 0.7 %collective-permute-start.1 = (f32[128,256]{1,0:T(8,128)}, f32[128,256]{1,0:T(8,128)S(1)}, u32[]{:S(2)}, u32[]{:S(2)}) collective-permute-start(f32[128,256]{1,0:T(8,128)} %weights.1), channel_id=1, source_target_pairs={{0,1},{1,0},{2,3},{3,2},{4,5},{5,4},{6,7},{7,6},{8,9},{9,8},{10,11... | collective-permute-start | bytes 393224 | tf_op jit(solution)/shard_map/ppermute | solution.py:83
  5.8 1.3 %prepare.1 = (bf16[3,128,1024]{2,1,0:T(8,128)(2,1)S(1)}, f32[8,128]{1,0:T(8,128)S(1)}, f32[2,4,512]{2,1,0:T(4,128)S(1)}) custom-call(f32[128,1024]{1,0:T(8,128)} %centers.1, f32[2,4,512]{2,1,0:T(4,128)} %targets.1), custom_call_target="tpu_custom_call" | custom-call | tf_op jit(solution)/shard_map/prepare/pallas_call | solution.py:57
  7.1 0.0 collective-permute-done
  7.1 2.5 %collective-permute-start.5 = (f32[16,1024]{1,0:T(8,128)S(1)}, f32[16,1024]{1,0:T(8,128)S(1)}, u32[]{:S(2)}, u32[]{:S(2)}) collective-permute-start(f32[16,1024]{1,0:T(8,128)S(1)} %pad_maximum_fusion.rows), channel_id=1, source_target_pairs={{0,7},{1,6},{2,5},{3,4},{4,3},{5,2},{6,1},{7,0},{8,15},{9,14},{10,... | collective-permute-start | bytes 196616 | tf_op jit(solution)/shard_map/ppermute | solution.py:96
  9.6 0.4 %collective-permute-start.4 = (f32[16,1024]{1,0:T(8,128)S(1)}, f32[16,1024]{1,0:T(8,128)S(1)}, u32[]{:S(2)}, u32[]{:S(2)}) collective-permute-start(f32[16,1024]{1,0:T(8,128)S(1)} %pad_maximum_fusion.rows), channel_id=1, source_target_pairs={{0,5},{1,4},{2,7},{3,6},{4,1},{5,0},{6,3},{7,2},{8,13},{9,12},{10,... | collective-permute-start | bytes 196616 | tf_op jit(solution)/shard_map/ppermute | solution.py:96
  10.1 0.2 collective-permute-start.3
  10.3 0.2 collective-permute-start.2
  11.2 0.3 kernel.4
  11.5 0.6 %collective-permute-done.5.rows = f32[16,1024]{1,0:T(8,128)S(1)} collective-permute-done((f32[16,1024]{1,0:T(8,128)S(1)}, f32[16,1024]{1,0:T(8,128)S(1)}, u32[]{:S(2)}, u32[]{:S(2)}) %collective-permute-start.5) | collective-permute-done | bytes 65568 | tf_op jit(solution)/shard_map/ppermute | solution.py:96
  12.1 0.3 kernel.7
  12.4 1.2 %collective-permute-done.4.rows = f32[16,1024]{1,0:T(8,128)S(1)} collective-permute-done((f32[16,1024]{1,0:T(8,128)S(1)}, f32[16,1024]{1,0:T(8,128)S(1)}, u32[]{:S(2)}, u32[]{:S(2)}) %collective-permute-start.4) | collective-permute-done | bytes 65568 | tf_op jit(solution)/shard_map/ppermute | solution.py:96
  13.7 0.3 kernel.6
  14.0 0.2 collective-permute-done.3.rows
  14.2 0.0 copy-start
  14.2 0.3 kernel.5
  14.5 0.0 collective-permute-done.2.refs_5_
  14.5 0.0 collective-permute-done.1.refs_3_
  14.6 0.5 %collective-permute-start.6 = (f32[64,128]{1,0:T(8,128)S(1)}, f32[64,128]{1,0:T(8,128)S(1)}, u32[]{:S(2)}, u32[]{:S(2)}) collective-permute-start(f32[64,128]{1,0:T(8,128)S(1)} %pad_maximum_fusion.1.refs_0_), channel_id=1, source_target_pairs={{0,1},{1,0},{2,3},{3,2},{4,5},{5,4},{6,7},{7,6},{8,9},{9,8},{10,11... | collective-permute-start | bytes 98312 | tf_op jit(solution)/shard_map/ppermute | solution.py:83
  15.1 0.9 %collective-permute-done.6.refs_1_ = f32[64,128]{1,0:T(8,128)S(1)} collective-permute-done((f32[64,128]{1,0:T(8,128)S(1)}, f32[64,128]{1,0:T(8,128)S(1)}, u32[]{:S(2)}, u32[]{:S(2)}) %collective-permute-start.6) | collective-permute-done | bytes 32800 | tf_op jit(solution)/shard_map/ppermute | solution.py:83
  15.9 0.0 copy-done
  15.9 0.6 %predict.1 = (f32[64,128]{1,0:T(8,128)S(1)}, f32[64,128]{1,0:T(8,128)S(1)}, f32[9,8,128]{2,1,0:T(8,128)S(1)}, f32[9,8,128]{2,1,0:T(8,128)S(1)}, f32[9,8,128]{2,1,0:T(8,128)S(1)}, /*index=5*/f32[9,8,128]{2,1,0:T(8,128)S(1)}) custom-call(f32[64,128]{1,0:T(8,128)S(1)} %pad_maximum_fusion.1.refs_0_, f32[64,128]{1,0:T(8,128)S(1)} %collective-permute-done.6.refs_1_, ...), custom_call_target="tpu_custom_call" | custom-call | tf_op jit(solution)/shard_map/predict/pallas_call | solution.py:57
  16.5 2.1 %collective-permute-start.7 = (f32[9,8,128]{2,1,0:T(8,128)S(1)}, f32[9,8,128]{2,1,0:T(8,128)S(1)}, u32[]{:S(2)}, u32[]{:S(2)}) collective-permute-start(f32[9,8,128]{2,1,0:T(8,128)S(1)} %get-tuple-element.35), channel_id=1, source_target_pairs={{0,7},{1,6},{2,5},{3,4},{4,3},{5,2},{6,1},{7,0},{8,15},{9,14},{10,... | collective-permute-start | bytes 110600 | tf_op jit(solution)/shard_map/ppermute | solution.py:96
  18.6 0.4 %collective-permute-start.8 = (f32[9,8,128]{2,1,0:T(8,128)S(1)}, f32[9,8,128]{2,1,0:T(8,128)S(1)}, u32[]{:S(2)}, u32[]{:S(2)}) collective-permute-start(f32[9,8,128]{2,1,0:T(8,128)S(1)} %get-tuple-element.36), channel_id=1, source_target_pairs={{0,5},{1,4},{2,7},{3,6},{4,1},{5,0},{6,3},{7,2},{8,13},{9,12},{10,... | collective-permute-start | bytes 110600 | tf_op jit(solution)/shard_map/ppermute | solution.py:96
  19.0 0.7 %collective-permute-start.9 = (f32[9,8,128]{2,1,0:T(8,128)S(1)}, f32[9,8,128]{2,1,0:T(8,128)S(1)}, u32[]{:S(2)}, u32[]{:S(2)}) collective-permute-start(f32[9,8,128]{2,1,0:T(8,128)S(1)} %get-tuple-element.37), channel_id=1, source_target_pairs={{0,3},{1,2},{2,1},{3,0},{4,7},{5,6},{6,5},{7,4},{8,11},{9,10},{10,... | collective-permute-start | bytes 110600 | tf_op jit(solution)/shard_map/ppermute | solution.py:96
  19.7 1.1 %collective-permute-done.7.refs_0_ = f32[9,8,128]{2,1,0:T(8,128)S(1)} collective-permute-done((f32[9,8,128]{2,1,0:T(8,128)S(1)}, f32[9,8,128]{2,1,0:T(8,128)S(1)}, u32[]{:S(2)}, u32[]{:S(2)}) %collective-permute-start.7) | collective-permute-done | bytes 36896 | tf_op jit(solution)/shard_map/ppermute | solution.py:96
  20.8 1.2 %collective-permute-done.8.refs_1_ = f32[9,8,128]{2,1,0:T(8,128)S(1)} collective-permute-done((f32[9,8,128]{2,1,0:T(8,128)S(1)}, f32[9,8,128]{2,1,0:T(8,128)S(1)}, u32[]{:S(2)}, u32[]{:S(2)}) %collective-permute-start.8) | collective-permute-done | bytes 36896 | tf_op jit(solution)/shard_map/ppermute | solution.py:96
  22.0 0.4 %collective-permute-done.9.refs_2_ = f32[9,8,128]{2,1,0:T(8,128)S(1)} collective-permute-done((f32[9,8,128]{2,1,0:T(8,128)S(1)}, f32[9,8,128]{2,1,0:T(8,128)S(1)}, u32[]{:S(2)}, u32[]{:S(2)}) %collective-permute-start.9) | collective-permute-done | bytes 36896 | tf_op jit(solution)/shard_map/ppermute | solution.py:96
  22.5 3.0 %collective-permute-start.10 = (f32[9,8,128]{2,1,0:T(8,128)S(1)}, f32[9,8,128]{2,1,0:T(8,128)S(1)}, u32[]{:S(2)}, u32[]{:S(2)}) collective-permute-start(f32[9,8,128]{2,1,0:T(8,128)S(1)} %quad.1.mine), channel_id=1, source_target_pairs={{0,8},{2,10},{4,12},{6,14},{8,0},{10,2},{12,4},{14,6},{1,9},{3,11}... | collective-permute-start | bytes 110600 | tf_op jit(solution)/shard_map/ppermute | solution.py:87
  25.5 2.0 %collective-permute-done.10.other = f32[9,8,128]{2,1,0:T(8,128)S(1)} collective-permute-done((f32[9,8,128]{2,1,0:T(8,128)S(1)}, f32[9,8,128]{2,1,0:T(8,128)S(1)}, u32[]{:S(2)}, u32[]{:S(2)}) %collective-permute-start.10) | collective-permute-done | bytes 36896 | tf_op jit(solution)/shard_map/ppermute | solution.py:87
  27.5 0.1 high.1
  27.7 0.0 collective-permute-start.11
  27.7 1.0 %collective-permute-start.12 = (f32[9,8,128]{2,1,0:T(8,128)S(1)}, f32[9,8,128]{2,1,0:T(8,128)S(1)}, u32[]{:S(2)}, u32[]{:S(2)}) collective-permute-start(f32[9,8,128]{2,1,0:T(8,128)S(1)} %high.1), channel_id=1, source_target_pairs={{0,3},{1,2},{2,1},{3,0},{4,7},{5,6},{6,5},{7,4},{8,11},{9,10},{10,... | collective-permute-start | bytes 110600 | tf_op jit(solution)/shard_map/ppermute | solution.py:96
  28.7 1.4 %collective-permute-start.13 = (f32[9,8,128]{2,1,0:T(8,128)S(1)}, f32[9,8,128]{2,1,0:T(8,128)S(1)}, u32[]{:S(2)}, u32[]{:S(2)}) collective-permute-start(f32[9,8,128]{2,1,0:T(8,128)S(1)} %high.1), channel_id=1, source_target_pairs={{0,5},{1,4},{2,7},{3,6},{4,1},{5,0},{6,3},{7,2},{8,13},{9,12},{10,... | collective-permute-start | bytes 110600 | tf_op jit(solution)/shard_map/ppermute | solution.py:96
  30.1 0.9 %collective-permute-start.14 = (f32[9,8,128]{2,1,0:T(8,128)S(1)}, f32[9,8,128]{2,1,0:T(8,128)S(1)}, u32[]{:S(2)}, u32[]{:S(2)}) collective-permute-start(f32[9,8,128]{2,1,0:T(8,128)S(1)} %high.1), channel_id=1, source_target_pairs={{0,7},{1,6},{2,5},{3,4},{4,3},{5,2},{6,1},{7,0},{8,15},{9,14},{10,... | collective-permute-start | bytes 110600 | tf_op jit(solution)/shard_map/ppermute | solution.py:96
  31.0 0.0 collective-permute-done.11.refs_0_
  31.0 0.1 collective-permute-done.12.refs_1_
  31.1 1.0 %collective-permute-done.13.refs_2_ = f32[9,8,128]{2,1,0:T(8,128)S(1)} collective-permute-done((f32[9,8,128]{2,1,0:T(8,128)S(1)}, f32[9,8,128]{2,1,0:T(8,128)S(1)}, u32[]{:S(2)}, u32[]{:S(2)}) %collective-permute-start.13) | collective-permute-done | bytes 36896 | tf_op jit(solution)/shard_map/ppermute | solution.py:96
  32.1 2.3 %collective-permute-done.14.refs_3_ = f32[9,8,128]{2,1,0:T(8,128)S(1)} collective-permute-done((f32[9,8,128]{2,1,0:T(8,128)S(1)}, f32[9,8,128]{2,1,0:T(8,128)S(1)}, u32[]{:S(2)}, u32[]{:S(2)}) %collective-permute-start.14) | collective-permute-done | bytes 36896 | tf_op jit(solution)/shard_map/ppermute | solution.py:96
  34.4 0.3 second.1
  34.7 0.6 %collective-permute-start.15 = (f32[4,256]{1,0:T(4,128)S(1)}, f32[4,256]{1,0:T(4,128)S(1)}, u32[]{:S(2)}, u32[]{:S(2)}) collective-permute-start(f32[4,256]{1,0:T(4,128)S(1)} %get-tuple-element.41), channel_id=1, source_target_pairs={{0,1},{1,0},{2,3},{3,2},{4,5},{5,4},{6,7},{7,6},{8,9},{9,8},{10,11... | collective-permute-start | bytes 12296 | tf_op jit(solution)/shard_map/ppermute | solution.py:83
  35.3 1.1 %update.1 = f32[128,256]{1,0:T(8,128)} custom-call(f32[64,128]{1,0:T(8,128)S(1)} %get-tuple-element.32.k0, f32[64,128]{1,0:T(8,128)S(1)} %get-tuple-element.33.k1, f32[64,256]{1,0:T(8,128)S(1)} %get-tuple-element.38.res0, f32[64,256]{1,0:T(8,128)S(1)} %get-tuple-element.39.res1, f32[128,256]{1,0:T(8,128)S(1)} %copy-done), custom_call_target="tpu_custom_call" | custom-call | tf_op jit(solution)/shard_map/update/pallas_call | solution.py:57
  36.3 0.0 collective-permute-done.15.back
  36.3 0.6 %finish.1 = f32[4,512]{1,0:T(4,128)} custom-call(f32[4,256]{1,0:T(4,128)S(1)} %get-tuple-element.40.mine, f32[4,256]{1,0:T(4,128)S(1)} %collective-permute-done.15.back), custom_call_target="tpu_custom_call" | custom-call | tf_op jit(solution)/shard_map/finish/pallas_call | solution.py:57
  (4 shorter events, 0.0 us)
Async XLA Ops:
  1.5 5.6 %collective-permute-start = (f32[8,1024]{1,0:T(8,128)S(1)}, f32[8,1024]{1,0:T(8,128)S(1)}, u32[]{:S(2)}, u32[]{:S(2)}) collective-permute-start(f32[8,1024]{1,0:T(8,128)S(1)} %pick.1), channel_id=1, source_target_pairs={{0,9},{1,8},{2,11},{3,10},{4,13},{5,12},{6,15},{7,14},{8,1},{9,0},... | collective-permute-start | bytes 98312 | tf_op jit(solution)/shard_map/ppermute | solution.py:96
  5.1 9.5 %collective-permute-start.1 = (f32[128,256]{1,0:T(8,128)}, f32[128,256]{1,0:T(8,128)S(1)}, u32[]{:S(2)}, u32[]{:S(2)}) collective-permute-start(f32[128,256]{1,0:T(8,128)} %weights.1), channel_id=1, source_target_pairs={{0,1},{1,0},{2,3},{3,2},{4,5},{5,4},{6,7},{7,6},{8,9},{9,8},{10,11... | collective-permute-start | bytes 393224 | tf_op jit(solution)/shard_map/ppermute | solution.py:83
  7.1 5.0 %collective-permute-start.5 = (f32[16,1024]{1,0:T(8,128)S(1)}, f32[16,1024]{1,0:T(8,128)S(1)}, u32[]{:S(2)}, u32[]{:S(2)}) collective-permute-start(f32[16,1024]{1,0:T(8,128)S(1)} %pad_maximum_fusion.rows), channel_id=1, source_target_pairs={{0,7},{1,6},{2,5},{3,4},{4,3},{5,2},{6,1},{7,0},{8,15},{9,14},{10,... | collective-permute-start | bytes 196616 | tf_op jit(solution)/shard_map/ppermute | solution.py:96
  9.6 4.0 %collective-permute-start.4 = (f32[16,1024]{1,0:T(8,128)S(1)}, f32[16,1024]{1,0:T(8,128)S(1)}, u32[]{:S(2)}, u32[]{:S(2)}) collective-permute-start(f32[16,1024]{1,0:T(8,128)S(1)} %pad_maximum_fusion.rows), channel_id=1, source_target_pairs={{0,5},{1,4},{2,7},{3,6},{4,1},{5,0},{6,3},{7,2},{8,13},{9,12},{10,... | collective-permute-start | bytes 196616 | tf_op jit(solution)/shard_map/ppermute | solution.py:96
  10.1 4.1 %collective-permute-start.3 = (f32[16,1024]{1,0:T(8,128)S(1)}, f32[16,1024]{1,0:T(8,128)S(1)}, u32[]{:S(2)}, u32[]{:S(2)}) collective-permute-start(f32[16,1024]{1,0:T(8,128)S(1)} %pad_maximum_fusion.rows), channel_id=1, source_target_pairs={{0,3},{1,2},{2,1},{3,0},{4,7},{5,6},{6,5},{7,4},{8,11},{9,10},{10,... | collective-permute-start | bytes 196616 | tf_op jit(solution)/shard_map/ppermute | solution.py:96
  10.3 4.3 %collective-permute-start.2 = (f32[2,4,512]{2,1,0:T(4,128)S(1)}, f32[2,4,512]{2,1,0:T(4,128)S(1)}, u32[]{:S(2)}, u32[]{:S(2)}) collective-permute-start(f32[2,4,512]{2,1,0:T(4,128)S(1)} %get-tuple-element.28.refs_4_), channel_id=1, source_target_pairs={{0,1},{1,0},{2,3},{3,2},{4,5},{5,4},{6,7},{7,6},{8,9},{9,8},{10,11... | collective-permute-start | bytes 49160 | tf_op jit(solution)/shard_map/ppermute | solution.py:83
  14.2 1.7 %copy-start = (f32[128,256]{1,0:T(8,128)S(1)}, f32[128,256]{1,0:T(8,128)}, u32[]{:S(2)}) copy-start(f32[128,256]{1,0:T(8,128)} %weights.1) | copy-start | bytes 393220
  14.6 1.4 %collective-permute-start.6 = (f32[64,128]{1,0:T(8,128)S(1)}, f32[64,128]{1,0:T(8,128)S(1)}, u32[]{:S(2)}, u32[]{:S(2)}) collective-permute-start(f32[64,128]{1,0:T(8,128)S(1)} %pad_maximum_fusion.1.refs_0_), channel_id=1, source_target_pairs={{0,1},{1,0},{2,3},{3,2},{4,5},{5,4},{6,7},{7,6},{8,9},{9,8},{10,11... | collective-permute-start | bytes 98312 | tf_op jit(solution)/shard_map/ppermute | solution.py:83
  16.5 4.3 %collective-permute-start.7 = (f32[9,8,128]{2,1,0:T(8,128)S(1)}, f32[9,8,128]{2,1,0:T(8,128)S(1)}, u32[]{:S(2)}, u32[]{:S(2)}) collective-permute-start(f32[9,8,128]{2,1,0:T(8,128)S(1)} %get-tuple-element.35), channel_id=1, source_target_pairs={{0,7},{1,6},{2,5},{3,4},{4,3},{5,2},{6,1},{7,0},{8,15},{9,14},{10,... | collective-permute-start | bytes 110600 | tf_op jit(solution)/shard_map/ppermute | solution.py:96
  18.6 3.4 %collective-permute-start.8 = (f32[9,8,128]{2,1,0:T(8,128)S(1)}, f32[9,8,128]{2,1,0:T(8,128)S(1)}, u32[]{:S(2)}, u32[]{:S(2)}) collective-permute-start(f32[9,8,128]{2,1,0:T(8,128)S(1)} %get-tuple-element.36), channel_id=1, source_target_pairs={{0,5},{1,4},{2,7},{3,6},{4,1},{5,0},{6,3},{7,2},{8,13},{9,12},{10,... | collective-permute-start | bytes 110600 | tf_op jit(solution)/shard_map/ppermute | solution.py:96
  19.0 3.4 %collective-permute-start.9 = (f32[9,8,128]{2,1,0:T(8,128)S(1)}, f32[9,8,128]{2,1,0:T(8,128)S(1)}, u32[]{:S(2)}, u32[]{:S(2)}) collective-permute-start(f32[9,8,128]{2,1,0:T(8,128)S(1)} %get-tuple-element.37), channel_id=1, source_target_pairs={{0,3},{1,2},{2,1},{3,0},{4,7},{5,6},{6,5},{7,4},{8,11},{9,10},{10,... | collective-permute-start | bytes 110600 | tf_op jit(solution)/shard_map/ppermute | solution.py:96
  22.5 5.0 %collective-permute-start.10 = (f32[9,8,128]{2,1,0:T(8,128)S(1)}, f32[9,8,128]{2,1,0:T(8,128)S(1)}, u32[]{:S(2)}, u32[]{:S(2)}) collective-permute-start(f32[9,8,128]{2,1,0:T(8,128)S(1)} %quad.1.mine), channel_id=1, source_target_pairs={{0,8},{2,10},{4,12},{6,14},{8,0},{10,2},{12,4},{14,6},{1,9},{3,11}... | collective-permute-start | bytes 110600 | tf_op jit(solution)/shard_map/ppermute | solution.py:87
  27.7 3.3 %collective-permute-start.11 = (f32[9,8,128]{2,1,0:T(8,128)S(1)}, f32[9,8,128]{2,1,0:T(8,128)S(1)}, u32[]{:S(2)}, u32[]{:S(2)}) collective-permute-start(f32[9,8,128]{2,1,0:T(8,128)S(1)} %high.1), channel_id=1, source_target_pairs={{0,1},{1,0},{2,3},{3,2},{4,5},{5,4},{6,7},{7,6},{8,9},{9,8},{10,11... | collective-permute-start | bytes 110600 | tf_op jit(solution)/shard_map/ppermute | solution.py:83
  27.7 3.4 %collective-permute-start.12 = (f32[9,8,128]{2,1,0:T(8,128)S(1)}, f32[9,8,128]{2,1,0:T(8,128)S(1)}, u32[]{:S(2)}, u32[]{:S(2)}) collective-permute-start(f32[9,8,128]{2,1,0:T(8,128)S(1)} %high.1), channel_id=1, source_target_pairs={{0,3},{1,2},{2,1},{3,0},{4,7},{5,6},{6,5},{7,4},{8,11},{9,10},{10,... | collective-permute-start | bytes 110600 | tf_op jit(solution)/shard_map/ppermute | solution.py:96
  28.7 3.4 %collective-permute-start.13 = (f32[9,8,128]{2,1,0:T(8,128)S(1)}, f32[9,8,128]{2,1,0:T(8,128)S(1)}, u32[]{:S(2)}, u32[]{:S(2)}) collective-permute-start(f32[9,8,128]{2,1,0:T(8,128)S(1)} %high.1), channel_id=1, source_target_pairs={{0,5},{1,4},{2,7},{3,6},{4,1},{5,0},{6,3},{7,2},{8,13},{9,12},{10,... | collective-permute-start | bytes 110600 | tf_op jit(solution)/shard_map/ppermute | solution.py:96
  30.1 4.3 %collective-permute-start.14 = (f32[9,8,128]{2,1,0:T(8,128)S(1)}, f32[9,8,128]{2,1,0:T(8,128)S(1)}, u32[]{:S(2)}, u32[]{:S(2)}) collective-permute-start(f32[9,8,128]{2,1,0:T(8,128)S(1)} %high.1), channel_id=1, source_target_pairs={{0,7},{1,6},{2,5},{3,4},{4,3},{5,2},{6,1},{7,0},{8,15},{9,14},{10,... | collective-permute-start | bytes 110600 | tf_op jit(solution)/shard_map/ppermute | solution.py:96
  34.7 1.6 %collective-permute-start.15 = (f32[4,256]{1,0:T(4,128)S(1)}, f32[4,256]{1,0:T(4,128)S(1)}, u32[]{:S(2)}, u32[]{:S(2)}) collective-permute-start(f32[4,256]{1,0:T(4,128)S(1)} %get-tuple-element.41), channel_id=1, source_target_pairs={{0,1},{1,0},{2,3},{3,2},{4,5},{5,4},{6,7},{7,6},{8,9},{9,8},{10,11... | collective-permute-start | bytes 12296 | tf_op jit(solution)/shard_map/ppermute | solution.py:83

commit v6 on v5

--- a/solution.py
+++ b/solution.py
@@ -11,7 +11,7 @@
 
 LANES = 128
 QUAD = 4
-KEPT_BYTES = 1 << 20
+KEPT_BYTES = 400 << 10
 
 
 class Plan(NamedTuple):
@@ -49,16 +49,17 @@
 
 
 def small(x):
-    return math.prod(x.shape) * jnp.dtype(x.dtype).itemsize <= KEPT_BYTES
-
-
-def call(body, outs, name, *args, **kwargs):
+    bytes_each = jnp.dtype(x.dtype).itemsize
+    return bytes_each == 2 or math.prod(x.shape) * bytes_each <= KEPT_BYTES
+
+
+def call(body, outs, name, *args, out_space=pltpu.VMEM, **kwargs):
     args = [a if isinstance(a, tuple) else (a, pltpu.VMEM) for a in args]
     return pl.pallas_call(
         body,
         out_shape=outs,
         in_specs=[pl.BlockSpec(memory_space=space) for _, space in args],
-        out_specs=[pl.BlockSpec(memory_space=pltpu.VMEM)] * len(outs),
+        out_specs=[pl.BlockSpec(memory_space=out_space)] * len(outs),
         name=name,
         **kwargs,
     )(
@@ -140,6 +141,21 @@
     return out
 
 
+def parts_dot(left, right, axis):
+    n = left[0].shape[0]
+    total = 0.0
+    for i in (2, 1, 0):
+        part = lax.dot_general(
+            jnp.concatenate(left[: 3 - i], 0),
+            right[i],
+            (((1,), (axis,)), ((), ())),
+            preferred_element_type=jnp.float32,
+        )
+        for j in reversed(range(3 - i)):
+            total = total + part[j * n : (j + 1) * n]
+    return total
+
+
 def prepare_body(centers, targets, split_out, row_out, targets_out, held, sems):
     copies = [
         pltpu.make_async_copy(a, b, sems.at[i])
@@ -158,17 +174,8 @@
 
 def kernel_body(gamma, rows, split, row, out):
     x = rows[...]
-    n = x.shape[0]
     row_sq = jnp.sum(x * x, axis=1, keepdims=True)
-    xs = parts(x)
-    cross = 0.0
-    for i in (2, 1, 0):
-        left = jnp.concatenate(xs[: 3 - i], 0)
-        part = lax.dot_general(
-            left, split[i], (((1,), (1,)), ((), ())), preferred_element_type=jnp.float32
-        )
-        for j in reversed(range(3 - i)):
-            cross = cross + part[j * n : (j + 1) * n]
+    cross = parts_dot(parts(x), split, 1)
     out[...] = jnp.exp(-gamma[:1] * (row_sq + row[:1] - 2.0 * cross))
 
 
@@ -189,28 +196,41 @@
     return [half[:, i : i + LANES] for i in range(0, cols, LANES)]
 
 
+def half_sums(plan, k, split):
+    span = plan.high * plan.each
+    return jnp.concatenate(
+        [
+            parts_dot(parts(k[:span]), split[1], 0),
+            parts_dot(parts(k[span:]), split[0], 0),
+        ],
+        0,
+    )
+
+
+def weights_body(plan, own, w_mine, w_theirs, split_out, out):
+    for side, w in enumerate((w_mine, w_theirs)):
+        for i, part in enumerate(parts(w[...])):
+            split_out[side, i] = part
+    out[...] = half_sums(plan, own[...], split_out)
+
+
 def predict_body(plan, *refs):
-    own, swapped, w_mine, w_theirs, t_mine, t_theirs, k0_out, k1_out, *outs = refs
+    own, swapped, mine_sums, split, t_mine, t_theirs, k0_out, k1_out, *outs = refs
     each, high = plan.each, plan.high
-    n = own.shape[0]
     me = lax.axis_index("row")
     span = high * each
+    sums = half_sums(plan, swapped[...], split)
     for q in range(QUAD):
         for h in range(high):
             at = q * span + h * each
             crossed = (q > 0) ^ (h.bit_count() & 1)
             tile = slice(at, at + each)
             k0_out[tile], k1_out[tile] = by_batch(me == crossed, own[tile], swapped[tile])
+            for b, rows in enumerate(by_batch(me == crossed, mine_sums[tile], sums[tile])):
+                for c in range(plan.col_tiles):
+                    to = (b * plan.col_tiles + c) * high + h
+                    outs[q][to] = rows[:, c * LANES : (c + 1) * LANES]
     k0, k1 = k0_out[...], k1_out[...]
-    for b, k in enumerate((k0, k1)):
-        kept_part = dot(k[:span], w_theirs[...], ((1,), (0,)))
-        sent_part = dot(k[span:], w_mine[...], ((1,), (0,)))
-        part = jnp.concatenate([kept_part, sent_part], 0)
-        for q, out in enumerate(outs):
-            for c in range(plan.col_tiles):
-                tile = part[q * span : (q + 1) * span, c * LANES : (c + 1) * LANES]
-                at = (b * plan.col_tiles + c) * high
-                out[at : at + high] = tile.reshape(high, each, LANES)
     for c, (mine, theirs) in enumerate(
         zip(target_tiles(t_mine, 1 - me), target_tiles(t_theirs, 1 - me))
     ):
@@ -253,49 +273,64 @@
             out[plan.sums + u * t + r] = mine[plan.sums + u * t + r] + tile
 
 
-def second_body(plan, rate, *refs):
-    *packets, out0, out1, mine_out, theirs_out = refs
+def unpack(plan, packets, b):
     span = plan.high * plan.each
+    rows = []
+    for packet in packets:
+        at = [(b * plan.col_tiles + c) * plan.high for c in range(plan.col_tiles)]
+        tiles = [packet[i : i + plan.high].reshape(span, LANES) for i in at]
+        rows.append(jnp.concatenate(tiles, 1))
+    return jnp.concatenate(rows, 0)
+
+
+def gram_of(plan, packet, q):
+    t = plan.gram_rows
+    tiles = [packet[plan.sums + u * t : plan.sums + (u + 1) * t] for u in range(plan.gram_tiles)]
+    packed = jnp.concatenate(seen_by(plan, tiles, q), 2)
+    lane = lax.broadcasted_iota(jnp.int32, packed.shape, 2) // plan.width
+    return jnp.stack([jnp.where(lane == i, packed, 0.0) for i in range(plan.pack)], 1)
+
+
+def chip_body(plan, rate, *refs):
+    *packets, mine_out, theirs_out = refs
+    packets = packets[::-1]
     half = plan.each // 2
-    for b, out in enumerate((out0, out1)):
-        for q, packet in enumerate(packets):
-            for c in range(plan.col_tiles):
-                at = (b * plan.col_tiles + c) * plan.high
-                out[q * span : (q + 1) * span, c * LANES : (c + 1) * LANES] = packet[
-                    at : at + plan.high
-                ].reshape(span, LANES)
-    res0 = out0[...]
-    res0 = jnp.concatenate([res0] * plan.pack, 0)
-    t = plan.gram_rows
-    grams = []
-    for q, packet in enumerate(packets):
-        tiles = [
-            packet[plan.sums + u * t : plan.sums + (u + 1) * t] for u in range(plan.gram_tiles)
-        ]
-        tiles = seen_by(plan, tiles, q)
-        packed = jnp.concatenate(tiles, 2)
-        lane = lax.broadcasted_iota(jnp.int32, packed.shape, 2) // plan.width
-        rows = [jnp.where(lane == i, packed, 0.0) for i in range(plan.pack)]
-        grams.append(jnp.stack(rows, 1).reshape(span, packed.shape[2]))
-    gram = jnp.concatenate(grams, 0)
-    out1[...] = out1[...] - rate * dot(gram, res0, ((1,), (0,)))
+    res0 = jnp.concatenate([unpack(plan, packets, 0)] * plan.pack, 0)
+    gram = gram_of(plan, packets[0], 0)[0, 0]
+    at = [(plan.col_tiles + c) * plan.high for c in range(plan.col_tiles)]
+    late = jnp.concatenate([packets[0][i] for i in at], 1)
+    late = late - rate * dot(gram, res0, ((1,), (0,)))
     first = lax.axis_index("row") == 0
-    a, b = out1[:half], out1[half : 2 * half]
+    a, b = late[:half], late[half:]
     mine_out[...] = jnp.where(first, a, b)
     theirs_out[...] = jnp.where(first, b, a)
 
 
-def update_body(rate, k0, k1, res0, res1, weights, out):
-    grad = dot(k0[...], res0[...], ((0,), (0,))) + dot(k1[...], res1[...], ((0,), (0,)))
+def update_body(plan, rate, *refs):
+    k0, k1, weights, *packets, out = refs
+    packets = packets[::-1]
+    res0, late = unpack(plan, packets, 0), unpack(plan, packets, 1)
+    grams = [gram_of(plan, packet, q) for q, packet in enumerate(packets)]
+    gram = jnp.concatenate([g.reshape(-1, g.shape[-1]) for g in grams], 0)
+    res1 = late - rate * dot(gram, jnp.concatenate([res0] * plan.pack, 0), ((1,), (0,)))
+    grad = dot(k0[...], res0, ((0,), (0,))) + dot(k1[...], res1, ((0,), (0,)))
     out[...] = weights[...] - rate * grad
 
 
-def finish_body(mine, back, out):
+def finish_body(weights, mine, back, weights_out, residual_out, residual, sems):
+    copies = [
+        pltpu.make_async_copy(a, b, sems.at[i])
+        for i, (a, b) in enumerate(((weights, weights_out), (residual, residual_out)))
+    ]
+    copies[0].start()
     first = lax.axis_index("row") == 0
     a, b = mine[...], back[...]
     cols = a.shape[1]
-    out[:, :cols] = jnp.where(first, a, b)
-    out[:, cols:] = jnp.where(first, b, a)
+    residual[:, :cols] = jnp.where(first, a, b)
+    residual[:, cols:] = jnp.where(first, b, a)
+    copies[1].start()
+    for c in copies:
+        c.wait()
 
 
 def per_device(dataset, centers, weights, batch_index, targets, gamma):
@@ -346,7 +381,6 @@
     rows = local
     for bit in bits:
         rows = jnp.concatenate([rows, across(rows, QUAD * bit)], 0)
-    rows, split, row, targets = lax.optimization_barrier((rows, split, row, targets))
     own = [
         call(kernel_body, [kept(span, count)], "kernel", spread, x, split, row)[0]
         for x in [rows] + [across(rows, q) for q in quad]
@@ -356,14 +390,23 @@
     )
     own = jnp.concatenate(own, 0)
     packet = (plan.tiles, each, LANES)
+    swapped = swap_cores(own)
+    weight_split, mine_sums = call(
+        functools.partial(weights_body, plan),
+        [pltpu.VMEM((2, 3, count, cols), jnp.bfloat16), kept(n, cols)],
+        "weights",
+        own,
+        weights,
+        weights_other,
+    )
     k0, k1, keep, *sent = call(
         functools.partial(predict_body, plan),
         [kept(n, count)] * 2 + [kept(*packet)] * QUAD,
         "predict",
         own,
-        swap_cores(own),
-        weights,
-        weights_other,
+        swapped,
+        mine_sums,
+        weight_split,
         targets,
         targets_other,
     )
@@ -382,25 +425,33 @@
             total,
             partner(total, QUAD * bit),
         )
-    res0, res1, mine, theirs = call(
-        functools.partial(second_body, plan, rate),
-        [kept(n, cols)] * 2 + [kept(rows_here, cols)] * 2,
-        "second",
-        swap_cores(total),
-        *[across(total, q) for q in quad],
+    packets = [across(total, q) for q in reversed(quad)] + [swap_cores(total)]
+    mine, theirs = call(
+        functools.partial(chip_body, plan, rate), [kept(rows_here, cols)] * 2, "chip", *packets
     )
     back = swap_cores(theirs)
     (new_weights,) = call(
-        functools.partial(update_body, rate),
-        [stored(count, cols)],
+        functools.partial(update_body, plan, rate),
+        [kept(count, cols)],
         "update",
         k0,
         k1,
-        res0,
-        res1,
         weights,
-    )
-    (residual,) = call(finish_body, [stored(rows_here, 2 * cols)], "finish", mine, back)
+        *packets,
+    )
+    new_weights, residual = call(
+        finish_body,
+        [stored(count, cols), stored(rows_here, 2 * cols)],
+        "finish",
+        new_weights,
+        mine,
+        back,
+        out_space=pl.ANY,
+        scratch_shapes=[
+            pltpu.VMEM((rows_here, 2 * cols), jnp.float32),
+            pltpu.SemaphoreType.DMA((2,)),
+        ],
+    )
     return (new_weights, residual)
 
 

time: 37.1 us -> 35.2 us (0.949)
  waiting for transfers between devices: 11.1 us -> 9.65 us
    ppermute x10, waiting for transfers between devices: 8.21 us -> 6.79 us  [across(): return lax.ppermute(x, ('center', 'row'), pairs)]
    pallas_call x12 -> x13, Pallas kernels: 6.2 us -> 5.85 us  [call(): pl.pallas_call(body, out_shape=outs, in_specs=[pl.BlockSpec(memory_space=...]
where the time goes in v6:
time: 35.2 us; the launch traced here: 35 us
  starting transfers between devices  18.1 us (51%)
  waiting for transfers between devices  9.65 us (27%)
  Pallas kernels  5.85 us (17%)
  between operations  1.37 us (4%)
    ppermute x10, starting transfers between devices, across(): return lax.ppermute(x, ('center', 'row'), pairs)  13.3 us
    ppermute x10, waiting for transfers between devices, across(): return lax.ppermute(x, ('center', 'row'), pairs)  6.79 us
    pallas_call x13, Pallas kernels, call(): pl.pallas_call(body, out_shape=outs, in_specs=[pl.BlockSpec(memory_space=...  5.85 us
    ppermute x1, starting transfers between devices, partner(): lax.ppermute(x, 'center', [(i, i ^ bits) for i in range(lax.axis_size('ce...  3.07 us
    ppermute x1, waiting for transfers between devices, partner(): lax.ppermute(x, 'center', [(i, i ^ bits) for i in range(lax.axis_size('ce...  1.99 us
    ppermute x5, starting transfers between devices, swap_cores(): return lax.ppermute(x, 'row', [(0, 1), (1, 0)])  1.71 us
    ppermute x5, waiting for transfers between devices, swap_cores(): return lax.ppermute(x, 'row', [(0, 1), (1, 0)])  0.87 us
  transfers between devices with their start and end apart: 16, of which 11 were waited for; matrix products, arithmetic and copies ran while one was open for 0% of the time, Pallas kernels for 10%

profile of v6, /device:TPU:0, one launch (start us, length us, event | category | flops | bytes accessed | tf_op | source)
XLA Modules:
  0.0 35.0 jit_solution(11459565673473338871)
XLA Ops:
  0.6 0.9 %pick.1 = f32[8,1024]{1,0:T(8,128)S(1)} custom-call(s32[2,4]{1,0:T(2,128)} %index.1, f32[16,1024]{1,0:T(8,128)} %dataset.1), custom_call_target="tpu_custom_call" | custom-call | tf_op jit(solution)/shard_map/pick/pallas_call | solution.py:58
  1.5 3.6 %collective-permute-start = (f32[8,1024]{1,0:T(8,128)S(1)}, f32[8,1024]{1,0:T(8,128)S(1)}, u32[]{:S(2)}, u32[]{:S(2)}) collective-permute-start(f32[8,1024]{1,0:T(8,128)S(1)} %pick.1), channel_id=1, source_target_pairs={{0,9},{1,8},{2,11},{3,10},{4,13},{5,12},{6,15},{7,14},{8,1},{9,0},... | collective-permute-start | bytes 98312 | tf_op jit(solution)/shard_map/ppermute | solution.py:97
  5.1 0.7 %collective-permute-start.1 = (f32[128,256]{1,0:T(8,128)}, f32[128,256]{1,0:T(8,128)S(1)}, u32[]{:S(2)}, u32[]{:S(2)}) collective-permute-start(f32[128,256]{1,0:T(8,128)} %refs_2_.1), channel_id=1, source_target_pairs={{0,1},{1,0},{2,3},{3,2},{4,5},{5,4},{6,7},{7,6},{8,9},{9,8},{10,11... | collective-permute-start | bytes 393224 | tf_op jit(solution)/shard_map/ppermute | solution.py:84
  5.8 1.1 %collective-permute-done = f32[8,1024]{1,0:T(8,128)S(1)} collective-permute-done((f32[8,1024]{1,0:T(8,128)S(1)}, f32[8,1024]{1,0:T(8,128)S(1)}, u32[]{:S(2)}, u32[]{:S(2)}) %collective-permute-start) | collective-permute-done | bytes 32800 | tf_op jit(solution)/shard_map/ppermute | solution.py:97
  6.9 2.8 %collective-permute-start.5 = (f32[16,1024]{1,0:T(8,128)S(1)}, f32[16,1024]{1,0:T(8,128)S(1)}, u32[]{:S(2)}, u32[]{:S(2)}) collective-permute-start(f32[16,1024]{1,0:T(8,128)S(1)} %pad_maximum_fusion.rows), channel_id=1, source_target_pairs={{0,7},{1,6},{2,5},{3,4},{4,3},{5,2},{6,1},{7,0},{8,15},{9,14},{10,... | collective-permute-start | bytes 196616 | tf_op jit(solution)/shard_map/ppermute | solution.py:97
  9.6 0.4 %collective-permute-start.4 = (f32[16,1024]{1,0:T(8,128)S(1)}, f32[16,1024]{1,0:T(8,128)S(1)}, u32[]{:S(2)}, u32[]{:S(2)}) collective-permute-start(f32[16,1024]{1,0:T(8,128)S(1)} %pad_maximum_fusion.rows), channel_id=1, source_target_pairs={{0,5},{1,4},{2,7},{3,6},{4,1},{5,0},{6,3},{7,2},{8,13},{9,12},{10,... | collective-permute-start | bytes 196616 | tf_op jit(solution)/shard_map/ppermute | solution.py:97
  10.1 0.2 collective-permute-start.3
  10.3 1.3 %prepare.1 = (bf16[3,128,1024]{2,1,0:T(8,128)(2,1)S(1)}, f32[8,128]{1,0:T(8,128)S(1)}, f32[2,4,512]{2,1,0:T(4,128)S(1)}) custom-call(f32[128,1024]{1,0:T(8,128)} %centers.1, f32[2,4,512]{2,1,0:T(4,128)} %targets.1), custom_call_target="tpu_custom_call" | custom-call | tf_op jit(solution)/shard_map/prepare/pallas_call | solution.py:58
  11.6 0.2 collective-permute-start.2
  12.4 0.3 kernel.4
  12.8 0.0 collective-permute-done.5.rows
  12.8 0.3 kernel.7
  13.1 0.5 %collective-permute-done.4.rows = f32[16,1024]{1,0:T(8,128)S(1)} collective-permute-done((f32[16,1024]{1,0:T(8,128)S(1)}, f32[16,1024]{1,0:T(8,128)S(1)}, u32[]{:S(2)}, u32[]{:S(2)}) %collective-permute-start.4) | collective-permute-done | bytes 65568 | tf_op jit(solution)/shard_map/ppermute | solution.py:97
  13.7 0.3 kernel.6
  14.0 0.2 collective-permute-done.3.rows
  14.2 0.0 copy-start
  14.2 0.3 kernel.5
  14.5 0.0 collective-permute-done.2.refs_5_
  14.5 0.0 collective-permute-done.1.w_theirs
  14.6 0.5 %collective-permute-start.6 = (f32[64,128]{1,0:T(8,128)S(1)}, f32[64,128]{1,0:T(8,128)S(1)}, u32[]{:S(2)}, u32[]{:S(2)}) collective-permute-start(f32[64,128]{1,0:T(8,128)S(1)} %pad_maximum_fusion.1.own.refs_0_), channel_id=1, source_target_pairs={{0,1},{1,0},{2,3},{3,2},{4,5},{5,4},{6,7},{7,6},{8,9},{9,8},{10,11... | collective-permute-start | bytes 98312 | tf_op jit(solution)/shard_map/ppermute | solution.py:84
  15.1 0.0 copy-done
  15.1 0.2 weights.1
  15.3 0.6 %collective-permute-done.6.refs_1_ = f32[64,128]{1,0:T(8,128)S(1)} collective-permute-done((f32[64,128]{1,0:T(8,128)S(1)}, f32[64,128]{1,0:T(8,128)S(1)}, u32[]{:S(2)}, u32[]{:S(2)}) %collective-permute-start.6) | collective-permute-done | bytes 32800 | tf_op jit(solution)/shard_map/ppermute | solution.py:84
  15.9 0.4 %predict.1 = (f32[64,128]{1,0:T(8,128)S(1)}, f32[64,128]{1,0:T(8,128)S(1)}, f32[9,8,128]{2,1,0:T(8,128)S(1)}, f32[9,8,128]{2,1,0:T(8,128)S(1)}, f32[9,8,128]{2,1,0:T(8,128)S(1)}, /*index=5*/f32[9,8,128]{2,1,0:T(8,128)S(1)}) custom-call(f32[64,128]{1,0:T(8,128)S(1)} %pad_maximum_fusion.1.own.refs_0_, f32[64,128]{1,0:T(8,128)S(1)} %collective-permute-done.6.refs_1_, ...), custom_call_target="tpu_custom_call" | custom-call | tf_op jit(solution)/shard_map/predict/pallas_call | solution.py:58
  16.3 2.1 %collective-permute-start.7 = (f32[9,8,128]{2,1,0:T(8,128)S(1)}, f32[9,8,128]{2,1,0:T(8,128)S(1)}, u32[]{:S(2)}, u32[]{:S(2)}) collective-permute-start(f32[9,8,128]{2,1,0:T(8,128)S(1)} %get-tuple-element.29), channel_id=1, source_target_pairs={{0,7},{1,6},{2,5},{3,4},{4,3},{5,2},{6,1},{7,0},{8,15},{9,14},{10,... | collective-permute-start | bytes 110600 | tf_op jit(solution)/shard_map/ppermute | solution.py:97
  18.4 0.4 %collective-permute-start.8 = (f32[9,8,128]{2,1,0:T(8,128)S(1)}, f32[9,8,128]{2,1,0:T(8,128)S(1)}, u32[]{:S(2)}, u32[]{:S(2)}) collective-permute-start(f32[9,8,128]{2,1,0:T(8,128)S(1)} %get-tuple-element.30), channel_id=1, source_target_pairs={{0,5},{1,4},{2,7},{3,6},{4,1},{5,0},{6,3},{7,2},{8,13},{9,12},{10,... | collective-permute-start | bytes 110600 | tf_op jit(solution)/shard_map/ppermute | solution.py:97
  18.8 0.7 %collective-permute-start.9 = (f32[9,8,128]{2,1,0:T(8,128)S(1)}, f32[9,8,128]{2,1,0:T(8,128)S(1)}, u32[]{:S(2)}, u32[]{:S(2)}) collective-permute-start(f32[9,8,128]{2,1,0:T(8,128)S(1)} %get-tuple-element.31), channel_id=1, source_target_pairs={{0,3},{1,2},{2,1},{3,0},{4,7},{5,6},{6,5},{7,4},{8,11},{9,10},{10,... | collective-permute-start | bytes 110600 | tf_op jit(solution)/shard_map/ppermute | solution.py:97
  19.5 1.1 %collective-permute-done.7.refs_0_ = f32[9,8,128]{2,1,0:T(8,128)S(1)} collective-permute-done((f32[9,8,128]{2,1,0:T(8,128)S(1)}, f32[9,8,128]{2,1,0:T(8,128)S(1)}, u32[]{:S(2)}, u32[]{:S(2)}) %collective-permute-start.7) | collective-permute-done | bytes 36896 | tf_op jit(solution)/shard_map/ppermute | solution.py:97
  20.6 1.2 %collective-permute-done.8.refs_1_ = f32[9,8,128]{2,1,0:T(8,128)S(1)} collective-permute-done((f32[9,8,128]{2,1,0:T(8,128)S(1)}, f32[9,8,128]{2,1,0:T(8,128)S(1)}, u32[]{:S(2)}, u32[]{:S(2)}) %collective-permute-start.8) | collective-permute-done | bytes 36896 | tf_op jit(solution)/shard_map/ppermute | solution.py:97
  21.8 0.4 %collective-permute-done.9.refs_2_ = f32[9,8,128]{2,1,0:T(8,128)S(1)} collective-permute-done((f32[9,8,128]{2,1,0:T(8,128)S(1)}, f32[9,8,128]{2,1,0:T(8,128)S(1)}, u32[]{:S(2)}, u32[]{:S(2)}) %collective-permute-start.9) | collective-permute-done | bytes 36896 | tf_op jit(solution)/shard_map/ppermute | solution.py:97
  22.3 3.1 %collective-permute-start.10 = (f32[9,8,128]{2,1,0:T(8,128)S(1)}, f32[9,8,128]{2,1,0:T(8,128)S(1)}, u32[]{:S(2)}, u32[]{:S(2)}) collective-permute-start(f32[9,8,128]{2,1,0:T(8,128)S(1)} %quad.1.mine), channel_id=1, source_target_pairs={{0,8},{2,10},{4,12},{6,14},{8,0},{10,2},{12,4},{14,6},{1,9},{3,11}... | collective-permute-start | bytes 110600 | tf_op jit(solution)/shard_map/ppermute | solution.py:88
  25.3 2.0 %collective-permute-done.10.other = f32[9,8,128]{2,1,0:T(8,128)S(1)} collective-permute-done((f32[9,8,128]{2,1,0:T(8,128)S(1)}, f32[9,8,128]{2,1,0:T(8,128)S(1)}, u32[]{:S(2)}, u32[]{:S(2)}) %collective-permute-start.10) | collective-permute-done | bytes 36896 | tf_op jit(solution)/shard_map/ppermute | solution.py:88
  27.3 0.1 high.1
  27.5 1.2 %collective-permute-start.11 = (f32[9,8,128]{2,1,0:T(8,128)S(1)}, f32[9,8,128]{2,1,0:T(8,128)S(1)}, u32[]{:S(2)}, u32[]{:S(2)}) collective-permute-start(f32[9,8,128]{2,1,0:T(8,128)S(1)} %high.1), channel_id=1, source_target_pairs={{0,7},{1,6},{2,5},{3,4},{4,3},{5,2},{6,1},{7,0},{8,15},{9,14},{10,... | collective-permute-start | bytes 110600 | tf_op jit(solution)/shard_map/ppermute | solution.py:97
  28.6 0.9 %collective-permute-start.12 = (f32[9,8,128]{2,1,0:T(8,128)S(1)}, f32[9,8,128]{2,1,0:T(8,128)S(1)}, u32[]{:S(2)}, u32[]{:S(2)}) collective-permute-start(f32[9,8,128]{2,1,0:T(8,128)S(1)} %high.1), channel_id=1, source_target_pairs={{0,5},{1,4},{2,7},{3,6},{4,1},{5,0},{6,3},{7,2},{8,13},{9,12},{10,... | collective-permute-start | bytes 110600 | tf_op jit(solution)/shard_map/ppermute | solution.py:97
  29.5 1.1 %collective-permute-start.13 = (f32[9,8,128]{2,1,0:T(8,128)S(1)}, f32[9,8,128]{2,1,0:T(8,128)S(1)}, u32[]{:S(2)}, u32[]{:S(2)}) collective-permute-start(f32[9,8,128]{2,1,0:T(8,128)S(1)} %high.1), channel_id=1, source_target_pairs={{0,3},{1,2},{2,1},{3,0},{4,7},{5,6},{6,5},{7,4},{8,11},{9,10},{10,... | collective-permute-start | bytes 110600 | tf_op jit(solution)/shard_map/ppermute | solution.py:97
  30.6 0.2 collective-permute-start.14
  30.8 1.3 %collective-permute-done.11.refs_3_.refs_0_ = f32[9,8,128]{2,1,0:T(8,128)S(1)} collective-permute-done((f32[9,8,128]{2,1,0:T(8,128)S(1)}, f32[9,8,128]{2,1,0:T(8,128)S(1)}, u32[]{:S(2)}, u32[]{:S(2)}) %collective-permute-start.11) | collective-permute-done | bytes 36896 | tf_op jit(solution)/shard_map/ppermute | solution.py:97
  32.1 0.0 collective-permute-done.12.refs_4_.refs_1_
  32.1 0.9 %collective-permute-done.13.refs_5_.refs_2_ = f32[9,8,128]{2,1,0:T(8,128)S(1)} collective-permute-done((f32[9,8,128]{2,1,0:T(8,128)S(1)}, f32[9,8,128]{2,1,0:T(8,128)S(1)}, u32[]{:S(2)}, u32[]{:S(2)}) %collective-permute-start.13) | collective-permute-done | bytes 36896 | tf_op jit(solution)/shard_map/ppermute | solution.py:97
  33.0 0.0 collective-permute-done.14.refs_6_.refs_3_
  33.0 0.2 chip.1
  33.1 0.2 collective-permute-start.15
  33.3 0.7 %update.1.weights = f32[128,256]{1,0:T(8,128)S(1)} custom-call(f32[64,128]{1,0:T(8,128)S(1)} %get-tuple-element.26.refs_0_, f32[64,128]{1,0:T(8,128)S(1)} %get-tuple-element.27.refs_1_, f32[128,256]{1,0:T(8,128)S(1)} %copy-done, f32[9,8,128]{2,1,0:T(8,128)S(1)} %collective-permute-done.11.refs_3_.refs_0_, ...), custom_call_target="tpu_custom_call" | custom-call | tf_op jit(solution)/shard_map/update/pallas_call | solution.py:58
  34.1 0.2 collective-permute-done.15.back
  34.3 0.7 %finish.1 = (f32[128,256]{1,0:T(8,128)}, f32[4,512]{1,0:T(4,128)}) custom-call(f32[128,256]{1,0:T(8,128)S(1)} %update.1.weights, f32[4,256]{1,0:T(4,128)S(1)} %get-tuple-element.32.mine, f32[4,256]{1,0:T(4,128)S(1)} %collective-permute-done.15.back), custom_call_target="tpu_custom_call" | custom-call | tf_op jit(solution)/shard_map/finish/pallas_call | solution.py:58
  (4 shorter events, 0.0 us)
Async XLA Ops:
  1.5 5.4 %collective-permute-start = (f32[8,1024]{1,0:T(8,128)S(1)}, f32[8,1024]{1,0:T(8,128)S(1)}, u32[]{:S(2)}, u32[]{:S(2)}) collective-permute-start(f32[8,1024]{1,0:T(8,128)S(1)} %pick.1), channel_id=1, source_target_pairs={{0,9},{1,8},{2,11},{3,10},{4,13},{5,12},{6,15},{7,14},{8,1},{9,0},... | collective-permute-start | bytes 98312 | tf_op jit(solution)/shard_map/ppermute | solution.py:97
  5.1 9.5 %collective-permute-start.1 = (f32[128,256]{1,0:T(8,128)}, f32[128,256]{1,0:T(8,128)S(1)}, u32[]{:S(2)}, u32[]{:S(2)}) collective-permute-start(f32[128,256]{1,0:T(8,128)} %refs_2_.1), channel_id=1, source_target_pairs={{0,1},{1,0},{2,3},{3,2},{4,5},{5,4},{6,7},{7,6},{8,9},{9,8},{10,11... | collective-permute-start | bytes 393224 | tf_op jit(solution)/shard_map/ppermute | solution.py:84
  6.9 5.9 %collective-permute-start.5 = (f32[16,1024]{1,0:T(8,128)S(1)}, f32[16,1024]{1,0:T(8,128)S(1)}, u32[]{:S(2)}, u32[]{:S(2)}) collective-permute-start(f32[16,1024]{1,0:T(8,128)S(1)} %pad_maximum_fusion.rows), channel_id=1, source_target_pairs={{0,7},{1,6},{2,5},{3,4},{4,3},{5,2},{6,1},{7,0},{8,15},{9,14},{10,... | collective-permute-start | bytes 196616 | tf_op jit(solution)/shard_map/ppermute | solution.py:97
  9.6 4.0 %collective-permute-start.4 = (f32[16,1024]{1,0:T(8,128)S(1)}, f32[16,1024]{1,0:T(8,128)S(1)}, u32[]{:S(2)}, u32[]{:S(2)}) collective-permute-start(f32[16,1024]{1,0:T(8,128)S(1)} %pad_maximum_fusion.rows), channel_id=1, source_target_pairs={{0,5},{1,4},{2,7},{3,6},{4,1},{5,0},{6,3},{7,2},{8,13},{9,12},{10,... | collective-permute-start | bytes 196616 | tf_op jit(solution)/shard_map/ppermute | solution.py:97
  10.1 4.1 %collective-permute-start.3 = (f32[16,1024]{1,0:T(8,128)S(1)}, f32[16,1024]{1,0:T(8,128)S(1)}, u32[]{:S(2)}, u32[]{:S(2)}) collective-permute-start(f32[16,1024]{1,0:T(8,128)S(1)} %pad_maximum_fusion.rows), channel_id=1, source_target_pairs={{0,3},{1,2},{2,1},{3,0},{4,7},{5,6},{6,5},{7,4},{8,11},{9,10},{10,... | collective-permute-start | bytes 196616 | tf_op jit(solution)/shard_map/ppermute | solution.py:97
  11.6 2.9 %collective-permute-start.2 = (f32[2,4,512]{2,1,0:T(4,128)S(1)}, f32[2,4,512]{2,1,0:T(4,128)S(1)}, u32[]{:S(2)}, u32[]{:S(2)}) collective-permute-start(f32[2,4,512]{2,1,0:T(4,128)S(1)} %get-tuple-element.20.refs_4_), channel_id=1, source_target_pairs={{0,1},{1,0},{2,3},{3,2},{4,5},{5,4},{6,7},{7,6},{8,9},{9,8},{10,11... | collective-permute-start | bytes 49160 | tf_op jit(solution)/shard_map/ppermute | solution.py:84
  14.2 0.9 %copy-start = (f32[128,256]{1,0:T(8,128)S(1)}, f32[128,256]{1,0:T(8,128)}, u32[]{:S(2)}) copy-start(f32[128,256]{1,0:T(8,128)} %refs_2_.1) | copy-start | bytes 393220
  14.6 1.4 %collective-permute-start.6 = (f32[64,128]{1,0:T(8,128)S(1)}, f32[64,128]{1,0:T(8,128)S(1)}, u32[]{:S(2)}, u32[]{:S(2)}) collective-permute-start(f32[64,128]{1,0:T(8,128)S(1)} %pad_maximum_fusion.1.own.refs_0_), channel_id=1, source_target_pairs={{0,1},{1,0},{2,3},{3,2},{4,5},{5,4},{6,7},{7,6},{8,9},{9,8},{10,11... | collective-permute-start | bytes 98312 | tf_op jit(solution)/shard_map/ppermute | solution.py:84
  16.3 4.3 %collective-permute-start.7 = (f32[9,8,128]{2,1,0:T(8,128)S(1)}, f32[9,8,128]{2,1,0:T(8,128)S(1)}, u32[]{:S(2)}, u32[]{:S(2)}) collective-permute-start(f32[9,8,128]{2,1,0:T(8,128)S(1)} %get-tuple-element.29), channel_id=1, source_target_pairs={{0,7},{1,6},{2,5},{3,4},{4,3},{5,2},{6,1},{7,0},{8,15},{9,14},{10,... | collective-permute-start | bytes 110600 | tf_op jit(solution)/shard_map/ppermute | solution.py:97
  18.4 3.4 %collective-permute-start.8 = (f32[9,8,128]{2,1,0:T(8,128)S(1)}, f32[9,8,128]{2,1,0:T(8,128)S(1)}, u32[]{:S(2)}, u32[]{:S(2)}) collective-permute-start(f32[9,8,128]{2,1,0:T(8,128)S(1)} %get-tuple-element.30), channel_id=1, source_target_pairs={{0,5},{1,4},{2,7},{3,6},{4,1},{5,0},{6,3},{7,2},{8,13},{9,12},{10,... | collective-permute-start | bytes 110600 | tf_op jit(solution)/shard_map/ppermute | solution.py:97
  18.8 3.4 %collective-permute-start.9 = (f32[9,8,128]{2,1,0:T(8,128)S(1)}, f32[9,8,128]{2,1,0:T(8,128)S(1)}, u32[]{:S(2)}, u32[]{:S(2)}) collective-permute-start(f32[9,8,128]{2,1,0:T(8,128)S(1)} %get-tuple-element.31), channel_id=1, source_target_pairs={{0,3},{1,2},{2,1},{3,0},{4,7},{5,6},{6,5},{7,4},{8,11},{9,10},{10,... | collective-permute-start | bytes 110600 | tf_op jit(solution)/shard_map/ppermute | solution.py:97
  22.3 5.1 %collective-permute-start.10 = (f32[9,8,128]{2,1,0:T(8,128)S(1)}, f32[9,8,128]{2,1,0:T(8,128)S(1)}, u32[]{:S(2)}, u32[]{:S(2)}) collective-permute-start(f32[9,8,128]{2,1,0:T(8,128)S(1)} %quad.1.mine), channel_id=1, source_target_pairs={{0,8},{2,10},{4,12},{6,14},{8,0},{10,2},{12,4},{14,6},{1,9},{3,11}... | collective-permute-start | bytes 110600 | tf_op jit(solution)/shard_map/ppermute | solution.py:88
  27.5 4.6 %collective-permute-start.11 = (f32[9,8,128]{2,1,0:T(8,128)S(1)}, f32[9,8,128]{2,1,0:T(8,128)S(1)}, u32[]{:S(2)}, u32[]{:S(2)}) collective-permute-start(f32[9,8,128]{2,1,0:T(8,128)S(1)} %high.1), channel_id=1, source_target_pairs={{0,7},{1,6},{2,5},{3,4},{4,3},{5,2},{6,1},{7,0},{8,15},{9,14},{10,... | collective-permute-start | bytes 110600 | tf_op jit(solution)/shard_map/ppermute | solution.py:97
  28.6 3.5 %collective-permute-start.12 = (f32[9,8,128]{2,1,0:T(8,128)S(1)}, f32[9,8,128]{2,1,0:T(8,128)S(1)}, u32[]{:S(2)}, u32[]{:S(2)}) collective-permute-start(f32[9,8,128]{2,1,0:T(8,128)S(1)} %high.1), channel_id=1, source_target_pairs={{0,5},{1,4},{2,7},{3,6},{4,1},{5,0},{6,3},{7,2},{8,13},{9,12},{10,... | collective-permute-start | bytes 110600 | tf_op jit(solution)/shard_map/ppermute | solution.py:97
  29.5 3.4 %collective-permute-start.13 = (f32[9,8,128]{2,1,0:T(8,128)S(1)}, f32[9,8,128]{2,1,0:T(8,128)S(1)}, u32[]{:S(2)}, u32[]{:S(2)}) collective-permute-start(f32[9,8,128]{2,1,0:T(8,128)S(1)} %high.1), channel_id=1, source_target_pairs={{0,3},{1,2},{2,1},{3,0},{4,7},{5,6},{6,5},{7,4},{8,11},{9,10},{10,... | collective-permute-start | bytes 110600 | tf_op jit(solution)/shard_map/ppermute | solution.py:97
  30.6 2.4 %collective-permute-start.14 = (f32[9,8,128]{2,1,0:T(8,128)S(1)}, f32[9,8,128]{2,1,0:T(8,128)S(1)}, u32[]{:S(2)}, u32[]{:S(2)}) collective-permute-start(f32[9,8,128]{2,1,0:T(8,128)S(1)} %high.1), channel_id=1, source_target_pairs={{0,1},{1,0},{2,3},{3,2},{4,5},{5,4},{6,7},{7,6},{8,9},{9,8},{10,11... | collective-permute-start | bytes 110600 | tf_op jit(solution)/shard_map/ppermute | solution.py:84
  33.1 1.2 %collective-permute-start.15 = (f32[4,256]{1,0:T(4,128)S(1)}, f32[4,256]{1,0:T(4,128)S(1)}, u32[]{:S(2)}, u32[]{:S(2)}) collective-permute-start(f32[4,256]{1,0:T(4,128)S(1)} %get-tuple-element.33), channel_id=1, source_target_pairs={{0,1},{1,0},{2,3},{3,2},{4,5},{5,4},{6,7},{7,6},{8,9},{9,8},{10,11... | collective-permute-start | bytes 12296 | tf_op jit(solution)/shard_map/ppermute | solution.py:84

commit v7 on v4

v7 whole, which is shorter than its diff:
```python
import functools
import math
from typing import NamedTuple

import jax
import jax.numpy as jnp
from jax import lax
from jax.experimental import pallas as pl
from jax.experimental.pallas import tpu as pltpu
from jax.sharding import PartitionSpec as P

LANES = 128
QUAD = 4
KEPT_BYTES = 400 << 10


class Plan(NamedTuple):
    high: int
    each: int
    col_tiles: int
    width: int
    pack: int

    @property
    def chips(self):
        return self.width // self.each

    @property
    def sums(self):
        return self.col_tiles * self.high

    @property
    def gram_rows(self):
        return self.chips // 2 // self.pack

    @property
    def gram_cols(self):
        return self.width * self.pack // LANES

    @property
    def grams(self):
        return self.gram_rows * self.gram_cols

    @property
    def tiles(self):
        return self.sums + self.grams

    def blocks(self):
        for q in range(QUAD):
            for h in range(self.high):
                yield q, h, int(q > 0) ^ (h.bit_count() & 1)


def dot(a, b, contract):
    return lax.dot_general(
        a,
        b,
        (contract, ((), ())),
        precision=lax.Precision.HIGHEST,
        preferred_element_type=jnp.float32,
    )


def small(x):
    bytes_each = jnp.dtype(x.dtype).itemsize
    return bytes_each == 2 or math.prod(x.shape) * bytes_each <= KEPT_BYTES


def call(body, outs, name, *args, out_space=pltpu.VMEM, **kwargs):
    args = [a if isinstance(a, tuple) else (a, pltpu.VMEM) for a in args]
    return pl.pallas_call(
        body,
        out_shape=outs,
        in_specs=[pl.BlockSpec(memory_space=space) for _, space in args],
        out_specs=[pl.BlockSpec(memory_space=out_space)] * len(outs),
        name=name,
        **kwargs,
    )(
        *[
            pltpu.with_memory_space_constraint(a, space)
            if space == pltpu.VMEM and small(a)
            else a
            for a, space in args
        ]
    )


def stored(*shape):
    return jax.ShapeDtypeStruct(shape, jnp.float32)


def kept(*shape):
    return pltpu.VMEM(shape, jnp.float32) if small(stored(*shape)) else stored(*shape)


def swap_cores(x):
    return lax.ppermute(x, "row", [(0, 1), (1, 0)])


def partner(x, bits):
    return lax.ppermute(x, "center", [(i, i ^ bits) for i in range(lax.axis_size("center"))])


def across(x, bits):
    pairs = [
        (2 * i + core, 2 * (i ^ bits) + 1 - core)
        for i in range(lax.axis_size("center"))
        for core in range(2)
    ]
    return lax.ppermute(x, ("center", "row"), pairs)


def pick_body(index, dataset, out, index_s, data, sems):
    copies = [
        pltpu.make_async_copy(a, b, sems.at[i])
        for i, (a, b) in enumerate(((index, index_s), (dataset, data)))
    ]
    for c in copies:
        c.start()
    for c in copies:
        c.wait()
    batches, count = index.shape
    for b in range(batches):
        for j in range(count):
            at = b * count + j
            out[at : at + 1] = data[pl.ds(index_s[b, j], 1), :]


def parts(x):
    out = []
    for _ in range(3):
        out.append(x.astype(jnp.bfloat16))
        x = x - out[-1].astype(jnp.float32)
    return out


def parts_dot(left, right, axis):
    n = left[0].shape[0]
    total = 0.0
    for i in (2, 1, 0):
        part = lax.dot_general(
            jnp.concatenate(left[: 3 - i], 0),
            right[i],
            (((1,), (axis,)), ((), ())),
            preferred_element_type=jnp.float32,
        )
        for j in reversed(range(3 - i)):
            total = total + part[j * n : (j + 1) * n]
    return total


def prepare_body(centers, split_out, row_out, held, sem):
    copy = pltpu.make_async_copy(centers, held, sem)
    copy.start()
    copy.wait()
    c = held[...]
    for i, part in enumerate(parts(c)):
        split_out[i] = part
    sq = jnp.sum(c * c, axis=1, keepdims=True)
    row_out[...] = jnp.broadcast_to(sq, (c.shape[0], LANES)).T[: row_out.shape[0]]


def weights_body(mine, theirs, split_out):
    first = lax.axis_index("row") == 0
    a, b = mine[...], theirs[...]
    cols = a.shape[1]
    for side, w in enumerate((jnp.where(first, a, b), jnp.where(first, b, a))):
        for i, part in enumerate(parts(w)):
            split_out[i, :, side * cols : (side + 1) * cols] = part


def block_body(plan, gamma, rows, split, row, weights, *refs):
    *targets, k_out, out = refs
    x = rows[...]
    row_sq = jnp.sum(x * x, axis=1, keepdims=True)
    cross = parts_dot(parts(x), split, 1)
    k = jnp.exp(-gamma[:1] * (row_sq + row[:1] - 2.0 * cross))
    k_out[...] = k
    part = parts_dot(parts(k), weights, 0)
    high = plan.high
    for c in range(plan.col_tiles):
        tile = part[:, c * LANES : (c + 1) * LANES]
        out[c * high : (c + 1) * high] = tile.reshape(high, plan.each, LANES)
    for t in targets:
        wanted = jnp.concatenate([t[b] for b in range(t.shape[0])], 0)
        for c in range(plan.col_tiles):
            out[c * high] = out[c * high] - wanted[:, c * LANES : (c + 1) * LANES]


def by_batch(is_first, mine, theirs):
    first, second = jnp.where(is_first, mine, theirs), jnp.where(is_first, theirs, mine)
    half = mine.shape[0] // 2
    low = lax.broadcasted_iota(jnp.int32, mine.shape, 0) < half
    return (
        jnp.where(low, first, pltpu.roll(second, half, 0)),
        jnp.where(low, pltpu.roll(first, half, 0), second),
    )


def chip_at(q, h):
    return lax.axis_index("center") ^ (QUAD * h + q)


def gram_body(plan, own, swapped, k0_out, k1_out, keep, send):
    each = plan.each
    me = lax.axis_index("row")
    for q, h, crossed in plan.blocks():
        at = (q * plan.high + h) * each
        tile = slice(at, at + each)
        to = pl.ds(pl.multiple_of(chip_at(q, h) * each, each), each)
        k0_out[to], k1_out[to] = by_batch(me == crossed, own[tile], swapped[tile])
    k0 = jnp.concatenate([k0_out[...]] * plan.pack, 0)
    gram = dot(k1_out[...], k0, ((1,), (1,)))
    gram = gram.reshape(plan.chips // 2, 2, each, gram.shape[1])
    even, odd = gram[:, 0], gram[:, 1]
    half = each // 2
    low = lax.broadcasted_iota(jnp.int32, even.shape, 1) < half
    core0 = jnp.where(low, even, pltpu.roll(odd, half, 1))
    core1 = jnp.where(low, pltpu.roll(even, half, 1), odd)
    t = plan.gram_rows
    lane = lax.broadcasted_iota(jnp.int32, (t,) + even.shape[1:], 2)
    sides = []
    for core in (core0, core1):
        packed = core[:t]
        for i in range(1, plan.pack):
            packed = jnp.where(lane >= i * plan.width, core[i * t : (i + 1) * t], packed)
        sides.append(packed)
    first = me == 0
    for out, x in (
        (keep, jnp.where(first, sides[0], sides[1])),
        (send, jnp.where(first, sides[1], sides[0])),
    ):
        for u in range(plan.gram_cols):
            out[u * t : (u + 1) * t] = x[:, :, u * LANES : (u + 1) * LANES]


def quad_body(plan, *refs):
    *sums, gram, out = refs
    total = sums[0][...]
    for other in sums[1:]:
        total = total + other[...]
    out[: plan.sums] = total
    out[plan.sums :] = gram[...]


def high_body(plan, bit, mine, gram, other, out):
    for at in range(0, plan.sums, plan.high):
        for h in range(plan.high):
            out[at + h] = mine[at + h] + other[at + (h ^ bit)]
    out[plan.sums :] = gram[...] + other[plan.sums :]


def solve_body(plan, rate, *refs):
    mine, refs = refs[:QUAD][::-1], refs[QUAD:]
    theirs, refs = refs[:QUAD][::-1], refs[QUAD:]
    k0, k1, weights, weights_out, residual_out, res0, res1, weights_new, residual, sems = refs
    each, high = plan.each, plan.high
    half = each // 2
    me = lax.axis_index("row")
    for q, h, crossed in plan.blocks():
        to = pl.ds(pl.multiple_of(chip_at(q, h) * each, each), each)
        for c in range(plan.col_tiles):
            at = c * high + h
            cols = slice(c * LANES, (c + 1) * LANES)
            res0[to, cols], res1[to, cols] = by_batch(me == crossed, mine[q][at], theirs[q][at])
    grams = lambda packet: packet[plan.sums :]
    here = grams(mine[0]) + grams(theirs[1]) + grams(theirs[2]) + grams(theirs[3])
    there = grams(theirs[0]) + grams(mine[1]) + grams(mine[2]) + grams(mine[3])
    first = me == 0
    t = plan.gram_rows
    rows = []
    for x in (jnp.where(first, here, there), jnp.where(first, there, here)):
        x = jnp.concatenate([x[u * t : (u + 1) * t] for u in range(plan.gram_cols)], 2)
        lane = lax.broadcasted_iota(jnp.int32, x.shape, 2) // plan.width
        rows += [jnp.where(lane == i, x, 0.0) for i in range(plan.pack)]
    gram = jnp.concatenate(rows, 0)
    gram = gram.reshape(-1, gram.shape[2])
    step = dot(gram, jnp.concatenate([res0[...]] * plan.pack, 0), ((1,), (0,))) * rate
    core0, core1 = (
        x.reshape(plan.chips // 2, each, -1) for x in (step[: plan.width // 2], step[plan.width // 2 :])
    )
    low = lax.broadcasted_iota(jnp.int32, core0.shape, 1) < half
    even = jnp.where(low, core0, pltpu.roll(core1, half, 1))
    odd = jnp.where(low, pltpu.roll(core0, half, 1), core1)
    res1[...] = res1[...] - jnp.stack([even, odd], 1).reshape(res1.shape)
    tile = res1[pl.ds(pl.multiple_of(lax.axis_index("center") * each, each), each), :]
    residual[...] = jnp.where(first, tile[:half], tile[half:])
    copies = [
        pltpu.make_async_copy(a, b, sems.at[i])
        for i, (a, b) in enumerate(((residual, residual_out), (weights_new, weights_out)))
    ]
    copies[0].start()
    cols = weights.shape[1]
    side = lambda x: jnp.where(first, x[:, :cols], x[:, cols:])
    grad = dot(k0[...], side(res0[...]), ((0,), (0,))) + dot(
        k1[...], side(res1[...]), ((0,), (0,))
    )
    weights_new[...] = weights[...] - rate * grad
    copies[1].start()
    for c in copies:
        c.wait()


def per_device(dataset, centers, weights, batch_index, targets, gamma):
    shards = lax.axis_size("center")
    cores = lax.axis_size("row")
    batches, rows_here = batch_index.shape
    assert cores == 2 and batches == 2 and shards % QUAD == 0 and shards & (shards - 1) == 0
    features = dataset.shape[1]
    count, cols = weights.shape
    each = batches * rows_here
    high = shards // QUAD
    span = high * each
    n = shards * each
    width = shards * cores * rows_here
    rate = 0.5 / width
    plan = Plan(high, each, 2 * cols // LANES, width, max(1, LANES // width))
    quad = range(1, QUAD)
    bits = [1 << i for i in range(high.bit_length() - 1)]

    (local,) = call(
        pick_body,
        [kept(each, features)],
        "pick",
        (batch_index, pl.ANY),
        (dataset, pl.ANY),
        scratch_shapes=[
            pltpu.SMEM(batch_index.shape, jnp.int32),
            pltpu.VMEM(dataset.shape, jnp.float32),
            pltpu.SemaphoreType.DMA((2,)),
        ],
    )
    split, row = call(
        prepare_body,
        [pltpu.VMEM((3, count, features), jnp.bfloat16), kept(8, count)],
        "prepare",
        (centers, pl.ANY),
        scratch_shapes=[pltpu.VMEM(centers.shape, jnp.float32), pltpu.SemaphoreType.DMA],
    )
    spread = jnp.broadcast_to(gamma, (8, count))
    (weight_split,) = call(
        weights_body,
        [pltpu.VMEM((3, count, 2 * cols), jnp.bfloat16)],
        "weights",
        weights,
        swap_cores(weights),
    )
    rows = local
    for bit in bits:
        rows = jnp.concatenate([rows, across(rows, QUAD * bit)], 0)
    own, packets = [], []
    for q, x in enumerate([rows] + [across(rows, q) for q in quad]):
        k, packet = call(
            functools.partial(block_body, plan),
            [kept(span, count), kept(plan.sums, each, LANES)],
            "block",
            spread,
            x,
            split,
            row,
            weight_split,
            *([targets] if q == 0 else []),
        )
        own.append(k)
        packets.append(packet)
    sums = [across(packets[q], q) for q in reversed(quad)]
    own = jnp.concatenate(own, 0)
    k0, k1, gram, gram_sent = call(
        functools.partial(gram_body, plan),
        [kept(n, count)] * 2 + [kept(plan.grams, each, LANES)] * 2,
        "gram",
        own,
        swap_cores(own),
    )
    shape = kept(plan.tiles, each, LANES)
    (total,) = call(
        functools.partial(quad_body, plan), [shape], "quad", packets[0], *sums, gram_sent
    )
    for i, bit in enumerate(bits):
        if i == 0:
            other = across(total, QUAD * bit)
        else:
            gram = total[plan.sums :]
            other = jnp.concatenate(
                [across(total[: plan.sums], QUAD * bit), partner(gram, QUAD * bit)], 0
            )
        (total,) = call(
            functools.partial(high_body, plan, bit), [shape], "high", total, gram, other
        )
    mine = [across(total, q) for q in reversed(quad)] + [total]
    new_weights, residual = call(
        functools.partial(solve_body, plan, rate),
        [stored(count, cols), stored(rows_here, 2 * cols)],
        "solve",
        *mine,
        *[swap_cores(x) for x in mine],
        k0,
        k1,
        weights,
        out_space=pl.ANY,
        scratch_shapes=[
            pltpu.VMEM((width, 2 * cols), jnp.float32),
            pltpu.VMEM((width, 2 * cols), jnp.float32),
            pltpu.VMEM((count, cols), jnp.float32),
            pltpu.VMEM((rows_here, 2 * cols), jnp.float32),
            pltpu.SemaphoreType.DMA((2,)),
        ],
    )
    return (new_weights, residual)


def solution(mesh):
    return jax.shard_map(
        per_device,
        mesh=mesh,
        in_specs=(
            P(("groups", "center", "row"), None),
            P(("groups", "center"), None),
            P(("groups", "center"), "row"),
            P(None, ("groups", "center", "row")),
            P(None, ("groups", "center", "row"), None),
            P("groups"),
        ),
        out_specs=(P(("groups", "center"), "row"), P(("groups", "center", "row"), None)),
        check_vma=False,
    )
```

time: 38.9 us -> 36.6 us (0.941)
  waiting for transfers between devices: 11.8 us -> 7.37 us
  starting transfers between devices: 18.2 us -> 20.6 us
  Pallas kernels: 6.9 us -> 6.36 us
    ppermute x10 -> x11, starting transfers between devices: 13.6 us -> 18.1 us  [across(): return lax.ppermute(x, ('center', 'row'), pairs)]
    ppermute x1 -> x0, starting transfers between devices: 3.63 us -> none  [partner(): lax.ppermute(x, 'center', [(i, i ^ bits) for i in range(lax.axis_size('ce...]
    ppermute x1 -> x0, waiting for transfers between devices: 2.5 us -> none  [partner(): lax.ppermute(x, 'center', [(i, i ^ bits) for i in range(lax.axis_size('ce...]
    ppermute x10 -> x11, waiting for transfers between devices: 8.39 us -> 6.35 us  [across(): return lax.ppermute(x, ('center', 'row'), pairs)]
    ppermute x5 -> x6, starting transfers between devices: 0.95 us -> 2.54 us  [swap_cores(): return lax.ppermute(x, 'row', [(0, 1), (1, 0)])]
    pallas_call x12 -> x11, Pallas kernels: 6.9 us -> 6.36 us  [call(): pl.pallas_call(body, out_shape=outs, in_specs=[pl.BlockSpec(memory_space=...]
    ppermute x5 -> x6, waiting for transfers between devices: 0.87 us -> 1.01 us  [swap_cores(): return lax.ppermute(x, 'row', [(0, 1), (1, 0)])]
  transfers between devices with their start and end apart: 16 -> 17, of which waited for: 10 -> 9; matrix products, arithmetic and copies ran while one was open for 0% -> 0% of each run, Pallas kernels for 11% -> 11%
where the time goes in v7:
time: 36.6 us; the launch traced here: 36.3 us
  starting transfers between devices  20.6 us (56%)
  waiting for transfers between devices  7.37 us (20%)
  Pallas kernels  6.36 us (17%)
  between operations  1.37 us (4%)
  local copies, waits for them, and re-layouts  0.64 us (2%)
    ppermute x11, starting transfers between devices, across(): return lax.ppermute(x, ('center', 'row'), pairs)  18.1 us
    pallas_call x11, Pallas kernels, call(): pl.pallas_call(body, out_shape=outs, in_specs=[pl.BlockSpec(memory_space=...  6.36 us
    ppermute x11, waiting for transfers between devices, across(): return lax.ppermute(x, ('center', 'row'), pairs)  6.35 us
    ppermute x6, starting transfers between devices, swap_cores(): return lax.ppermute(x, 'row', [(0, 1), (1, 0)])  2.54 us
    ppermute x6, waiting for transfers between devices, swap_cores(): return lax.ppermute(x, 'row', [(0, 1), (1, 0)])  1.01 us
  transfers between devices with their start and end apart: 17, of which 9 were waited for; matrix products, arithmetic and copies ran while one was open for 0% of the time, Pallas kernels for 11%

profile of v7, /device:TPU:0, one launch (start us, length us, event | category | flops | bytes accessed | tf_op | source)
XLA Modules:
  0.0 36.3 jit_solution(930709521935389360)
XLA Ops:
  0.6 0.9 %pick.1 = f32[8,1024]{1,0:T(8,128)S(1)} custom-call(s32[2,4]{1,0:T(2,128)} %index.1, f32[16,1024]{1,0:T(8,128)} %dataset.1), custom_call_target="tpu_custom_call" | custom-call | tf_op jit(solution)/shard_map/pick/pallas_call | solution.py:71
  1.5 3.6 %collective-permute-start = (f32[8,1024]{1,0:T(8,128)S(1)}, f32[8,1024]{1,0:T(8,128)S(1)}, u32[]{:S(2)}, u32[]{:S(2)}) collective-permute-start(f32[8,1024]{1,0:T(8,128)S(1)} %pick.1), channel_id=1, source_target_pairs={{0,9},{1,8},{2,11},{3,10},{4,13},{5,12},{6,15},{7,14},{8,1},{9,0},... | collective-permute-start | bytes 98312 | tf_op jit(solution)/shard_map/ppermute | solution.py:110
  5.1 0.7 %collective-permute-start.1 = (f32[128,256]{1,0:T(8,128)}, f32[128,256]{1,0:T(8,128)S(1)}, u32[]{:S(2)}, u32[]{:S(2)}) collective-permute-start(f32[128,256]{1,0:T(8,128)} %refs_10_.1), channel_id=1, source_target_pairs={{0,1},{1,0},{2,3},{3,2},{4,5},{5,4},{6,7},{7,6},{8,9},{9,8},{10,11... | collective-permute-start | bytes 393224 | tf_op jit(solution)/shard_map/ppermute | solution.py:97
  5.8 1.1 %collective-permute-done = f32[8,1024]{1,0:T(8,128)S(1)} collective-permute-done((f32[8,1024]{1,0:T(8,128)S(1)}, f32[8,1024]{1,0:T(8,128)S(1)}, u32[]{:S(2)}, u32[]{:S(2)}) %collective-permute-start) | collective-permute-done | bytes 32800 | tf_op jit(solution)/shard_map/ppermute | solution.py:110
  6.9 2.8 %collective-permute-start.2 = (f32[16,1024]{1,0:T(8,128)S(1)}, f32[16,1024]{1,0:T(8,128)S(1)}, u32[]{:S(2)}, u32[]{:S(2)}) collective-permute-start(f32[16,1024]{1,0:T(8,128)S(1)} %pad_maximum_fusion.rows), channel_id=1, source_target_pairs={{0,7},{1,6},{2,5},{3,4},{4,3},{5,2},{6,1},{7,0},{8,15},{9,14},{10,... | collective-permute-start | bytes 196616 | tf_op jit(solution)/shard_map/ppermute | solution.py:110
  10.3 0.0 copy-start
  10.3 1.4 %prepare.1 = (bf16[3,128,1024]{2,1,0:T(8,128)(2,1)S(1)}, f32[8,128]{1,0:T(8,128)S(1)}) custom-call(f32[128,1024]{1,0:T(8,128)} %centers.1), custom_call_target="tpu_custom_call" | custom-call | tf_op jit(solution)/shard_map/prepare/pallas_call | solution.py:71
  11.7 0.5 %collective-permute-start.4 = (f32[16,1024]{1,0:T(8,128)S(1)}, f32[16,1024]{1,0:T(8,128)S(1)}, u32[]{:S(2)}, u32[]{:S(2)}) collective-permute-start(f32[16,1024]{1,0:T(8,128)S(1)} %pad_maximum_fusion.rows), channel_id=1, source_target_pairs={{0,5},{1,4},{2,7},{3,6},{4,1},{5,0},{6,3},{7,2},{8,13},{9,12},{10,... | collective-permute-start | bytes 196616 | tf_op jit(solution)/shard_map/ppermute | solution.py:110
  12.2 0.2 collective-permute-start.6
  12.3 0.0 collective-permute-done.1.theirs
  12.3 0.0 copy-done
  12.3 0.0 copy-start.1
  12.3 0.1 weights.1
  12.4 0.6 %copy-done.1 = f32[2,4,512]{2,1,0:T(4,128)S(1)} copy-done((f32[2,4,512]{2,1,0:T(4,128)S(1)}, f32[2,4,512]{2,1,0:T(4,128)}, u32[]{:S(2)}) %copy-start.1) | copy-done | bytes 16408
  13.1 0.6 %block.4 = (f32[16,128]{1,0:T(8,128)S(1)}, f32[8,8,128]{2,1,0:T(8,128)S(1)}) custom-call(f32[8,128]{1,0:T(8,128)S(1)} %broadcast_in_dim.2.gamma, f32[16,1024]{1,0:T(8,128)S(1)} %pad_maximum_fusion.rows, bf16[3,128,1024]{2,1,0:T(8,128)(2,1)S(1)} %get-tuple-element.16.split, f32[8,128]{1,0:T(8,128)S(1)} %get-tuple-element.17.row, ...), custom_call_target="tpu_custom_call" | custom-call | tf_op jit(solution)/shard_map/block/pallas_call | solution.py:71
  13.7 0.0 collective-permute-done.2.rows
  13.7 0.6 %block.5 = (f32[16,128]{1,0:T(8,128)S(1)}, f32[8,8,128]{2,1,0:T(8,128)S(1)}) custom-call(f32[8,128]{1,0:T(8,128)S(1)} %broadcast_in_dim.2.gamma, f32[16,1024]{1,0:T(8,128)S(1)} %collective-permute-done.2.rows, bf16[3,128,1024]{2,1,0:T(8,128)(2,1)S(1)} %get-tuple-element.16.split, f32[8,128]{1,0:T(8,128)S(1)} %get-tuple-element.17.row, ...), custom_call_target="tpu_custom_call" | custom-call | tf_op jit(solution)/shard_map/block/pallas_call | solution.py:71
  14.3 2.6 %collective-permute-start.3 = (f32[8,8,128]{2,1,0:T(8,128)S(1)}, f32[8,8,128]{2,1,0:T(8,128)S(1)}, u32[]{:S(2)}, u32[]{:S(2)}) collective-permute-start(f32[8,8,128]{2,1,0:T(8,128)S(1)} %get-tuple-element.19), channel_id=1, source_target_pairs={{0,7},{1,6},{2,5},{3,4},{4,3},{5,2},{6,1},{7,0},{8,15},{9,14},{10,... | collective-permute-start | bytes 98312 | tf_op jit(solution)/shard_map/ppermute | solution.py:110
  16.9 0.0 collective-permute-done.6.rows
  16.9 0.6 %block.7 = (f32[16,128]{1,0:T(8,128)S(1)}, f32[8,8,128]{2,1,0:T(8,128)S(1)}) custom-call(f32[8,128]{1,0:T(8,128)S(1)} %broadcast_in_dim.2.gamma, f32[16,1024]{1,0:T(8,128)S(1)} %collective-permute-done.6.rows, bf16[3,128,1024]{2,1,0:T(8,128)(2,1)S(1)} %get-tuple-element.16.split, f32[8,128]{1,0:T(8,128)S(1)} %get-tuple-element.17.row, ...), custom_call_target="tpu_custom_call" | custom-call | tf_op jit(solution)/shard_map/block/pallas_call | solution.py:71
  17.5 0.0 collective-permute-done.4.rows
  17.5 0.6 %block.6 = (f32[16,128]{1,0:T(8,128)S(1)}, f32[8,8,128]{2,1,0:T(8,128)S(1)}) custom-call(f32[8,128]{1,0:T(8,128)S(1)} %broadcast_in_dim.2.gamma, f32[16,1024]{1,0:T(8,128)S(1)} %collective-permute-done.4.rows, bf16[3,128,1024]{2,1,0:T(8,128)(2,1)S(1)} %get-tuple-element.16.split, f32[8,128]{1,0:T(8,128)S(1)} %get-tuple-element.17.row, ...), custom_call_target="tpu_custom_call" | custom-call | tf_op jit(solution)/shard_map/block/pallas_call | solution.py:71
  18.2 0.2 collective-permute-start.8
  18.4 0.9 %collective-permute-start.5 = (f32[8,8,128]{2,1,0:T(8,128)S(1)}, f32[8,8,128]{2,1,0:T(8,128)S(1)}, u32[]{:S(2)}, u32[]{:S(2)}) collective-permute-start(f32[8,8,128]{2,1,0:T(8,128)S(1)} %get-tuple-element.20), channel_id=1, source_target_pairs={{0,5},{1,4},{2,7},{3,6},{4,1},{5,0},{6,3},{7,2},{8,13},{9,12},{10,... | collective-permute-start | bytes 98312 | tf_op jit(solution)/shard_map/ppermute | solution.py:110
  19.3 0.3 collective-permute-start.7
  19.5 0.0 collective-permute-done.8.swapped
  19.5 0.3 gram.1
  19.8 0.0 collective-permute-done.3.refs_1_
  19.8 1.9 %collective-permute-done.5.refs_2_ = f32[8,8,128]{2,1,0:T(8,128)S(1)} collective-permute-done((f32[8,8,128]{2,1,0:T(8,128)S(1)}, f32[8,8,128]{2,1,0:T(8,128)S(1)}, u32[]{:S(2)}, u32[]{:S(2)}) %collective-permute-start.5) | collective-permute-done | bytes 32800 | tf_op jit(solution)/shard_map/ppermute | solution.py:110
  21.7 1.0 %collective-permute-done.7.refs_3_ = f32[8,8,128]{2,1,0:T(8,128)S(1)} collective-permute-done((f32[8,8,128]{2,1,0:T(8,128)S(1)}, f32[8,8,128]{2,1,0:T(8,128)S(1)}, u32[]{:S(2)}, u32[]{:S(2)}) %collective-permute-start.7) | collective-permute-done | bytes 32800 | tf_op jit(solution)/shard_map/ppermute | solution.py:110
  22.7 3.2 %collective-permute-start.9 = (f32[10,8,128]{2,1,0:T(8,128)S(1)}, f32[10,8,128]{2,1,0:T(8,128)S(1)}, u32[]{:S(2)}, u32[]{:S(2)}) collective-permute-start(f32[10,8,128]{2,1,0:T(8,128)S(1)} %quad.1.mine), channel_id=1, source_target_pairs={{0,9},{1,8},{2,11},{3,10},{4,13},{5,12},{6,15},{7,14},{8,1},{9,0},... | collective-permute-start | bytes 122888 | tf_op jit(solution)/shard_map/ppermute | solution.py:110
  25.9 1.7 %collective-permute-done.9.other = f32[10,8,128]{2,1,0:T(8,128)S(1)} collective-permute-done((f32[10,8,128]{2,1,0:T(8,128)S(1)}, f32[10,8,128]{2,1,0:T(8,128)S(1)}, u32[]{:S(2)}, u32[]{:S(2)}) %collective-permute-start.9) | collective-permute-done | bytes 40992 | tf_op jit(solution)/shard_map/ppermute | solution.py:110
  27.6 1.1 %collective-permute-start.10 = (f32[10,8,128]{2,1,0:T(8,128)S(1)}, f32[10,8,128]{2,1,0:T(8,128)S(1)}, u32[]{:S(2)}, u32[]{:S(2)}) collective-permute-start(f32[10,8,128]{2,1,0:T(8,128)S(1)} %high.1.refs_3_), channel_id=1, source_target_pairs={{0,7},{1,6},{2,5},{3,4},{4,3},{5,2},{6,1},{7,0},{8,15},{9,14},{10,... | collective-permute-start | bytes 122888 | tf_op jit(solution)/shard_map/ppermute | solution.py:110
  28.7 0.6 %collective-permute-start.11 = (f32[10,8,128]{2,1,0:T(8,128)S(1)}, f32[10,8,128]{2,1,0:T(8,128)S(1)}, u32[]{:S(2)}, u32[]{:S(2)}) collective-permute-start(f32[10,8,128]{2,1,0:T(8,128)S(1)} %high.1.refs_3_), channel_id=1, source_target_pairs={{0,5},{1,4},{2,7},{3,6},{4,1},{5,0},{6,3},{7,2},{8,13},{9,12},{10,... | collective-permute-start | bytes 122888 | tf_op jit(solution)/shard_map/ppermute | solution.py:110
  29.3 2.3 %collective-permute-start.12 = (f32[10,8,128]{2,1,0:T(8,128)S(1)}, f32[10,8,128]{2,1,0:T(8,128)S(1)}, u32[]{:S(2)}, u32[]{:S(2)}) collective-permute-start(f32[10,8,128]{2,1,0:T(8,128)S(1)} %high.1.refs_3_), channel_id=1, source_target_pairs={{0,3},{1,2},{2,1},{3,0},{4,7},{5,6},{6,5},{7,4},{8,11},{9,10},{10,... | collective-permute-start | bytes 122888 | tf_op jit(solution)/shard_map/ppermute | solution.py:110
  31.6 0.0 collective-permute-start.16
  31.6 0.3 collective-permute-done.10.refs_0_
  31.9 1.5 %collective-permute-start.13 = (f32[10,8,128]{2,1,0:T(8,128)S(1)}, f32[10,8,128]{2,1,0:T(8,128)S(1)}, u32[]{:S(2)}, u32[]{:S(2)}) collective-permute-start(f32[10,8,128]{2,1,0:T(8,128)S(1)} %collective-permute-done.10.refs_0_), channel_id=1, source_target_pairs={{0,1},{1,0},{2,3},{3,2},{4,5},{5,4},{6,7},{7,6},{8,9},{9,8},{10,11... | collective-permute-start | bytes 122888 | tf_op jit(solution)/shard_map/ppermute | solution.py:97
  33.4 0.0 collective-permute-done.11.refs_1_
  33.4 0.0 collective-permute-start.14
  33.4 0.4 %collective-permute-done.12.refs_2_ = f32[10,8,128]{2,1,0:T(8,128)S(1)} collective-permute-done((f32[10,8,128]{2,1,0:T(8,128)S(1)}, f32[10,8,128]{2,1,0:T(8,128)S(1)}, u32[]{:S(2)}, u32[]{:S(2)}) %collective-permute-start.12) | collective-permute-done | bytes 40992 | tf_op jit(solution)/shard_map/ppermute | solution.py:110
  33.8 0.2 collective-permute-start.15
  34.0 0.0 collective-permute-done.16.refs_7_
  34.0 0.2 collective-permute-done.13.refs_4_
  34.3 0.4 collective-permute-done.14.refs_5_
  34.6 0.4 %collective-permute-done.15.refs_6_ = f32[10,8,128]{2,1,0:T(8,128)S(1)} collective-permute-done((f32[10,8,128]{2,1,0:T(8,128)S(1)}, f32[10,8,128]{2,1,0:T(8,128)S(1)}, u32[]{:S(2)}, u32[]{:S(2)}) %collective-permute-start.15) | collective-permute-done | bytes 40992 | tf_op jit(solution)/shard_map/ppermute | solution.py:97
  35.0 1.3 %solve.1 = (f32[128,256]{1,0:T(8,128)}, f32[4,512]{1,0:T(4,128)}) custom-call(f32[10,8,128]{2,1,0:T(8,128)S(1)} %collective-permute-done.10.refs_0_, f32[10,8,128]{2,1,0:T(8,128)S(1)} %collective-permute-done.11.refs_1_, f32[10,8,128]{2,1,0:T(8,128)S(1)} %collective-permute-done.12.refs_2_, f32[10,8,128]{2,1,0:T(8,128)S(1)} %high.1.refs_3_, ...), custom_call_target="tpu_custom_call" | custom-call | tf_op jit(solution)/shard_map/solve/pallas_call | solution.py:71
  (8 shorter events, 0.0 us)
Async XLA Ops:
  1.5 5.4 %collective-permute-start = (f32[8,1024]{1,0:T(8,128)S(1)}, f32[8,1024]{1,0:T(8,128)S(1)}, u32[]{:S(2)}, u32[]{:S(2)}) collective-permute-start(f32[8,1024]{1,0:T(8,128)S(1)} %pick.1), channel_id=1, source_target_pairs={{0,9},{1,8},{2,11},{3,10},{4,13},{5,12},{6,15},{7,14},{8,1},{9,0},... | collective-permute-start | bytes 98312 | tf_op jit(solution)/shard_map/ppermute | solution.py:110
  5.1 7.3 %collective-permute-start.1 = (f32[128,256]{1,0:T(8,128)}, f32[128,256]{1,0:T(8,128)S(1)}, u32[]{:S(2)}, u32[]{:S(2)}) collective-permute-start(f32[128,256]{1,0:T(8,128)} %refs_10_.1), channel_id=1, source_target_pairs={{0,1},{1,0},{2,3},{3,2},{4,5},{5,4},{6,7},{7,6},{8,9},{9,8},{10,11... | collective-permute-start | bytes 393224 | tf_op jit(solution)/shard_map/ppermute | solution.py:97
  6.9 6.8 %collective-permute-start.2 = (f32[16,1024]{1,0:T(8,128)S(1)}, f32[16,1024]{1,0:T(8,128)S(1)}, u32[]{:S(2)}, u32[]{:S(2)}) collective-permute-start(f32[16,1024]{1,0:T(8,128)S(1)} %pad_maximum_fusion.rows), channel_id=1, source_target_pairs={{0,7},{1,6},{2,5},{3,4},{4,3},{5,2},{6,1},{7,0},{8,15},{9,14},{10,... | collective-permute-start | bytes 196616 | tf_op jit(solution)/shard_map/ppermute | solution.py:110
  10.3 2.1 %copy-start = (f32[128,256]{1,0:T(8,128)S(1)}, f32[128,256]{1,0:T(8,128)}, u32[]{:S(2)}) copy-start(f32[128,256]{1,0:T(8,128)} %refs_10_.1) | copy-start | bytes 393220
  11.7 5.9 %collective-permute-start.4 = (f32[16,1024]{1,0:T(8,128)S(1)}, f32[16,1024]{1,0:T(8,128)S(1)}, u32[]{:S(2)}, u32[]{:S(2)}) collective-permute-start(f32[16,1024]{1,0:T(8,128)S(1)} %pad_maximum_fusion.rows), channel_id=1, source_target_pairs={{0,5},{1,4},{2,7},{3,6},{4,1},{5,0},{6,3},{7,2},{8,13},{9,12},{10,... | collective-permute-start | bytes 196616 | tf_op jit(solution)/shard_map/ppermute | solution.py:110
  12.2 4.8 %collective-permute-start.6 = (f32[16,1024]{1,0:T(8,128)S(1)}, f32[16,1024]{1,0:T(8,128)S(1)}, u32[]{:S(2)}, u32[]{:S(2)}) collective-permute-start(f32[16,1024]{1,0:T(8,128)S(1)} %pad_maximum_fusion.rows), channel_id=1, source_target_pairs={{0,3},{1,2},{2,1},{3,0},{4,7},{5,6},{6,5},{7,4},{8,11},{9,10},{10,... | collective-permute-start | bytes 196616 | tf_op jit(solution)/shard_map/ppermute | solution.py:110
  12.3 0.7 %copy-start.1 = (f32[2,4,512]{2,1,0:T(4,128)S(1)}, f32[2,4,512]{2,1,0:T(4,128)}, u32[]{:S(2)}) copy-start(f32[2,4,512]{2,1,0:T(4,128)} %refs_0_.1) | copy-start | bytes 49156
  14.3 5.5 %collective-permute-start.3 = (f32[8,8,128]{2,1,0:T(8,128)S(1)}, f32[8,8,128]{2,1,0:T(8,128)S(1)}, u32[]{:S(2)}, u32[]{:S(2)}) collective-permute-start(f32[8,8,128]{2,1,0:T(8,128)S(1)} %get-tuple-element.19), channel_id=1, source_target_pairs={{0,7},{1,6},{2,5},{3,4},{4,3},{5,2},{6,1},{7,0},{8,15},{9,14},{10,... | collective-permute-start | bytes 98312 | tf_op jit(solution)/shard_map/ppermute | solution.py:110
  18.2 1.4 %collective-permute-start.8 = (f32[64,128]{1,0:T(8,128)S(1)}, f32[64,128]{1,0:T(8,128)S(1)}, u32[]{:S(2)}, u32[]{:S(2)}) collective-permute-start(f32[64,128]{1,0:T(8,128)S(1)} %constant_dynamic-update-slice_fusion.own), channel_id=1, source_target_pairs={{0,1},{1,0},{2,3},{3,2},{4,5},{5,4},{6,7},{7,6},{8,9},{9,8},{10,11... | collective-permute-start | bytes 98312 | tf_op jit(solution)/shard_map/ppermute | solution.py:97
  18.4 3.3 %collective-permute-start.5 = (f32[8,8,128]{2,1,0:T(8,128)S(1)}, f32[8,8,128]{2,1,0:T(8,128)S(1)}, u32[]{:S(2)}, u32[]{:S(2)}) collective-permute-start(f32[8,8,128]{2,1,0:T(8,128)S(1)} %get-tuple-element.20), channel_id=1, source_target_pairs={{0,5},{1,4},{2,7},{3,6},{4,1},{5,0},{6,3},{7,2},{8,13},{9,12},{10,... | collective-permute-start | bytes 98312 | tf_op jit(solution)/shard_map/ppermute | solution.py:110
  19.3 3.4 %collective-permute-start.7 = (f32[8,8,128]{2,1,0:T(8,128)S(1)}, f32[8,8,128]{2,1,0:T(8,128)S(1)}, u32[]{:S(2)}, u32[]{:S(2)}) collective-permute-start(f32[8,8,128]{2,1,0:T(8,128)S(1)} %get-tuple-element.21), channel_id=1, source_target_pairs={{0,3},{1,2},{2,1},{3,0},{4,7},{5,6},{6,5},{7,4},{8,11},{9,10},{10,... | collective-permute-start | bytes 98312 | tf_op jit(solution)/shard_map/ppermute | solution.py:110
  22.7 4.9 %collective-permute-start.9 = (f32[10,8,128]{2,1,0:T(8,128)S(1)}, f32[10,8,128]{2,1,0:T(8,128)S(1)}, u32[]{:S(2)}, u32[]{:S(2)}) collective-permute-start(f32[10,8,128]{2,1,0:T(8,128)S(1)} %quad.1.mine), channel_id=1, source_target_pairs={{0,9},{1,8},{2,11},{3,10},{4,13},{5,12},{6,15},{7,14},{8,1},{9,0},... | collective-permute-start | bytes 122888 | tf_op jit(solution)/shard_map/ppermute | solution.py:110
  27.6 4.3 %collective-permute-start.10 = (f32[10,8,128]{2,1,0:T(8,128)S(1)}, f32[10,8,128]{2,1,0:T(8,128)S(1)}, u32[]{:S(2)}, u32[]{:S(2)}) collective-permute-start(f32[10,8,128]{2,1,0:T(8,128)S(1)} %high.1.refs_3_), channel_id=1, source_target_pairs={{0,7},{1,6},{2,5},{3,4},{4,3},{5,2},{6,1},{7,0},{8,15},{9,14},{10,... | collective-permute-start | bytes 122888 | tf_op jit(solution)/shard_map/ppermute | solution.py:110
  28.7 4.7 %collective-permute-start.11 = (f32[10,8,128]{2,1,0:T(8,128)S(1)}, f32[10,8,128]{2,1,0:T(8,128)S(1)}, u32[]{:S(2)}, u32[]{:S(2)}) collective-permute-start(f32[10,8,128]{2,1,0:T(8,128)S(1)} %high.1.refs_3_), channel_id=1, source_target_pairs={{0,5},{1,4},{2,7},{3,6},{4,1},{5,0},{6,3},{7,2},{8,13},{9,12},{10,... | collective-permute-start | bytes 122888 | tf_op jit(solution)/shard_map/ppermute | solution.py:110
  29.3 4.5 %collective-permute-start.12 = (f32[10,8,128]{2,1,0:T(8,128)S(1)}, f32[10,8,128]{2,1,0:T(8,128)S(1)}, u32[]{:S(2)}, u32[]{:S(2)}) collective-permute-start(f32[10,8,128]{2,1,0:T(8,128)S(1)} %high.1.refs_3_), channel_id=1, source_target_pairs={{0,3},{1,2},{2,1},{3,0},{4,7},{5,6},{6,5},{7,4},{8,11},{9,10},{10,... | collective-permute-start | bytes 122888 | tf_op jit(solution)/shard_map/ppermute | solution.py:110
  31.6 2.4 %collective-permute-start.16 = (f32[10,8,128]{2,1,0:T(8,128)S(1)}, f32[10,8,128]{2,1,0:T(8,128)S(1)}, u32[]{:S(2)}, u32[]{:S(2)}) collective-permute-start(f32[10,8,128]{2,1,0:T(8,128)S(1)} %high.1.refs_3_), channel_id=1, source_target_pairs={{0,1},{1,0},{2,3},{3,2},{4,5},{5,4},{6,7},{7,6},{8,9},{9,8},{10,11... | collective-permute-start | bytes 122888 | tf_op jit(solution)/shard_map/ppermute | solution.py:97
  31.9 2.3 %collective-permute-start.13 = (f32[10,8,128]{2,1,0:T(8,128)S(1)}, f32[10,8,128]{2,1,0:T(8,128)S(1)}, u32[]{:S(2)}, u32[]{:S(2)}) collective-permute-start(f32[10,8,128]{2,1,0:T(8,128)S(1)} %collective-permute-done.10.refs_0_), channel_id=1, source_target_pairs={{0,1},{1,0},{2,3},{3,2},{4,5},{5,4},{6,7},{7,6},{8,9},{9,8},{10,11... | collective-permute-start | bytes 122888 | tf_op jit(solution)/shard_map/ppermute | solution.py:97
  33.4 1.2 %collective-permute-start.14 = (f32[10,8,128]{2,1,0:T(8,128)S(1)}, f32[10,8,128]{2,1,0:T(8,128)S(1)}, u32[]{:S(2)}, u32[]{:S(2)}) collective-permute-start(f32[10,8,128]{2,1,0:T(8,128)S(1)} %collective-permute-done.11.refs_1_), channel_id=1, source_target_pairs={{0,1},{1,0},{2,3},{3,2},{4,5},{5,4},{6,7},{7,6},{8,9},{9,8},{10,11... | collective-permute-start | bytes 122888 | tf_op jit(solution)/shard_map/ppermute | solution.py:97
  33.8 1.2 %collective-permute-start.15 = (f32[10,8,128]{2,1,0:T(8,128)S(1)}, f32[10,8,128]{2,1,0:T(8,128)S(1)}, u32[]{:S(2)}, u32[]{:S(2)}) collective-permute-start(f32[10,8,128]{2,1,0:T(8,128)S(1)} %collective-permute-done.12.refs_2_), channel_id=1, source_target_pairs={{0,1},{1,0},{2,3},{3,2},{4,5},{5,4},{6,7},{7,6},{8,9},{9,8},{10,11... | collective-permute-start | bytes 122888 | tf_op jit(solution)/shard_map/ppermute | solution.py:97

commit v8 on v7

--- a/solution.py
+++ b/solution.py
@@ -8,6 +8,7 @@
 from jax.experimental import pallas as pl
 from jax.experimental.pallas import tpu as pltpu
 from jax.sharding import PartitionSpec as P
+
 
 LANES = 128
 QUAD = 4
@@ -66,14 +67,13 @@
     return bytes_each == 2 or math.prod(x.shape) * bytes_each <= KEPT_BYTES
 
 
-def call(body, outs, name, *args, out_space=pltpu.VMEM, **kwargs):
+def call(body, outs, *args, out_space=pltpu.VMEM, **kwargs):
     args = [a if isinstance(a, tuple) else (a, pltpu.VMEM) for a in args]
     return pl.pallas_call(
         body,
         out_shape=outs,
         in_specs=[pl.BlockSpec(memory_space=space) for _, space in args],
         out_specs=[pl.BlockSpec(memory_space=out_space)] * len(outs),
-        name=name,
         **kwargs,
     )(
         *[
@@ -169,22 +169,28 @@
             split_out[i, :, side * cols : (side + 1) * cols] = part
 
 
-def block_body(plan, gamma, rows, split, row, weights, *refs):
-    *targets, k_out, out = refs
-    x = rows[...]
+def block_body(plan, members, gamma, split, row, weights, *refs):
+    rows, refs = refs[:members], refs[members:]
+    targets, outs = refs[: -2 * members], refs[-2 * members :]
+    x = jnp.concatenate([r[...] for r in rows], 0)
     row_sq = jnp.sum(x * x, axis=1, keepdims=True)
     cross = parts_dot(parts(x), split, 1)
     k = jnp.exp(-gamma[:1] * (row_sq + row[:1] - 2.0 * cross))
-    k_out[...] = k
     part = parts_dot(parts(k), weights, 0)
     high = plan.high
-    for c in range(plan.col_tiles):
-        tile = part[:, c * LANES : (c + 1) * LANES]
-        out[c * high : (c + 1) * high] = tile.reshape(high, plan.each, LANES)
+    span = high * plan.each
+    for i in range(members):
+        k_out, out = outs[i], outs[members + i]
+        k_out[...] = k[i * span : (i + 1) * span]
+        for c in range(plan.col_tiles):
+            tile = part[i * span : (i + 1) * span, c * LANES : (c + 1) * LANES]
+            out[c * high : (c + 1) * high] = tile.reshape(high, plan.each, LANES)
     for t in targets:
         wanted = jnp.concatenate([t[b] for b in range(t.shape[0])], 0)
         for c in range(plan.col_tiles):
-            out[c * high] = out[c * high] - wanted[:, c * LANES : (c + 1) * LANES]
+            outs[members][c * high] = (
+                outs[members][c * high] - wanted[:, c * LANES : (c + 1) * LANES]
+            )
 
 
 def by_batch(is_first, mine, theirs):
@@ -301,7 +307,7 @@
         c.wait()
 
 
-def per_device(dataset, centers, weights, batch_index, targets, gamma):
+def body(dataset, centers, weights, batch_index, targets, gamma):
     shards = lax.axis_size("center")
     cores = lax.axis_size("row")
     batches, rows_here = batch_index.shape
@@ -321,7 +327,6 @@
     (local,) = call(
         pick_body,
         [kept(each, features)],
-        "pick",
         (batch_index, pl.ANY),
         (dataset, pl.ANY),
         scratch_shapes=[
@@ -333,49 +338,42 @@
     split, row = call(
         prepare_body,
         [pltpu.VMEM((3, count, features), jnp.bfloat16), kept(8, count)],
-        "prepare",
         (centers, pl.ANY),
         scratch_shapes=[pltpu.VMEM(centers.shape, jnp.float32), pltpu.SemaphoreType.DMA],
     )
     spread = jnp.broadcast_to(gamma, (8, count))
     (weight_split,) = call(
-        weights_body,
-        [pltpu.VMEM((3, count, 2 * cols), jnp.bfloat16)],
-        "weights",
-        weights,
-        swap_cores(weights),
+        weights_body, [pltpu.VMEM((3, count, 2 * cols), jnp.bfloat16)], weights, swap_cores(weights)
     )
     rows = local
     for bit in bits:
         rows = jnp.concatenate([rows, across(rows, QUAD * bit)], 0)
-    own, packets = [], []
-    for q, x in enumerate([rows] + [across(rows, q) for q in quad]):
-        k, packet = call(
-            functools.partial(block_body, plan),
-            [kept(span, count), kept(plan.sums, each, LANES)],
-            "block",
+    received = [rows] + [across(rows, q) for q in quad]
+    own, packets = [None] * QUAD, [None] * QUAD
+    for group in ((0,), (3,), (2, 1)):
+        done = call(
+            functools.partial(block_body, plan, len(group)),
+            [kept(span, count)] * len(group)
+            + [kept(plan.sums, each, LANES)] * len(group),
             spread,
-            x,
             split,
             row,
             weight_split,
-            *([targets] if q == 0 else []),
+            *[received[q] for q in group],
+            *([targets] if group == (0,) else []),
         )
-        own.append(k)
-        packets.append(packet)
+        for i, q in enumerate(group):
+            own[q], packets[q] = done[i], done[len(group) + i]
     sums = [across(packets[q], q) for q in reversed(quad)]
     own = jnp.concatenate(own, 0)
     k0, k1, gram, gram_sent = call(
         functools.partial(gram_body, plan),
         [kept(n, count)] * 2 + [kept(plan.grams, each, LANES)] * 2,
-        "gram",
         own,
         swap_cores(own),
     )
     shape = kept(plan.tiles, each, LANES)
-    (total,) = call(
-        functools.partial(quad_body, plan), [shape], "quad", packets[0], *sums, gram_sent
-    )
+    (total,) = call(functools.partial(quad_body, plan), [shape], packets[0], *sums, gram_sent)
     for i, bit in enumerate(bits):
         if i == 0:
             other = across(total, QUAD * bit)
@@ -384,14 +382,11 @@
             other = jnp.concatenate(
                 [across(total[: plan.sums], QUAD * bit), partner(gram, QUAD * bit)], 0
             )
-        (total,) = call(
-            functools.partial(high_body, plan, bit), [shape], "high", total, gram, other
-        )
+        (total,) = call(functools.partial(high_body, plan, bit), [shape], total, gram, other)
     mine = [across(total, q) for q in reversed(quad)] + [total]
     new_weights, residual = call(
         functools.partial(solve_body, plan, rate),
         [stored(count, cols), stored(rows_here, 2 * cols)],
-        "solve",
         *mine,
         *[swap_cores(x) for x in mine],
         k0,
@@ -411,7 +406,7 @@
 
 def solution(mesh):
     return jax.shard_map(
-        per_device,
+        body,
         mesh=mesh,
         in_specs=(
             P(("groups", "center", "row"), None),

time: 36.6 us -> 36.1 us (0.986)
  Pallas kernels: 6.36 us -> 5.79 us
    pallas_call x11 -> x10, Pallas kernels: 6.36 us -> 5.79 us  [call(): pl.pallas_call(body, out_shape=outs, in_specs=[pl.BlockSpec(memory_space=...]
  transfers between devices with their start and end apart: 17 -> 17, of which waited for: 9 -> 9; matrix products, arithmetic and copies ran while one was open for 0% -> 0% of each run, Pallas kernels for 11% -> 10%
where the time goes in v8:
time: 36.1 us; the launch traced here: 35.8 us
  starting transfers between devices  20.6 us (57%)
  waiting for transfers between devices  7.36 us (20%)
  Pallas kernels  5.79 us (16%)
  between operations  1.39 us (4%)
  local copies, waits for them, and re-layouts  0.64 us (2%)
    ppermute x11, starting transfers between devices, across(): return lax.ppermute(x, ('center', 'row'), pairs)  18.1 us
    ppermute x11, waiting for transfers between devices, across(): return lax.ppermute(x, ('center', 'row'), pairs)  6.35 us
    pallas_call x10, Pallas kernels, call(): pl.pallas_call(body, out_shape=outs, in_specs=[pl.BlockSpec(memory_space=...  5.79 us
    ppermute x6, starting transfers between devices, swap_cores(): return lax.ppermute(x, 'row', [(0, 1), (1, 0)])  2.55 us
    ppermute x6, waiting for transfers between devices, swap_cores(): return lax.ppermute(x, 'row', [(0, 1), (1, 0)])  1.01 us
  transfers between devices with their start and end apart: 17, of which 9 were waited for; matrix products, arithmetic and copies ran while one was open for 0% of the time, Pallas kernels for 10%

profile of v8, /device:TPU:0, one launch (start us, length us, event | category | flops | bytes accessed | tf_op | source)
XLA Modules:
  0.0 35.8 jit_solution(8548168316309117352)
XLA Ops:
  0.6 0.9 %shard_map.82 = f32[8,1024]{1,0:T(8,128)S(1)} custom-call(s32[2,4]{1,0:T(2,128)} %index.1, f32[16,1024]{1,0:T(8,128)} %dataset.1), custom_call_target="tpu_custom_call" | custom-call | tf_op jit(solution)/shard_map/pallas_call | solution.py:72
  1.5 3.6 %collective-permute-start.1 = (f32[8,1024]{1,0:T(8,128)S(1)}, f32[8,1024]{1,0:T(8,128)S(1)}, u32[]{:S(2)}, u32[]{:S(2)}) collective-permute-start(f32[8,1024]{1,0:T(8,128)S(1)} %shard_map.82), channel_id=1, source_target_pairs={{0,9},{1,8},{2,11},{3,10},{4,13},{5,12},{6,15},{7,14},{8,1},{9,0},... | collective-permute-start | bytes 98312 | tf_op jit(solution)/shard_map/ppermute | solution.py:110
  5.1 0.7 %collective-permute-start = (f32[128,256]{1,0:T(8,128)}, f32[128,256]{1,0:T(8,128)S(1)}, u32[]{:S(2)}, u32[]{:S(2)}) collective-permute-start(f32[128,256]{1,0:T(8,128)} %refs_10_.1), channel_id=1, source_target_pairs={{0,1},{1,0},{2,3},{3,2},{4,5},{5,4},{6,7},{7,6},{8,9},{9,8},{10,11... | collective-permute-start | bytes 393224 | tf_op jit(solution)/shard_map/ppermute | solution.py:97
  5.8 1.1 %collective-permute-done.1 = f32[8,1024]{1,0:T(8,128)S(1)} collective-permute-done((f32[8,1024]{1,0:T(8,128)S(1)}, f32[8,1024]{1,0:T(8,128)S(1)}, u32[]{:S(2)}, u32[]{:S(2)}) %collective-permute-start.1) | collective-permute-done | bytes 32800 | tf_op jit(solution)/shard_map/ppermute | solution.py:110
  6.9 2.8 %collective-permute-start.2 = (f32[16,1024]{1,0:T(8,128)S(1)}, f32[16,1024]{1,0:T(8,128)S(1)}, u32[]{:S(2)}, u32[]{:S(2)}) collective-permute-start(f32[16,1024]{1,0:T(8,128)S(1)} %pad_maximum_fusion.refs_0_), channel_id=1, source_target_pairs={{0,7},{1,6},{2,5},{3,4},{4,3},{5,2},{6,1},{7,0},{8,15},{9,14},{10,... | collective-permute-start | bytes 196616 | tf_op jit(solution)/shard_map/ppermute | solution.py:110
  10.3 0.0 copy-start
  10.3 1.4 %shard_map.80 = (bf16[3,128,1024]{2,1,0:T(8,128)(2,1)S(1)}, f32[8,128]{1,0:T(8,128)S(1)}) custom-call(f32[128,1024]{1,0:T(8,128)} %centers.1), custom_call_target="tpu_custom_call" | custom-call | tf_op jit(solution)/shard_map/pallas_call | solution.py:72
  11.7 0.5 %collective-permute-start.4 = (f32[16,1024]{1,0:T(8,128)S(1)}, f32[16,1024]{1,0:T(8,128)S(1)}, u32[]{:S(2)}, u32[]{:S(2)}) collective-permute-start(f32[16,1024]{1,0:T(8,128)S(1)} %pad_maximum_fusion.refs_0_), channel_id=1, source_target_pairs={{0,5},{1,4},{2,7},{3,6},{4,1},{5,0},{6,3},{7,2},{8,13},{9,12},{10,... | collective-permute-start | bytes 196616 | tf_op jit(solution)/shard_map/ppermute | solution.py:110
  12.2 0.2 collective-permute-start.5
  12.3 0.0 collective-permute-done.theirs
  12.3 0.0 copy-done
  12.3 0.0 copy-start.1
  12.3 0.1 shard_map.81.weights
  12.4 0.6 %copy-done.1 = f32[2,4,512]{2,1,0:T(4,128)S(1)} copy-done((f32[2,4,512]{2,1,0:T(4,128)S(1)}, f32[2,4,512]{2,1,0:T(4,128)}, u32[]{:S(2)}) %copy-start.1) | copy-done | bytes 16408
  13.1 0.6 %shard_map.83 = (f32[16,128]{1,0:T(8,128)S(1)}, f32[8,8,128]{2,1,0:T(8,128)S(1)}) custom-call(f32[8,128]{1,0:T(8,128)S(1)} %broadcast_in_dim.2.gamma, bf16[3,128,1024]{2,1,0:T(8,128)(2,1)S(1)} %get-tuple-element.16.split, f32[8,128]{1,0:T(8,128)S(1)} %get-tuple-element.17.row, bf16[3,128,512]{2,1,0:T(8,128)(2,1)S(1)} %shard_map.81.weights, ...), custom_call_target="tpu_custom_call" | custom-call | tf_op jit(solution)/shard_map/pallas_call | solution.py:72
  13.7 0.0 collective-permute-done.2.refs_0_
  13.7 0.6 %shard_map.84 = (f32[16,128]{1,0:T(8,128)S(1)}, f32[8,8,128]{2,1,0:T(8,128)S(1)}) custom-call(f32[8,128]{1,0:T(8,128)S(1)} %broadcast_in_dim.2.gamma, bf16[3,128,1024]{2,1,0:T(8,128)(2,1)S(1)} %get-tuple-element.16.split, f32[8,128]{1,0:T(8,128)S(1)} %get-tuple-element.17.row, bf16[3,128,512]{2,1,0:T(8,128)(2,1)S(1)} %shard_map.81.weights, ...), custom_call_target="tpu_custom_call" | custom-call | tf_op jit(solution)/shard_map/pallas_call | solution.py:72
  14.3 2.6 %collective-permute-start.3 = (f32[8,8,128]{2,1,0:T(8,128)S(1)}, f32[8,8,128]{2,1,0:T(8,128)S(1)}, u32[]{:S(2)}, u32[]{:S(2)}) collective-permute-start(f32[8,8,128]{2,1,0:T(8,128)S(1)} %get-tuple-element.19), channel_id=1, source_target_pairs={{0,7},{1,6},{2,5},{3,4},{4,3},{5,2},{6,1},{7,0},{8,15},{9,14},{10,... | collective-permute-start | bytes 98312 | tf_op jit(solution)/shard_map/ppermute | solution.py:110
  16.9 0.0 collective-permute-done.4.refs_0_
  16.9 0.0 collective-permute-done.5.refs_1_
  16.9 0.7 %shard_map.85 = (f32[16,128]{1,0:T(8,128)S(1)}, f32[16,128]{1,0:T(8,128)S(1)}, f32[8,8,128]{2,1,0:T(8,128)S(1)}, f32[8,8,128]{2,1,0:T(8,128)S(1)}) custom-call(f32[8,128]{1,0:T(8,128)S(1)} %broadcast_in_dim.2.gamma, bf16[3,128,1024]{2,1,0:T(8,128)(2,1)S(1)} %get-tuple-element.16.split, f32[8,128]{1,0:T(8,128)S(1)} %get-tuple-element.17.row, ...), custom_call_target="tpu_custom_call" | custom-call | tf_op jit(solution)/shard_map/pallas_call | solution.py:72
  17.6 0.2 collective-permute-start.8
  17.8 0.9 %collective-permute-start.6 = (f32[8,8,128]{2,1,0:T(8,128)S(1)}, f32[8,8,128]{2,1,0:T(8,128)S(1)}, u32[]{:S(2)}, u32[]{:S(2)}) collective-permute-start(f32[8,8,128]{2,1,0:T(8,128)S(1)} %get-tuple-element.20), channel_id=1, source_target_pairs={{0,5},{1,4},{2,7},{3,6},{4,1},{5,0},{6,3},{7,2},{8,13},{9,12},{10,... | collective-permute-start | bytes 98312 | tf_op jit(solution)/shard_map/ppermute | solution.py:110
  18.7 0.3 collective-permute-start.7
  19.0 0.0 collective-permute-done.8.swapped
  19.0 0.3 shard_map.86
  19.3 0.0 collective-permute-done.3.refs_1_
  19.3 1.9 %collective-permute-done.6.refs_2_ = f32[8,8,128]{2,1,0:T(8,128)S(1)} collective-permute-done((f32[8,8,128]{2,1,0:T(8,128)S(1)}, f32[8,8,128]{2,1,0:T(8,128)S(1)}, u32[]{:S(2)}, u32[]{:S(2)}) %collective-permute-start.6) | collective-permute-done | bytes 32800 | tf_op jit(solution)/shard_map/ppermute | solution.py:110
  21.2 1.0 %collective-permute-done.7.refs_3_ = f32[8,8,128]{2,1,0:T(8,128)S(1)} collective-permute-done((f32[8,8,128]{2,1,0:T(8,128)S(1)}, f32[8,8,128]{2,1,0:T(8,128)S(1)}, u32[]{:S(2)}, u32[]{:S(2)}) %collective-permute-start.7) | collective-permute-done | bytes 32800 | tf_op jit(solution)/shard_map/ppermute | solution.py:110
  22.1 3.2 %collective-permute-start.9 = (f32[10,8,128]{2,1,0:T(8,128)S(1)}, f32[10,8,128]{2,1,0:T(8,128)S(1)}, u32[]{:S(2)}, u32[]{:S(2)}) collective-permute-start(f32[10,8,128]{2,1,0:T(8,128)S(1)} %shard_map.87.mine), channel_id=1, source_target_pairs={{0,9},{1,8},{2,11},{3,10},{4,13},{5,12},{6,15},{7,14},{8,1},{9,0},... | collective-permute-start | bytes 122888 | tf_op jit(solution)/shard_map/ppermute | solution.py:110
  25.4 1.7 %collective-permute-done.9.other = f32[10,8,128]{2,1,0:T(8,128)S(1)} collective-permute-done((f32[10,8,128]{2,1,0:T(8,128)S(1)}, f32[10,8,128]{2,1,0:T(8,128)S(1)}, u32[]{:S(2)}, u32[]{:S(2)}) %collective-permute-start.9) | collective-permute-done | bytes 40992 | tf_op jit(solution)/shard_map/ppermute | solution.py:110
  27.0 1.1 %collective-permute-start.10 = (f32[10,8,128]{2,1,0:T(8,128)S(1)}, f32[10,8,128]{2,1,0:T(8,128)S(1)}, u32[]{:S(2)}, u32[]{:S(2)}) collective-permute-start(f32[10,8,128]{2,1,0:T(8,128)S(1)} %shard_map.88.refs_3_), channel_id=1, source_target_pairs={{0,7},{1,6},{2,5},{3,4},{4,3},{5,2},{6,1},{7,0},{8,15},{9,14},{10,... | collective-permute-start | bytes 122888 | tf_op jit(solution)/shard_map/ppermute | solution.py:110
  28.1 0.6 %collective-permute-start.11 = (f32[10,8,128]{2,1,0:T(8,128)S(1)}, f32[10,8,128]{2,1,0:T(8,128)S(1)}, u32[]{:S(2)}, u32[]{:S(2)}) collective-permute-start(f32[10,8,128]{2,1,0:T(8,128)S(1)} %shard_map.88.refs_3_), channel_id=1, source_target_pairs={{0,5},{1,4},{2,7},{3,6},{4,1},{5,0},{6,3},{7,2},{8,13},{9,12},{10,... | collective-permute-start | bytes 122888 | tf_op jit(solution)/shard_map/ppermute | solution.py:110
  28.8 2.3 %collective-permute-start.12 = (f32[10,8,128]{2,1,0:T(8,128)S(1)}, f32[10,8,128]{2,1,0:T(8,128)S(1)}, u32[]{:S(2)}, u32[]{:S(2)}) collective-permute-start(f32[10,8,128]{2,1,0:T(8,128)S(1)} %shard_map.88.refs_3_), channel_id=1, source_target_pairs={{0,3},{1,2},{2,1},{3,0},{4,7},{5,6},{6,5},{7,4},{8,11},{9,10},{10,... | collective-permute-start | bytes 122888 | tf_op jit(solution)/shard_map/ppermute | solution.py:110
  31.1 0.0 collective-permute-start.16
  31.1 0.3 collective-permute-done.10.refs_0_
  31.4 1.5 %collective-permute-start.13 = (f32[10,8,128]{2,1,0:T(8,128)S(1)}, f32[10,8,128]{2,1,0:T(8,128)S(1)}, u32[]{:S(2)}, u32[]{:S(2)}) collective-permute-start(f32[10,8,128]{2,1,0:T(8,128)S(1)} %collective-permute-done.10.refs_0_), channel_id=1, source_target_pairs={{0,1},{1,0},{2,3},{3,2},{4,5},{5,4},{6,7},{7,6},{8,9},{9,8},{10,11... | collective-permute-start | bytes 122888 | tf_op jit(solution)/shard_map/ppermute | solution.py:97
  32.9 0.0 collective-permute-done.11.refs_1_
  32.9 0.0 collective-permute-start.14
  32.9 0.4 %collective-permute-done.12.refs_2_ = f32[10,8,128]{2,1,0:T(8,128)S(1)} collective-permute-done((f32[10,8,128]{2,1,0:T(8,128)S(1)}, f32[10,8,128]{2,1,0:T(8,128)S(1)}, u32[]{:S(2)}, u32[]{:S(2)}) %collective-permute-start.12) | collective-permute-done | bytes 40992 | tf_op jit(solution)/shard_map/ppermute | solution.py:110
  33.3 0.2 collective-permute-start.15
  33.5 0.0 collective-permute-done.16.refs_7_
  33.5 0.2 collective-permute-done.13.refs_4_
  33.7 0.4 collective-permute-done.14.refs_5_
  34.1 0.4 %collective-permute-done.15.refs_6_ = f32[10,8,128]{2,1,0:T(8,128)S(1)} collective-permute-done((f32[10,8,128]{2,1,0:T(8,128)S(1)}, f32[10,8,128]{2,1,0:T(8,128)S(1)}, u32[]{:S(2)}, u32[]{:S(2)}) %collective-permute-start.15) | collective-permute-done | bytes 40992 | tf_op jit(solution)/shard_map/ppermute | solution.py:97
  34.5 1.3 %shard_map.89 = (f32[128,256]{1,0:T(8,128)}, f32[4,512]{1,0:T(4,128)}) custom-call(f32[10,8,128]{2,1,0:T(8,128)S(1)} %collective-permute-done.10.refs_0_, f32[10,8,128]{2,1,0:T(8,128)S(1)} %collective-permute-done.11.refs_1_, f32[10,8,128]{2,1,0:T(8,128)S(1)} %collective-permute-done.12.refs_2_, f32[10,8,128]{2,1,0:T(8,128)S(1)} %shard_map.88.refs_3_, ...), custom_call_target="tpu_custom_call" | custom-call | tf_op jit(solution)/shard_map/pallas_call | solution.py:72
  (8 shorter events, 0.0 us)
Async XLA Ops:
  1.5 5.4 %collective-permute-start.1 = (f32[8,1024]{1,0:T(8,128)S(1)}, f32[8,1024]{1,0:T(8,128)S(1)}, u32[]{:S(2)}, u32[]{:S(2)}) collective-permute-start(f32[8,1024]{1,0:T(8,128)S(1)} %shard_map.82), channel_id=1, source_target_pairs={{0,9},{1,8},{2,11},{3,10},{4,13},{5,12},{6,15},{7,14},{8,1},{9,0},... | collective-permute-start | bytes 98312 | tf_op jit(solution)/shard_map/ppermute | solution.py:110
  5.1 7.3 %collective-permute-start = (f32[128,256]{1,0:T(8,128)}, f32[128,256]{1,0:T(8,128)S(1)}, u32[]{:S(2)}, u32[]{:S(2)}) collective-permute-start(f32[128,256]{1,0:T(8,128)} %refs_10_.1), channel_id=1, source_target_pairs={{0,1},{1,0},{2,3},{3,2},{4,5},{5,4},{6,7},{7,6},{8,9},{9,8},{10,11... | collective-permute-start | bytes 393224 | tf_op jit(solution)/shard_map/ppermute | solution.py:97
  6.9 6.8 %collective-permute-start.2 = (f32[16,1024]{1,0:T(8,128)S(1)}, f32[16,1024]{1,0:T(8,128)S(1)}, u32[]{:S(2)}, u32[]{:S(2)}) collective-permute-start(f32[16,1024]{1,0:T(8,128)S(1)} %pad_maximum_fusion.refs_0_), channel_id=1, source_target_pairs={{0,7},{1,6},{2,5},{3,4},{4,3},{5,2},{6,1},{7,0},{8,15},{9,14},{10,... | collective-permute-start | bytes 196616 | tf_op jit(solution)/shard_map/ppermute | solution.py:110
  10.3 2.1 %copy-start = (f32[128,256]{1,0:T(8,128)S(1)}, f32[128,256]{1,0:T(8,128)}, u32[]{:S(2)}) copy-start(f32[128,256]{1,0:T(8,128)} %refs_10_.1) | copy-start | bytes 393220
  11.7 5.3 %collective-permute-start.4 = (f32[16,1024]{1,0:T(8,128)S(1)}, f32[16,1024]{1,0:T(8,128)S(1)}, u32[]{:S(2)}, u32[]{:S(2)}) collective-permute-start(f32[16,1024]{1,0:T(8,128)S(1)} %pad_maximum_fusion.refs_0_), channel_id=1, source_target_pairs={{0,5},{1,4},{2,7},{3,6},{4,1},{5,0},{6,3},{7,2},{8,13},{9,12},{10,... | collective-permute-start | bytes 196616 | tf_op jit(solution)/shard_map/ppermute | solution.py:110
  12.2 4.8 %collective-permute-start.5 = (f32[16,1024]{1,0:T(8,128)S(1)}, f32[16,1024]{1,0:T(8,128)S(1)}, u32[]{:S(2)}, u32[]{:S(2)}) collective-permute-start(f32[16,1024]{1,0:T(8,128)S(1)} %pad_maximum_fusion.refs_0_), channel_id=1, source_target_pairs={{0,3},{1,2},{2,1},{3,0},{4,7},{5,6},{6,5},{7,4},{8,11},{9,10},{10,... | collective-permute-start | bytes 196616 | tf_op jit(solution)/shard_map/ppermute | solution.py:110
  12.3 0.7 %copy-start.1 = (f32[2,4,512]{2,1,0:T(4,128)S(1)}, f32[2,4,512]{2,1,0:T(4,128)}, u32[]{:S(2)}) copy-start(f32[2,4,512]{2,1,0:T(4,128)} %refs_1_.1) | copy-start | bytes 49156
  14.3 5.0 %collective-permute-start.3 = (f32[8,8,128]{2,1,0:T(8,128)S(1)}, f32[8,8,128]{2,1,0:T(8,128)S(1)}, u32[]{:S(2)}, u32[]{:S(2)}) collective-permute-start(f32[8,8,128]{2,1,0:T(8,128)S(1)} %get-tuple-element.19), channel_id=1, source_target_pairs={{0,7},{1,6},{2,5},{3,4},{4,3},{5,2},{6,1},{7,0},{8,15},{9,14},{10,... | collective-permute-start | bytes 98312 | tf_op jit(solution)/shard_map/ppermute | solution.py:110
  17.6 1.4 %collective-permute-start.8 = (f32[64,128]{1,0:T(8,128)S(1)}, f32[64,128]{1,0:T(8,128)S(1)}, u32[]{:S(2)}, u32[]{:S(2)}) collective-permute-start(f32[64,128]{1,0:T(8,128)S(1)} %constant_dynamic-update-slice_fusion.own), channel_id=1, source_target_pairs={{0,1},{1,0},{2,3},{3,2},{4,5},{5,4},{6,7},{7,6},{8,9},{9,8},{10,11... | collective-permute-start | bytes 98312 | tf_op jit(solution)/shard_map/ppermute | solution.py:97
  17.8 3.3 %collective-permute-start.6 = (f32[8,8,128]{2,1,0:T(8,128)S(1)}, f32[8,8,128]{2,1,0:T(8,128)S(1)}, u32[]{:S(2)}, u32[]{:S(2)}) collective-permute-start(f32[8,8,128]{2,1,0:T(8,128)S(1)} %get-tuple-element.20), channel_id=1, source_target_pairs={{0,5},{1,4},{2,7},{3,6},{4,1},{5,0},{6,3},{7,2},{8,13},{9,12},{10,... | collective-permute-start | bytes 98312 | tf_op jit(solution)/shard_map/ppermute | solution.py:110
  18.7 3.4 %collective-permute-start.7 = (f32[8,8,128]{2,1,0:T(8,128)S(1)}, f32[8,8,128]{2,1,0:T(8,128)S(1)}, u32[]{:S(2)}, u32[]{:S(2)}) collective-permute-start(f32[8,8,128]{2,1,0:T(8,128)S(1)} %get-tuple-element.21), channel_id=1, source_target_pairs={{0,3},{1,2},{2,1},{3,0},{4,7},{5,6},{6,5},{7,4},{8,11},{9,10},{10,... | collective-permute-start | bytes 98312 | tf_op jit(solution)/shard_map/ppermute | solution.py:110
  22.1 4.9 %collective-permute-start.9 = (f32[10,8,128]{2,1,0:T(8,128)S(1)}, f32[10,8,128]{2,1,0:T(8,128)S(1)}, u32[]{:S(2)}, u32[]{:S(2)}) collective-permute-start(f32[10,8,128]{2,1,0:T(8,128)S(1)} %shard_map.87.mine), channel_id=1, source_target_pairs={{0,9},{1,8},{2,11},{3,10},{4,13},{5,12},{6,15},{7,14},{8,1},{9,0},... | collective-permute-start | bytes 122888 | tf_op jit(solution)/shard_map/ppermute | solution.py:110
  27.0 4.3 %collective-permute-start.10 = (f32[10,8,128]{2,1,0:T(8,128)S(1)}, f32[10,8,128]{2,1,0:T(8,128)S(1)}, u32[]{:S(2)}, u32[]{:S(2)}) collective-permute-start(f32[10,8,128]{2,1,0:T(8,128)S(1)} %shard_map.88.refs_3_), channel_id=1, source_target_pairs={{0,7},{1,6},{2,5},{3,4},{4,3},{5,2},{6,1},{7,0},{8,15},{9,14},{10,... | collective-permute-start | bytes 122888 | tf_op jit(solution)/shard_map/ppermute | solution.py:110
  28.1 4.7 %collective-permute-start.11 = (f32[10,8,128]{2,1,0:T(8,128)S(1)}, f32[10,8,128]{2,1,0:T(8,128)S(1)}, u32[]{:S(2)}, u32[]{:S(2)}) collective-permute-start(f32[10,8,128]{2,1,0:T(8,128)S(1)} %shard_map.88.refs_3_), channel_id=1, source_target_pairs={{0,5},{1,4},{2,7},{3,6},{4,1},{5,0},{6,3},{7,2},{8,13},{9,12},{10,... | collective-permute-start | bytes 122888 | tf_op jit(solution)/shard_map/ppermute | solution.py:110
  28.8 4.5 %collective-permute-start.12 = (f32[10,8,128]{2,1,0:T(8,128)S(1)}, f32[10,8,128]{2,1,0:T(8,128)S(1)}, u32[]{:S(2)}, u32[]{:S(2)}) collective-permute-start(f32[10,8,128]{2,1,0:T(8,128)S(1)} %shard_map.88.refs_3_), channel_id=1, source_target_pairs={{0,3},{1,2},{2,1},{3,0},{4,7},{5,6},{6,5},{7,4},{8,11},{9,10},{10,... | collective-permute-start | bytes 122888 | tf_op jit(solution)/shard_map/ppermute | solution.py:110
  31.1 2.4 %collective-permute-start.16 = (f32[10,8,128]{2,1,0:T(8,128)S(1)}, f32[10,8,128]{2,1,0:T(8,128)S(1)}, u32[]{:S(2)}, u32[]{:S(2)}) collective-permute-start(f32[10,8,128]{2,1,0:T(8,128)S(1)} %shard_map.88.refs_3_), channel_id=1, source_target_pairs={{0,1},{1,0},{2,3},{3,2},{4,5},{5,4},{6,7},{7,6},{8,9},{9,8},{10,11... | collective-permute-start | bytes 122888 | tf_op jit(solution)/shard_map/ppermute | solution.py:97
  31.4 2.3 %collective-permute-start.13 = (f32[10,8,128]{2,1,0:T(8,128)S(1)}, f32[10,8,128]{2,1,0:T(8,128)S(1)}, u32[]{:S(2)}, u32[]{:S(2)}) collective-permute-start(f32[10,8,128]{2,1,0:T(8,128)S(1)} %collective-permute-done.10.refs_0_), channel_id=1, source_target_pairs={{0,1},{1,0},{2,3},{3,2},{4,5},{5,4},{6,7},{7,6},{8,9},{9,8},{10,11... | collective-permute-start | bytes 122888 | tf_op jit(solution)/shard_map/ppermute | solution.py:97
  32.9 1.2 %collective-permute-start.14 = (f32[10,8,128]{2,1,0:T(8,128)S(1)}, f32[10,8,128]{2,1,0:T(8,128)S(1)}, u32[]{:S(2)}, u32[]{:S(2)}) collective-permute-start(f32[10,8,128]{2,1,0:T(8,128)S(1)} %collective-permute-done.11.refs_1_), channel_id=1, source_target_pairs={{0,1},{1,0},{2,3},{3,2},{4,5},{5,4},{6,7},{7,6},{8,9},{9,8},{10,11... | collective-permute-start | bytes 122888 | tf_op jit(solution)/shard_map/ppermute | solution.py:97
  33.3 1.2 %collective-permute-start.15 = (f32[10,8,128]{2,1,0:T(8,128)S(1)}, f32[10,8,128]{2,1,0:T(8,128)S(1)}, u32[]{:S(2)}, u32[]{:S(2)}) collective-permute-start(f32[10,8,128]{2,1,0:T(8,128)S(1)} %collective-permute-done.12.refs_2_), channel_id=1, source_target_pairs={{0,1},{1,0},{2,3},{3,2},{4,5},{5,4},{6,7},{7,6},{8,9},{9,8},{10,11... | collective-permute-start | bytes 122888 | tf_op jit(solution)/shard_map/ppermute | solution.py:97

commit v9 on v8

--- a/solution.py
+++ b/solution.py
@@ -207,7 +207,7 @@
     return lax.axis_index("center") ^ (QUAD * h + q)
 
 
-def gram_body(plan, own, swapped, k0_out, k1_out, keep, send):
+def gram_body(plan, own, swapped, turned, keep, send, k0_out, k1_out):
     each = plan.each
     me = lax.axis_index("row")
     for q, h, crossed in plan.blocks():
@@ -215,6 +215,7 @@
         tile = slice(at, at + each)
         to = pl.ds(pl.multiple_of(chip_at(q, h) * each, each), each)
         k0_out[to], k1_out[to] = by_batch(me == crossed, own[tile], swapped[tile])
+    turned[...] = jnp.concatenate([k0_out[...], k1_out[...]], 0).T
     k0 = jnp.concatenate([k0_out[...]] * plan.pack, 0)
     gram = dot(k1_out[...], k0, ((1,), (1,)))
     gram = gram.reshape(plan.chips // 2, 2, each, gram.shape[1])
@@ -259,7 +260,7 @@
 def solve_body(plan, rate, *refs):
     mine, refs = refs[:QUAD][::-1], refs[QUAD:]
     theirs, refs = refs[:QUAD][::-1], refs[QUAD:]
-    k0, k1, weights, weights_out, residual_out, res0, res1, weights_new, residual, sems = refs
+    turned, weights, weights_out, residual_out, res0, res1, weights_new, residual, sems = refs
     each, high = plan.each, plan.high
     half = each // 2
     me = lax.axis_index("row")
@@ -298,9 +299,8 @@
     copies[0].start()
     cols = weights.shape[1]
     side = lambda x: jnp.where(first, x[:, :cols], x[:, cols:])
-    grad = dot(k0[...], side(res0[...]), ((0,), (0,))) + dot(
-        k1[...], side(res1[...]), ((0,), (0,))
-    )
+    both = jnp.concatenate([side(res0[...]), side(res1[...])], 0)
+    grad = dot(turned[...], both, ((1,), (0,)))
     weights_new[...] = weights[...] - rate * grad
     copies[1].start()
     for c in copies:
@@ -350,7 +350,7 @@
         rows = jnp.concatenate([rows, across(rows, QUAD * bit)], 0)
     received = [rows] + [across(rows, q) for q in quad]
     own, packets = [None] * QUAD, [None] * QUAD
-    for group in ((0,), (3,), (2, 1)):
+    for group in ((0,), (3, 2, 1)):
         done = call(
             functools.partial(block_body, plan, len(group)),
             [kept(span, count)] * len(group)
@@ -366,11 +366,12 @@
             own[q], packets[q] = done[i], done[len(group) + i]
     sums = [across(packets[q], q) for q in reversed(quad)]
     own = jnp.concatenate(own, 0)
-    k0, k1, gram, gram_sent = call(
+    turned, gram, gram_sent = call(
         functools.partial(gram_body, plan),
-        [kept(n, count)] * 2 + [kept(plan.grams, each, LANES)] * 2,
+        [kept(count, 2 * n)] + [kept(plan.grams, each, LANES)] * 2,
         own,
         swap_cores(own),
+        scratch_shapes=[pltpu.VMEM((n, count), jnp.float32)] * 2,
     )
     shape = kept(plan.tiles, each, LANES)
     (total,) = call(functools.partial(quad_body, plan), [shape], packets[0], *sums, gram_sent)
@@ -389,8 +390,7 @@
         [stored(count, cols), stored(rows_here, 2 * cols)],
         *mine,
         *[swap_cores(x) for x in mine],
-        k0,
-        k1,
+        turned,
         weights,
         out_space=pl.ANY,
         scratch_shapes=[

time: 36.1 us -> 34.6 us (0.958)
  starting transfers between devices: 20.6 us -> 18.8 us
  waiting for transfers between devices: 7.36 us -> 8.34 us
  Pallas kernels: 5.79 us -> 5.14 us
    ppermute x11, starting transfers between devices: 18.1 us -> 16.6 us  [across(): return lax.ppermute(x, ('center', 'row'), pairs)]
    ppermute x11, waiting for transfers between devices: 6.35 us -> 7.08 us  [across(): return lax.ppermute(x, ('center', 'row'), pairs)]
    pallas_call x10 -> x9, Pallas kernels: 5.79 us -> 5.14 us  [call(): pl.pallas_call(body, out_shape=outs, in_specs=[pl.BlockSpec(memory_space=...]
    ppermute x6, starting transfers between devices: 2.55 us -> 2.16 us  [swap_cores(): return lax.ppermute(x, 'row', [(0, 1), (1, 0)])]
  transfers between devices with their start and end apart: 17 -> 17, of which waited for: 9 -> 11; matrix products, arithmetic and copies ran while one was open for 0% -> 0% of each run, Pallas kernels for 10% -> 7%
where the time goes in v9:
time: 34.6 us; the launch traced here: 34.3 us
  starting transfers between devices  18.8 us (54%)
  waiting for transfers between devices  8.34 us (24%)
  Pallas kernels  5.14 us (15%)
  between operations  1.4 us (4%)
  local copies, waits for them, and re-layouts  0.63 us (2%)
    ppermute x11, starting transfers between devices, across(): return lax.ppermute(x, ('center', 'row'), pairs)  16.6 us
    ppermute x11, waiting for transfers between devices, across(): return lax.ppermute(x, ('center', 'row'), pairs)  7.08 us
    pallas_call x9, Pallas kernels, call(): pl.pallas_call(body, out_shape=outs, in_specs=[pl.BlockSpec(memory_space=...  5.14 us
    ppermute x6, starting transfers between devices, swap_cores(): return lax.ppermute(x, 'row', [(0, 1), (1, 0)])  2.16 us
    ppermute x6, waiting for transfers between devices, swap_cores(): return lax.ppermute(x, 'row', [(0, 1), (1, 0)])  1.26 us
  transfers between devices with their start and end apart: 17, of which 11 were waited for; matrix products, arithmetic and copies ran while one was open for 0% of the time, Pallas kernels for 7%

profile of v9, /device:TPU:0, one launch (start us, length us, event | category | flops | bytes accessed | tf_op | source)
XLA Modules:
  0.0 34.3 jit_solution(7257131598688334404)
XLA Ops:
  0.6 0.9 %shard_map.82 = f32[8,1024]{1,0:T(8,128)S(1)} custom-call(s32[2,4]{1,0:T(2,128)} %index.1, f32[16,1024]{1,0:T(8,128)} %dataset.1), custom_call_target="tpu_custom_call" | custom-call | tf_op jit(solution)/shard_map/pallas_call | solution.py:72
  1.5 3.6 %collective-permute-start.1 = (f32[8,1024]{1,0:T(8,128)S(1)}, f32[8,1024]{1,0:T(8,128)S(1)}, u32[]{:S(2)}, u32[]{:S(2)}) collective-permute-start(f32[8,1024]{1,0:T(8,128)S(1)} %shard_map.82), channel_id=1, source_target_pairs={{0,9},{1,8},{2,11},{3,10},{4,13},{5,12},{6,15},{7,14},{8,1},{9,0},... | collective-permute-start | bytes 98312 | tf_op jit(solution)/shard_map/ppermute | solution.py:110
  5.1 0.7 %collective-permute-start = (f32[128,256]{1,0:T(8,128)}, f32[128,256]{1,0:T(8,128)S(1)}, u32[]{:S(2)}, u32[]{:S(2)}) collective-permute-start(f32[128,256]{1,0:T(8,128)} %refs_9_.1), channel_id=1, source_target_pairs={{0,1},{1,0},{2,3},{3,2},{4,5},{5,4},{6,7},{7,6},{8,9},{9,8},{10,11... | collective-permute-start | bytes 393224 | tf_op jit(solution)/shard_map/ppermute | solution.py:97
  5.8 1.1 %collective-permute-done.1 = f32[8,1024]{1,0:T(8,128)S(1)} collective-permute-done((f32[8,1024]{1,0:T(8,128)S(1)}, f32[8,1024]{1,0:T(8,128)S(1)}, u32[]{:S(2)}, u32[]{:S(2)}) %collective-permute-start.1) | collective-permute-done | bytes 32800 | tf_op jit(solution)/shard_map/ppermute | solution.py:110
  6.9 2.8 %collective-permute-start.2 = (f32[16,1024]{1,0:T(8,128)S(1)}, f32[16,1024]{1,0:T(8,128)S(1)}, u32[]{:S(2)}, u32[]{:S(2)}) collective-permute-start(f32[16,1024]{1,0:T(8,128)S(1)} %pad_maximum_fusion.refs_0_), channel_id=1, source_target_pairs={{0,7},{1,6},{2,5},{3,4},{4,3},{5,2},{6,1},{7,0},{8,15},{9,14},{10,... | collective-permute-start | bytes 196616 | tf_op jit(solution)/shard_map/ppermute | solution.py:110
  9.6 0.4 %collective-permute-start.3 = (f32[16,1024]{1,0:T(8,128)S(1)}, f32[16,1024]{1,0:T(8,128)S(1)}, u32[]{:S(2)}, u32[]{:S(2)}) collective-permute-start(f32[16,1024]{1,0:T(8,128)S(1)} %pad_maximum_fusion.refs_0_), channel_id=1, source_target_pairs={{0,5},{1,4},{2,7},{3,6},{4,1},{5,0},{6,3},{7,2},{8,13},{9,12},{10,... | collective-permute-start | bytes 196616 | tf_op jit(solution)/shard_map/ppermute | solution.py:110
  10.1 0.2 collective-permute-start.4
  10.9 0.0 copy-start
  10.9 1.4 %shard_map.80 = (bf16[3,128,1024]{2,1,0:T(8,128)(2,1)S(1)}, f32[8,128]{1,0:T(8,128)S(1)}) custom-call(f32[128,1024]{1,0:T(8,128)} %centers.1), custom_call_target="tpu_custom_call" | custom-call | tf_op jit(solution)/shard_map/pallas_call | solution.py:72
  12.3 0.0 collective-permute-done.theirs
  12.3 0.0 copy-done
  12.3 0.0 copy-start.1
  12.3 0.1 shard_map.81.weights
  12.4 0.6 %copy-done.1 = f32[2,4,512]{2,1,0:T(4,128)S(1)} copy-done((f32[2,4,512]{2,1,0:T(4,128)S(1)}, f32[2,4,512]{2,1,0:T(4,128)}, u32[]{:S(2)}) %copy-start.1) | copy-done | bytes 16408
  13.0 0.6 %shard_map.83 = (f32[16,128]{1,0:T(8,128)S(1)}, f32[8,8,128]{2,1,0:T(8,128)S(1)}) custom-call(f32[8,128]{1,0:T(8,128)S(1)} %broadcast_in_dim.2.gamma, bf16[3,128,1024]{2,1,0:T(8,128)(2,1)S(1)} %get-tuple-element.15.split, f32[8,128]{1,0:T(8,128)S(1)} %get-tuple-element.16.row, bf16[3,128,512]{2,1,0:T(8,128)(2,1)S(1)} %shard_map.81.weights, ...), custom_call_target="tpu_custom_call" | custom-call | tf_op jit(solution)/shard_map/pallas_call | solution.py:72
  13.6 0.0 collective-permute-done.2.refs_0_
  13.6 0.0 collective-permute-done.3.refs_1_
  13.7 0.5 %collective-permute-done.4.refs_2_ = f32[16,1024]{1,0:T(8,128)S(1)} collective-permute-done((f32[16,1024]{1,0:T(8,128)S(1)}, f32[16,1024]{1,0:T(8,128)S(1)}, u32[]{:S(2)}, u32[]{:S(2)}) %collective-permute-start.4) | collective-permute-done | bytes 65568 | tf_op jit(solution)/shard_map/ppermute | solution.py:110
  14.2 0.7 %shard_map.84 = (f32[16,128]{1,0:T(8,128)S(1)}, f32[16,128]{1,0:T(8,128)S(1)}, f32[16,128]{1,0:T(8,128)S(1)}, f32[8,8,128]{2,1,0:T(8,128)S(1)}, f32[8,8,128]{2,1,0:T(8,128)S(1)}, /*index=5*/f32[8,8,128]{2,1,0:T(8,128)S(1)}) custom-call(f32[8,128]{1,0:T(8,128)S(1)} %broadcast_in_dim.2.gamma, bf16[3,128,1024]{2,1,0:T(8,128)(2,1)S(1)} %get-tuple-element.15.split, ...), custom_call_target="tpu_custom_call" | custom-call | tf_op jit(solution)/shard_map/pallas_call | solution.py:72
  14.9 2.2 %collective-permute-start.5 = (f32[8,8,128]{2,1,0:T(8,128)S(1)}, f32[8,8,128]{2,1,0:T(8,128)S(1)}, u32[]{:S(2)}, u32[]{:S(2)}) collective-permute-start(f32[8,8,128]{2,1,0:T(8,128)S(1)} %get-tuple-element.18), channel_id=1, source_target_pairs={{0,7},{1,6},{2,5},{3,4},{4,3},{5,2},{6,1},{7,0},{8,15},{9,14},{10,... | collective-permute-start | bytes 98312 | tf_op jit(solution)/shard_map/ppermute | solution.py:110
  17.1 0.5 %collective-permute-start.8 = (f32[64,128]{1,0:T(8,128)S(1)}, f32[64,128]{1,0:T(8,128)S(1)}, u32[]{:S(2)}, u32[]{:S(2)}) collective-permute-start(f32[64,128]{1,0:T(8,128)S(1)} %constant_dynamic-update-slice_fusion.own), channel_id=1, source_target_pairs={{0,1},{1,0},{2,3},{3,2},{4,5},{5,4},{6,7},{7,6},{8,9},{9,8},{10,11... | collective-permute-start | bytes 98312 | tf_op jit(solution)/shard_map/ppermute | solution.py:97
  17.6 0.1 collective-permute-start.6
  17.7 0.7 %collective-permute-start.7 = (f32[8,8,128]{2,1,0:T(8,128)S(1)}, f32[8,8,128]{2,1,0:T(8,128)S(1)}, u32[]{:S(2)}, u32[]{:S(2)}) collective-permute-start(f32[8,8,128]{2,1,0:T(8,128)S(1)} %get-tuple-element.20), channel_id=1, source_target_pairs={{0,3},{1,2},{2,1},{3,0},{4,7},{5,6},{6,5},{7,4},{8,11},{9,10},{10,... | collective-permute-start | bytes 98312 | tf_op jit(solution)/shard_map/ppermute | solution.py:110
  18.4 0.1 collective-permute-done.8.swapped
  18.4 0.3 shard_map.85
  18.7 0.6 %collective-permute-done.5.refs_1_ = f32[8,8,128]{2,1,0:T(8,128)S(1)} collective-permute-done((f32[8,8,128]{2,1,0:T(8,128)S(1)}, f32[8,8,128]{2,1,0:T(8,128)S(1)}, u32[]{:S(2)}, u32[]{:S(2)}) %collective-permute-start.5) | collective-permute-done | bytes 32800 | tf_op jit(solution)/shard_map/ppermute | solution.py:110
  19.2 1.7 %collective-permute-done.6.refs_2_ = f32[8,8,128]{2,1,0:T(8,128)S(1)} collective-permute-done((f32[8,8,128]{2,1,0:T(8,128)S(1)}, f32[8,8,128]{2,1,0:T(8,128)S(1)}, u32[]{:S(2)}, u32[]{:S(2)}) %collective-permute-start.6) | collective-permute-done | bytes 32800 | tf_op jit(solution)/shard_map/ppermute | solution.py:110
  20.9 0.1 collective-permute-done.7.refs_3_
  21.0 3.1 %collective-permute-start.9 = (f32[10,8,128]{2,1,0:T(8,128)S(1)}, f32[10,8,128]{2,1,0:T(8,128)S(1)}, u32[]{:S(2)}, u32[]{:S(2)}) collective-permute-start(f32[10,8,128]{2,1,0:T(8,128)S(1)} %shard_map.86.mine), channel_id=1, source_target_pairs={{0,9},{1,8},{2,11},{3,10},{4,13},{5,12},{6,15},{7,14},{8,1},{9,0},... | collective-permute-start | bytes 122888 | tf_op jit(solution)/shard_map/ppermute | solution.py:110
  24.2 1.7 %collective-permute-done.9.other = f32[10,8,128]{2,1,0:T(8,128)S(1)} collective-permute-done((f32[10,8,128]{2,1,0:T(8,128)S(1)}, f32[10,8,128]{2,1,0:T(8,128)S(1)}, u32[]{:S(2)}, u32[]{:S(2)}) %collective-permute-start.9) | collective-permute-done | bytes 40992 | tf_op jit(solution)/shard_map/ppermute | solution.py:110
  25.9 1.9 %collective-permute-start.10 = (f32[10,8,128]{2,1,0:T(8,128)S(1)}, f32[10,8,128]{2,1,0:T(8,128)S(1)}, u32[]{:S(2)}, u32[]{:S(2)}) collective-permute-start(f32[10,8,128]{2,1,0:T(8,128)S(1)} %shard_map.87.refs_3_), channel_id=1, source_target_pairs={{0,7},{1,6},{2,5},{3,4},{4,3},{5,2},{6,1},{7,0},{8,15},{9,14},{10,... | collective-permute-start | bytes 122888 | tf_op jit(solution)/shard_map/ppermute | solution.py:110
  27.8 0.0 collective-permute-start.11
  27.8 1.6 %collective-permute-start.12 = (f32[10,8,128]{2,1,0:T(8,128)S(1)}, f32[10,8,128]{2,1,0:T(8,128)S(1)}, u32[]{:S(2)}, u32[]{:S(2)}) collective-permute-start(f32[10,8,128]{2,1,0:T(8,128)S(1)} %shard_map.87.refs_3_), channel_id=1, source_target_pairs={{0,3},{1,2},{2,1},{3,0},{4,7},{5,6},{6,5},{7,4},{8,11},{9,10},{10,... | collective-permute-start | bytes 122888 | tf_op jit(solution)/shard_map/ppermute | solution.py:110
  29.4 0.0 collective-permute-start.16
  29.4 0.8 %collective-permute-done.10.refs_0_ = f32[10,8,128]{2,1,0:T(8,128)S(1)} collective-permute-done((f32[10,8,128]{2,1,0:T(8,128)S(1)}, f32[10,8,128]{2,1,0:T(8,128)S(1)}, u32[]{:S(2)}, u32[]{:S(2)}) %collective-permute-start.10) | collective-permute-done | bytes 40992 | tf_op jit(solution)/shard_map/ppermute | solution.py:110
  30.2 0.4 %collective-permute-start.13 = (f32[10,8,128]{2,1,0:T(8,128)S(1)}, f32[10,8,128]{2,1,0:T(8,128)S(1)}, u32[]{:S(2)}, u32[]{:S(2)}) collective-permute-start(f32[10,8,128]{2,1,0:T(8,128)S(1)} %collective-permute-done.10.refs_0_), channel_id=1, source_target_pairs={{0,1},{1,0},{2,3},{3,2},{4,5},{5,4},{6,7},{7,6},{8,9},{9,8},{10,11... | collective-permute-start | bytes 122888 | tf_op jit(solution)/shard_map/ppermute | solution.py:97
  30.6 0.6 %collective-permute-done.11.refs_1_ = f32[10,8,128]{2,1,0:T(8,128)S(1)} collective-permute-done((f32[10,8,128]{2,1,0:T(8,128)S(1)}, f32[10,8,128]{2,1,0:T(8,128)S(1)}, u32[]{:S(2)}, u32[]{:S(2)}) %collective-permute-start.11) | collective-permute-done | bytes 40992 | tf_op jit(solution)/shard_map/ppermute | solution.py:110
  31.2 0.6 %collective-permute-start.14 = (f32[10,8,128]{2,1,0:T(8,128)S(1)}, f32[10,8,128]{2,1,0:T(8,128)S(1)}, u32[]{:S(2)}, u32[]{:S(2)}) collective-permute-start(f32[10,8,128]{2,1,0:T(8,128)S(1)} %collective-permute-done.11.refs_1_), channel_id=1, source_target_pairs={{0,1},{1,0},{2,3},{3,2},{4,5},{5,4},{6,7},{7,6},{8,9},{9,8},{10,11... | collective-permute-start | bytes 122888 | tf_op jit(solution)/shard_map/ppermute | solution.py:97
  31.8 0.0 collective-permute-done.12.refs_2_
  31.8 0.0 collective-permute-start.15
  31.9 0.0 collective-permute-done.16.refs_7_
  31.9 0.0 collective-permute-done.13.refs_4_
  31.9 0.8 %collective-permute-done.14.refs_5_ = f32[10,8,128]{2,1,0:T(8,128)S(1)} collective-permute-done((f32[10,8,128]{2,1,0:T(8,128)S(1)}, f32[10,8,128]{2,1,0:T(8,128)S(1)}, u32[]{:S(2)}, u32[]{:S(2)}) %collective-permute-start.14) | collective-permute-done | bytes 40992 | tf_op jit(solution)/shard_map/ppermute | solution.py:97
  32.7 0.4 %collective-permute-done.15.refs_6_ = f32[10,8,128]{2,1,0:T(8,128)S(1)} collective-permute-done((f32[10,8,128]{2,1,0:T(8,128)S(1)}, f32[10,8,128]{2,1,0:T(8,128)S(1)}, u32[]{:S(2)}, u32[]{:S(2)}) %collective-permute-start.15) | collective-permute-done | bytes 40992 | tf_op jit(solution)/shard_map/ppermute | solution.py:97
  33.1 1.2 %shard_map.88 = (f32[128,256]{1,0:T(8,128)}, f32[4,512]{1,0:T(4,128)}) custom-call(f32[10,8,128]{2,1,0:T(8,128)S(1)} %collective-permute-done.10.refs_0_, f32[10,8,128]{2,1,0:T(8,128)S(1)} %collective-permute-done.11.refs_1_, f32[10,8,128]{2,1,0:T(8,128)S(1)} %collective-permute-done.12.refs_2_, f32[10,8,128]{2,1,0:T(8,128)S(1)} %shard_map.87.refs_3_, ...), custom_call_target="tpu_custom_call" | custom-call | tf_op jit(solution)/shard_map/pallas_call | solution.py:72
  (8 shorter events, 0.0 us)
Async XLA Ops:
  1.5 5.4 %collective-permute-start.1 = (f32[8,1024]{1,0:T(8,128)S(1)}, f32[8,1024]{1,0:T(8,128)S(1)}, u32[]{:S(2)}, u32[]{:S(2)}) collective-permute-start(f32[8,1024]{1,0:T(8,128)S(1)} %shard_map.82), channel_id=1, source_target_pairs={{0,9},{1,8},{2,11},{3,10},{4,13},{5,12},{6,15},{7,14},{8,1},{9,0},... | collective-permute-start | bytes 98312 | tf_op jit(solution)/shard_map/ppermute | solution.py:110
  5.1 7.2 %collective-permute-start = (f32[128,256]{1,0:T(8,128)}, f32[128,256]{1,0:T(8,128)S(1)}, u32[]{:S(2)}, u32[]{:S(2)}) collective-permute-start(f32[128,256]{1,0:T(8,128)} %refs_9_.1), channel_id=1, source_target_pairs={{0,1},{1,0},{2,3},{3,2},{4,5},{5,4},{6,7},{7,6},{8,9},{9,8},{10,11... | collective-permute-start | bytes 393224 | tf_op jit(solution)/shard_map/ppermute | solution.py:97
  6.9 6.8 %collective-permute-start.2 = (f32[16,1024]{1,0:T(8,128)S(1)}, f32[16,1024]{1,0:T(8,128)S(1)}, u32[]{:S(2)}, u32[]{:S(2)}) collective-permute-start(f32[16,1024]{1,0:T(8,128)S(1)} %pad_maximum_fusion.refs_0_), channel_id=1, source_target_pairs={{0,7},{1,6},{2,5},{3,4},{4,3},{5,2},{6,1},{7,0},{8,15},{9,14},{10,... | collective-permute-start | bytes 196616 | tf_op jit(solution)/shard_map/ppermute | solution.py:110
  9.6 4.0 %collective-permute-start.3 = (f32[16,1024]{1,0:T(8,128)S(1)}, f32[16,1024]{1,0:T(8,128)S(1)}, u32[]{:S(2)}, u32[]{:S(2)}) collective-permute-start(f32[16,1024]{1,0:T(8,128)S(1)} %pad_maximum_fusion.refs_0_), channel_id=1, source_target_pairs={{0,5},{1,4},{2,7},{3,6},{4,1},{5,0},{6,3},{7,2},{8,13},{9,12},{10,... | collective-permute-start | bytes 196616 | tf_op jit(solution)/shard_map/ppermute | solution.py:110
  10.1 4.1 %collective-permute-start.4 = (f32[16,1024]{1,0:T(8,128)S(1)}, f32[16,1024]{1,0:T(8,128)S(1)}, u32[]{:S(2)}, u32[]{:S(2)}) collective-permute-start(f32[16,1024]{1,0:T(8,128)S(1)} %pad_maximum_fusion.refs_0_), channel_id=1, source_target_pairs={{0,3},{1,2},{2,1},{3,0},{4,7},{5,6},{6,5},{7,4},{8,11},{9,10},{10,... | collective-permute-start | bytes 196616 | tf_op jit(solution)/shard_map/ppermute | solution.py:110
  10.9 1.4 %copy-start = (f32[128,256]{1,0:T(8,128)S(1)}, f32[128,256]{1,0:T(8,128)}, u32[]{:S(2)}) copy-start(f32[128,256]{1,0:T(8,128)} %refs_9_.1) | copy-start | bytes 393220
  12.3 0.7 %copy-start.1 = (f32[2,4,512]{2,1,0:T(4,128)S(1)}, f32[2,4,512]{2,1,0:T(4,128)}, u32[]{:S(2)}) copy-start(f32[2,4,512]{2,1,0:T(4,128)} %refs_1_.1) | copy-start | bytes 49156
  14.9 4.4 %collective-permute-start.5 = (f32[8,8,128]{2,1,0:T(8,128)S(1)}, f32[8,8,128]{2,1,0:T(8,128)S(1)}, u32[]{:S(2)}, u32[]{:S(2)}) collective-permute-start(f32[8,8,128]{2,1,0:T(8,128)S(1)} %get-tuple-element.18), channel_id=1, source_target_pairs={{0,7},{1,6},{2,5},{3,4},{4,3},{5,2},{6,1},{7,0},{8,15},{9,14},{10,... | collective-permute-start | bytes 98312 | tf_op jit(solution)/shard_map/ppermute | solution.py:110
  17.1 1.3 %collective-permute-start.8 = (f32[64,128]{1,0:T(8,128)S(1)}, f32[64,128]{1,0:T(8,128)S(1)}, u32[]{:S(2)}, u32[]{:S(2)}) collective-permute-start(f32[64,128]{1,0:T(8,128)S(1)} %constant_dynamic-update-slice_fusion.own), channel_id=1, source_target_pairs={{0,1},{1,0},{2,3},{3,2},{4,5},{5,4},{6,7},{7,6},{8,9},{9,8},{10,11... | collective-permute-start | bytes 98312 | tf_op jit(solution)/shard_map/ppermute | solution.py:97
  17.6 3.4 %collective-permute-start.6 = (f32[8,8,128]{2,1,0:T(8,128)S(1)}, f32[8,8,128]{2,1,0:T(8,128)S(1)}, u32[]{:S(2)}, u32[]{:S(2)}) collective-permute-start(f32[8,8,128]{2,1,0:T(8,128)S(1)} %get-tuple-element.19), channel_id=1, source_target_pairs={{0,5},{1,4},{2,7},{3,6},{4,1},{5,0},{6,3},{7,2},{8,13},{9,12},{10,... | collective-permute-start | bytes 98312 | tf_op jit(solution)/shard_map/ppermute | solution.py:110
  17.7 3.3 %collective-permute-start.7 = (f32[8,8,128]{2,1,0:T(8,128)S(1)}, f32[8,8,128]{2,1,0:T(8,128)S(1)}, u32[]{:S(2)}, u32[]{:S(2)}) collective-permute-start(f32[8,8,128]{2,1,0:T(8,128)S(1)} %get-tuple-element.20), channel_id=1, source_target_pairs={{0,3},{1,2},{2,1},{3,0},{4,7},{5,6},{6,5},{7,4},{8,11},{9,10},{10,... | collective-permute-start | bytes 98312 | tf_op jit(solution)/shard_map/ppermute | solution.py:110
  21.0 4.8 %collective-permute-start.9 = (f32[10,8,128]{2,1,0:T(8,128)S(1)}, f32[10,8,128]{2,1,0:T(8,128)S(1)}, u32[]{:S(2)}, u32[]{:S(2)}) collective-permute-start(f32[10,8,128]{2,1,0:T(8,128)S(1)} %shard_map.86.mine), channel_id=1, source_target_pairs={{0,9},{1,8},{2,11},{3,10},{4,13},{5,12},{6,15},{7,14},{8,1},{9,0},... | collective-permute-start | bytes 122888 | tf_op jit(solution)/shard_map/ppermute | solution.py:110
  25.9 4.3 %collective-permute-start.10 = (f32[10,8,128]{2,1,0:T(8,128)S(1)}, f32[10,8,128]{2,1,0:T(8,128)S(1)}, u32[]{:S(2)}, u32[]{:S(2)}) collective-permute-start(f32[10,8,128]{2,1,0:T(8,128)S(1)} %shard_map.87.refs_3_), channel_id=1, source_target_pairs={{0,7},{1,6},{2,5},{3,4},{4,3},{5,2},{6,1},{7,0},{8,15},{9,14},{10,... | collective-permute-start | bytes 122888 | tf_op jit(solution)/shard_map/ppermute | solution.py:110
  27.8 3.4 %collective-permute-start.11 = (f32[10,8,128]{2,1,0:T(8,128)S(1)}, f32[10,8,128]{2,1,0:T(8,128)S(1)}, u32[]{:S(2)}, u32[]{:S(2)}) collective-permute-start(f32[10,8,128]{2,1,0:T(8,128)S(1)} %shard_map.87.refs_3_), channel_id=1, source_target_pairs={{0,5},{1,4},{2,7},{3,6},{4,1},{5,0},{6,3},{7,2},{8,13},{9,12},{10,... | collective-permute-start | bytes 122888 | tf_op jit(solution)/shard_map/ppermute | solution.py:110
  27.8 4.1 %collective-permute-start.12 = (f32[10,8,128]{2,1,0:T(8,128)S(1)}, f32[10,8,128]{2,1,0:T(8,128)S(1)}, u32[]{:S(2)}, u32[]{:S(2)}) collective-permute-start(f32[10,8,128]{2,1,0:T(8,128)S(1)} %shard_map.87.refs_3_), channel_id=1, source_target_pairs={{0,3},{1,2},{2,1},{3,0},{4,7},{5,6},{6,5},{7,4},{8,11},{9,10},{10,... | collective-permute-start | bytes 122888 | tf_op jit(solution)/shard_map/ppermute | solution.py:110
  29.4 2.4 %collective-permute-start.16 = (f32[10,8,128]{2,1,0:T(8,128)S(1)}, f32[10,8,128]{2,1,0:T(8,128)S(1)}, u32[]{:S(2)}, u32[]{:S(2)}) collective-permute-start(f32[10,8,128]{2,1,0:T(8,128)S(1)} %shard_map.87.refs_3_), channel_id=1, source_target_pairs={{0,1},{1,0},{2,3},{3,2},{4,5},{5,4},{6,7},{7,6},{8,9},{9,8},{10,11... | collective-permute-start | bytes 122888 | tf_op jit(solution)/shard_map/ppermute | solution.py:97
  30.2 1.7 %collective-permute-start.13 = (f32[10,8,128]{2,1,0:T(8,128)S(1)}, f32[10,8,128]{2,1,0:T(8,128)S(1)}, u32[]{:S(2)}, u32[]{:S(2)}) collective-permute-start(f32[10,8,128]{2,1,0:T(8,128)S(1)} %collective-permute-done.10.refs_0_), channel_id=1, source_target_pairs={{0,1},{1,0},{2,3},{3,2},{4,5},{5,4},{6,7},{7,6},{8,9},{9,8},{10,11... | collective-permute-start | bytes 122888 | tf_op jit(solution)/shard_map/ppermute | solution.py:97
  31.2 1.5 %collective-permute-start.14 = (f32[10,8,128]{2,1,0:T(8,128)S(1)}, f32[10,8,128]{2,1,0:T(8,128)S(1)}, u32[]{:S(2)}, u32[]{:S(2)}) collective-permute-start(f32[10,8,128]{2,1,0:T(8,128)S(1)} %collective-permute-done.11.refs_1_), channel_id=1, source_target_pairs={{0,1},{1,0},{2,3},{3,2},{4,5},{5,4},{6,7},{7,6},{8,9},{9,8},{10,11... | collective-permute-start | bytes 122888 | tf_op jit(solution)/shard_map/ppermute | solution.py:97
  31.8 1.2 %collective-permute-start.15 = (f32[10,8,128]{2,1,0:T(8,128)S(1)}, f32[10,8,128]{2,1,0:T(8,128)S(1)}, u32[]{:S(2)}, u32[]{:S(2)}) collective-permute-start(f32[10,8,128]{2,1,0:T(8,128)S(1)} %collective-permute-done.12.refs_2_), channel_id=1, source_target_pairs={{0,1},{1,0},{2,3},{3,2},{4,5},{5,4},{6,7},{7,6},{8,9},{9,8},{10,11... | collective-permute-start | bytes 122888 | tf_op jit(solution)/shard_map/ppermute | solution.py:97
